TPU v7x, 32 devices: a whole 2x2x4 slice. The times are simulated.
32 devices in a mesh: spatial: 8 (over y, x, core), fsdp: 4 (over z).
Axes of the slice: x: 2, y: 2, z: 4, core: 2. Of those that a mesh axis runs over, the one named last changes fastest.
Arguments:
- features: bfloat16 [4, 32, 64, 640], P('fsdp', 'spatial'), may hold values from -60 to 60
- step_index: int32 [1], replicated, may hold values from 0 to 49
- roster: float32 [50], replicated, may hold values from 1 to 999
- time_weight: float32 [320, 1280], replicated, may hold values from -0.3125 to 0.3125
- temb_weight: float32 [1280, 640], replicated, may hold values from -0.15625 to 0.15625
- norm_gains: float32 [3, 640], replicated, may hold values from 0.1 to 1.9
- conv_first: bfloat16 [5760, 640], P(None, 'fsdp'), may hold values from -0.078125 to 0.078125
- conv_second: bfloat16 [5760, 640], P(None, 'fsdp'), may hold values from -0.078125 to 0.078125
- attn_weight: bfloat16 [640, 1920], P(None, 'fsdp'), may hold values from -0.15811388 to 0.15811388
- out_weight: bfloat16 [640, 640], P(None, 'fsdp'), may hold values from -0.25 to 0.25
Outputs:
- refined: bfloat16 [4, 32, 64, 640], P('fsdp', 'spatial')
All inputs are finite; a program needn't handle non-finite values.
Results may differ from a plain program's by a relative error of at most 0.02.
Values may be sent and summed in bfloat16 or wider, within the bound.
No kernel may reach another device: no remote copies, remote signals or barrier semaphores. Data moves between devices by JAX's collectives and lax.ppermute only.
A program may use at most 192 MiB of HBM per device.

v0:
```python
import math

import jax
import jax.numpy as jnp
import numpy as np
from jax import lax
from jax.experimental import pallas as pl
from jax.experimental.pallas import tpu as pltpu
from jax.sharding import PartitionSpec as P


HEAD_DIM = 64
GROUPS = 32
EPSILON = 1e-05
LANES = 128
HIGHEST = lax.Precision.HIGHEST


NT = (((1,), (1,)), ((), ()))


def call(body, out_shape, scratch=(), scalars=0, flops=0):
    def run(*operands):
        specs = [
            pl.BlockSpec(memory_space=pltpu.SMEM if i < scalars else pltpu.VMEM)
            for i in range(len(operands))
        ]
        outs = jax.tree.map(lambda _: pl.BlockSpec(memory_space=pltpu.VMEM), out_shape)
        return pl.pallas_call(
            body,
            out_shape=out_shape,
            in_specs=specs,
            out_specs=outs,
            scratch_shapes=list(scratch),
            compiler_params=pltpu.CompilerParams(vmem_limit_bytes=60 * 2**20),
            cost_estimate=pl.CostEstimate(flops=flops, transcendentals=0, bytes_accessed=0)
            if flops
            else None,
        )(*operands)

    return run


def shift(values, axis, step):
    count = lax.axis_size(axis)
    return lax.ppermute(values, axis, [(i, (i + step) % count) for i in range(count)])


def silu(v):
    half = 0.5 * v
    return half + half * jnp.tanh(half)


def time_bias(step_index, roster, time_weight, temb_columns, rows):
    freqs, hidden = time_weight.shape
    kept = temb_columns.shape[1]
    half_len = freqs // 2
    steps = roster.shape[0]

    def body(i_ref, r_ref, w_ref, t_ref, o_ref):
        at = lax.broadcasted_iota(jnp.int32, (1, steps), 1)
        moment = jnp.sum(jnp.where(at == i_ref[0], r_ref[...], 0.0), axis=1, keepdims=True)
        row = lax.broadcasted_iota(jnp.int32, (half_len, 1), 0).astype(jnp.float32)
        angles = moment * jnp.exp(-math.log(10000.0) * row / half_len)
        time_hidden = jnp.sum(jnp.cos(angles) * w_ref[:half_len], axis=0, keepdims=True) + jnp.sum(
            jnp.sin(angles) * w_ref[half_len:], axis=0, keepdims=True
        )
        time_hidden = time_hidden / (1.0 + jnp.exp(-time_hidden))
        parts = []
        for start in range(0, hidden, LANES):
            piece = jnp.broadcast_to(time_hidden[:, start : start + LANES], (LANES, LANES))
            parts.append(piece.T[:, :1] * t_ref[start : start + LANES])
        summed = jnp.sum(sum(parts[1:], parts[0]), axis=0, keepdims=True)
        o_ref[...] = jnp.zeros((rows, LANES), jnp.float32)
        for start in range(0, kept, LANES):
            size = min(LANES, kept - start)
            cut = summed[:, start : start + size]
            if size < LANES:
                cut = jnp.concatenate([cut, jnp.zeros((1, LANES - size), jnp.float32)], axis=1)
            turned = jnp.broadcast_to(cut, (LANES, LANES)).T
            o_ref[start : start + size] = turned[:size]

    return call(body, jax.ShapeDtypeStruct((rows, LANES), jnp.float32), scalars=1)(
        step_index, roster[None, :], time_weight, temb_columns
    )


def group_of(rows, block, kept, width):
    index = np.arange(rows)
    group = (index // block * kept + index % block) // width
    return np.where(index % block < kept, group, -1)


def members(rows, block, kept, width):
    group = group_of(rows, block, kept, width)[:, None]
    return jnp.asarray(group == np.arange(LANES)[None, :], jnp.bfloat16)


def same_group(rows, block, kept, width):
    group = group_of(rows, block, kept, width)[:, None]
    return jnp.asarray((group == group.T) & (group >= 0), jnp.float32)


def three_parts(values):
    high = values.astype(jnp.bfloat16).astype(jnp.float32)
    rest = values - high
    middle = rest.astype(jnp.bfloat16).astype(jnp.float32)
    return high, middle, rest - middle


def group_sums(row, member):
    for dims in ((((1,), (0,)), ((), ())), NT):
        at = lax.broadcasted_iota(jnp.int32, (8, row.shape[1]), 0)
        high, middle, low = three_parts(row)
        parts = jnp.where(at == 0, high, jnp.where(at == 1, middle, jnp.where(at == 2, low, 0.0)))
        summed = lax.dot_general(
            parts.astype(jnp.bfloat16), member, dims, preferred_element_type=jnp.float32
        )
        row = jnp.sum(summed, axis=0, keepdims=True)
    return row


def local_stats(features, member, width):
    samples, length, channels = features.shape

    def body(x_ref, g_ref, o_ref):
        for i in range(samples):
            v = x_ref[i].astype(jnp.float32)
            mean = group_sums(jnp.sum(v, axis=0, keepdims=True), g_ref[...]) / (length * width)
            c = v - mean
            o_ref[i : i + 1] = mean
            o_ref[samples + i : samples + i + 1] = group_sums(
                jnp.sum(c * c, axis=0, keepdims=True), g_ref[...]
            )

    return call(body, jax.ShapeDtypeStruct((2 * samples, channels), jnp.float32))(features, member)


def place(where, pieces, axis, flops=0):
    first = pieces[0]
    size = first.shape[axis]
    shape = list(first.shape)
    shape[axis] = size * len(pieces)

    def body(w_ref, *refs):
        for k, piece in enumerate(refs[:-1]):
            start = pl.multiple_of(w_ref[k] * size, size)
            refs[-1][(slice(None),) * axis + (pl.ds(start, size),)] = piece[...]

    return call(body, jax.ShapeDtypeStruct(tuple(shape), first.dtype), scalars=1, flops=flops)(
        where, *pieces
    )


def merge_stats(p_ref, gain, entries):
    devices, rows, _ = p_ref.shape
    count = rows // 2
    mean = p_ref[0, :count]
    for d in range(1, devices):
        mean = mean + p_ref[d, :count]
    mean = mean / devices
    squares = jnp.zeros_like(mean)
    for d in range(devices):
        away = p_ref[d, :count] - mean
        squares = squares + p_ref[d, count:] + entries * (away * away)
    return mean, lax.rsqrt(squares / (entries * devices) + EPSILON) * gain


TAIL = 16


def rows_message(parts, gain, entries, mids):
    samples, mid, channels = mids.shape

    def body(p_ref, g_ref, m_ref, o_ref):
        mean, scale = merge_stats(p_ref, g_ref[...], entries)
        for i in range(samples):
            o_ref[i, :mid] = m_ref[i]
            rows = [*three_parts(mean[i : i + 1]), *three_parts(scale[i : i + 1])]
            rows.append(jnp.zeros((TAIL - len(rows), channels), jnp.float32))
            o_ref[i, mid:] = jnp.concatenate(rows, axis=0).astype(jnp.bfloat16)

    shape = jax.ShapeDtypeStruct((samples, mid + TAIL, channels), jnp.bfloat16)
    return call(body, shape)(parts, gain, mids)


def columns_message(parts, gain, entries, mids):
    shard, wide = mids.shape

    def body(p_ref, g_ref, m_ref, o_ref):
        o_ref[:, :wide] = m_ref[...]
        figures = jnp.concatenate(merge_stats(p_ref, g_ref[...], entries), axis=0)
        rows = [*three_parts(figures)]
        rows.append(jnp.zeros((LANES - 3 * figures.shape[0], shard), jnp.float32))
        rows = jnp.concatenate(rows, axis=0).astype(jnp.bfloat16)
        o_ref[:, wide:] = lax.dot_general(
            identity(shard, shard), rows, NT, preferred_element_type=jnp.float32
        ).astype(jnp.bfloat16)

    shape = jax.ShapeDtypeStruct((shard, wide + LANES), jnp.bfloat16)
    return call(body, shape)(parts, gain, mids)


def identity(rows, columns):
    at = lax.broadcasted_iota(jnp.int32, (rows, columns), 0)
    same = at == lax.broadcasted_iota(jnp.int32, (rows, columns), 1)
    return jnp.where(same, 1.0, 0.0).astype(jnp.bfloat16)


def tap_rows(weight, row, depth):
    return jnp.concatenate(
        [weight[:, (3 * row + b) * depth : (3 * row + b + 1) * depth] for b in range(3)], axis=0
    )


def pick_column(values, at, period):
    lane = lax.broadcasted_iota(jnp.int32, values.shape, 1)
    chosen = (lane == at) | (lane == at + period) | (lane == at + 2 * period)
    return jnp.sum(jnp.where(chosen, values, 0.0), axis=1, keepdims=True)


def column_shift(y, shard, width):
    lane = lax.broadcasted_iota(jnp.int32, (shard, LANES), 1) % width
    tiles = []
    for start in range(0, y.shape[1], LANES):
        left = y[:shard, start : start + LANES]
        right = y[2 * shard :, start : start + LANES]
        tiles.append(
            y[shard : 2 * shard, start : start + LANES]
            + jnp.where(lane > 0, pltpu.roll(left, 1, axis=1), 0.0)
            + jnp.where(lane < width - 1, pltpu.roll(right, LANES - 1, axis=1), 0.0)
        )
    return jnp.concatenate(tiles, axis=1)


def first_conv(ends, edges, mids, above, below, weight, bias, groups, pick, eye, width, group):
    n = len(edges)
    samples, edge, channels = edges[0].shape
    mid = mids[0].shape[1] - TAIL
    shard = bias.shape[0]
    count = n * samples
    inner = mid // width
    length = edge + mid

    def body(*refs):
        ends_ref = refs[0]
        e_refs, m_refs = refs[1 : 1 + n], refs[1 + n : 1 + 2 * n]
        a_ref, b_ref, w_ref, t_ref, g_ref, p_ref, i_ref = refs[1 + 2 * n : 8 + 2 * n]
        eo_ref, mo_ref, so_ref, fe_ref, fm_ref, buf, out_buf = refs[8 + 2 * n :]
        has_above = ends_ref[0].astype(jnp.float32)
        has_below = ends_ref[1].astype(jnp.float32)
        lane = lax.broadcasted_iota(jnp.int32, (shard, LANES), 1)
        sums = jnp.zeros((shard, LANES), jnp.float32)
        for j in range(n):
            for i in range(samples):
                q = j * samples + i
                tail = m_refs[j][i, mid:].astype(jnp.float32)
                mean = tail[0:1] + tail[1:2] + tail[2:3]
                scale = tail[3:4] + tail[4:5] + tail[5:6]

                def act(x):
                    return silu((x.astype(jnp.float32) - mean) * scale)

                e = e_refs[j][i]
                m = m_refs[j][i, :mid]
                ea = act(e).astype(jnp.bfloat16)
                buf[:width] = (act(a_ref[q]) * has_above).astype(jnp.bfloat16)
                buf[width : 2 * width] = ea[:width]
                buf[2 * width : 2 * width + mid] = act(m).astype(jnp.bfloat16)
                buf[2 * width + mid : 3 * width + mid] = ea[width:]
                buf[3 * width + mid :] = (act(b_ref[q]) * has_below).astype(jnp.bfloat16)
                y = jnp.zeros((3 * shard, length), jnp.float32)
                for a in range(3):
                    window = jnp.concatenate(
                        [
                            buf[a * width : (a + 1) * width],
                            buf[(a + 1 + inner) * width : (a + 2 + inner) * width],
                            buf[(a + 1) * width : (a + 1 + inner) * width],
                        ],
                        axis=0,
                    )
                    y = y + lax.dot_general(
                        tap_rows(w_ref, a, channels), window, NT, preferred_element_type=jnp.float32
                    )
                out = column_shift(y, shard, width) + t_ref[:, :1]
                eo_ref[:, q * edge : (q + 1) * edge] = out[:, :edge].astype(jnp.bfloat16)
                mo_ref[:, q * mid : (q + 1) * mid] = out[:, edge:].astype(jnp.bfloat16)
                fe_ref[:, q * edge : (q + 1) * edge] = lax.dot_general(
                    p_ref[...], e, NT, preferred_element_type=jnp.float32
                ).astype(jnp.bfloat16)
                fm_ref[:, q * mid : (q + 1) * mid] = lax.dot_general(
                    p_ref[...], m, NT, preferred_element_type=jnp.float32
                ).astype(jnp.bfloat16)
                out_buf[q] = out
                sums = jnp.where(lane == q, jnp.sum(out, axis=1, keepdims=True), sums)
        centers = jnp.dot(g_ref[...], sums, precision=HIGHEST) / (length * group)
        sums = jnp.zeros((shard, LANES), jnp.float32)
        for q in range(count):
            c = out_buf[q] - centers[:, q : q + 1]
            sums = jnp.where(lane == q, jnp.sum(c * c, axis=1, keepdims=True), sums)
        squares = jnp.dot(g_ref[...], sums, precision=HIGHEST)
        for start, found in ((0, centers), (count, squares)):
            so_ref[start : start + count] = lax.dot_general(
                i_ref[...], found, NT, precision=HIGHEST
            )[:count]

    out_shape = (
        jax.ShapeDtypeStruct((shard, count * edge), jnp.bfloat16),
        jax.ShapeDtypeStruct((shard, count * mid), jnp.bfloat16),
        jax.ShapeDtypeStruct((2 * count, shard), jnp.float32),
        jax.ShapeDtypeStruct((shard, count * edge), jnp.bfloat16),
        jax.ShapeDtypeStruct((shard, count * mid), jnp.bfloat16),
    )
    scratch = [
        pltpu.VMEM((length + 2 * width, channels), jnp.bfloat16),
        pltpu.VMEM((count, shard, length), jnp.float32),
    ]
    return call(body, out_shape, scratch, scalars=1, flops=6 * count * length * channels * 3 * shard)(
        ends, *edges, *mids, above, below, weight, bias, groups, pick, eye
    )


def second_conv(ends, edges, mids, above, below, weight, own_edges, own_mids, samples, width):
    n = len(edges)
    shard = edges[0].shape[0]
    count = n * samples
    edge, mid = edges[0].shape[1] // count, (mids[0].shape[1] - LANES) // count
    length = edge + mid

    def body(*refs):
        ends_ref = refs[0]
        e_refs, m_refs = refs[1 : 1 + n], refs[1 + n : 1 + 2 * n]
        a_ref, b_ref, w_ref, fe_ref, fm_ref = refs[1 + 2 * n : 6 + 2 * n]
        o_ref, buf = refs[6 + 2 * n :]
        has_above = ends_ref[0].astype(jnp.float32)
        has_below = ends_ref[1].astype(jnp.float32)
        lane = lax.broadcasted_iota(jnp.int32, (shard, LANES), 1)
        low = lane < width
        columns = [m_refs[j][:, count * mid :].astype(jnp.float32) for j in range(n)]

        def sample(t, i):
            for j in range(n):
                q = lax.rem(t - j + n, n) * samples + i
                mean, scale = (pick_column(columns[j], at, 2 * count) for at in (q, count + q))

                def act(x):
                    return silu((x.astype(jnp.float32) - mean) * scale)

                rows = slice(j * shard, (j + 1) * shard)
                natural = pl.ds(pl.multiple_of(lax.rem(ends_ref[2] + n - j, n) * shard, 16), shard)
                cut = pl.ds(pl.multiple_of(q * edge, LANES), edge)
                e = act(e_refs[j][:, cut])
                m = act(m_refs[j][:, pl.ds(pl.multiple_of(q * mid, LANES), mid)])
                top = pltpu.roll(act(a_ref[rows, cut]), width, axis=1) * has_above
                bottom = pltpu.roll(act(b_ref[rows, cut]), width, axis=1) * has_below
                turned = pltpu.roll(m, width, axis=1)
                buf[0, natural, :edge] = jnp.where(low, top, m).astype(jnp.bfloat16)
                buf[0, natural, edge:] = jnp.where(low, e, turned).astype(jnp.bfloat16)
                buf[1, natural, :edge] = e.astype(jnp.bfloat16)
                buf[1, natural, edge:] = m.astype(jnp.bfloat16)
                buf[2, natural, :edge] = jnp.where(low, m, bottom).astype(jnp.bfloat16)
                buf[2, natural, edge:] = jnp.where(low, turned, e).astype(jnp.bfloat16)
            y = jnp.zeros((3 * shard, length), jnp.float32)
            for a in range(3):
                y = y + jnp.dot(
                    tap_rows(w_ref, a, n * shard), buf[a], preferred_element_type=jnp.float32
                )
            out = column_shift(y, shard, width)
            q = t * samples + i
            cut = pl.ds(pl.multiple_of(q * edge, LANES), edge)
            o_ref[t, i, :, :edge] = (out[:, :edge] + fe_ref[:, cut].astype(jnp.float32)).astype(
                jnp.bfloat16
            )
            cut = pl.ds(pl.multiple_of(q * mid, LANES), mid)
            o_ref[t, i, :, edge:] = (out[:, edge:] + fm_ref[:, cut].astype(jnp.float32)).astype(
                jnp.bfloat16
            )

        @pl.loop(0, n)
        def _(t):
            for i in range(samples):
                sample(t, i)

    return call(
        body,
        jax.ShapeDtypeStruct((n, samples, shard, length), jnp.bfloat16),
        [pltpu.VMEM((3, n * shard, length), jnp.bfloat16)],
        scalars=1,
        flops=6 * count * length * n * shard * 3 * shard,
    )(ends, *edges, *mids, above, below, weight, own_edges, own_mids)


def split_dot(ones, column):
    high = column.astype(jnp.bfloat16)
    rest = column - high.astype(jnp.float32)
    middle = rest.astype(jnp.bfloat16)
    low = (rest - middle.astype(jnp.float32)).astype(jnp.bfloat16)
    lane = lax.broadcasted_iota(jnp.int32, (column.shape[0], LANES), 1)
    parts = jnp.where(lane == 0, high.astype(jnp.float32), 0.0)
    parts = jnp.where(lane == 1, middle.astype(jnp.float32), parts)
    parts = jnp.where(lane == 2, low.astype(jnp.float32), parts).astype(jnp.bfloat16)
    summed = jnp.dot(ones, parts, preferred_element_type=jnp.float32)
    return jnp.sum(summed, axis=1, keepdims=True)


def attention(chunks, weights, out_weight, gain, spread, unpad, used, width, group):
    pieces = len(chunks)
    samples, rows, length = chunks[0].shape
    channels = gain.shape[0] if unpad is None else unpad.shape[1]
    heads = channels // HEAD_DIM
    keys = pieces * length
    inner = length // width - 2
    blocks = weights.shape[0]

    def body(*refs):
        c_refs = refs[:pieces]
        w_ref, g_ref, a_ref, b_ref = refs[pieces : pieces + 4]
        v_ref = None if out_weight is None else refs[-5]
        o_ref, buf, query_buf, mixed_buf = refs[-4:]
        for i in range(samples):
            total = jnp.zeros((rows, 1), jnp.float32)
            for c in c_refs:
                total = total + jnp.sum(c[i].astype(jnp.float32), axis=1, keepdims=True)
            mean = split_dot(b_ref[...], split_dot(a_ref[...], total)) / (keys * group)
            total = jnp.zeros((rows, 1), jnp.float32)
            for c in c_refs:
                away = c[i].astype(jnp.float32) - mean
                total = total + jnp.sum(away * away, axis=1, keepdims=True)
            spread_of = split_dot(b_ref[...], split_dot(a_ref[...], total)) / (keys * group)
            scale = lax.rsqrt(spread_of + EPSILON) * g_ref[:, :1]
            for p, c in enumerate(c_refs):
                normed = ((c[i].astype(jnp.float32) - mean) * scale).astype(jnp.bfloat16)
                for g in range(blocks):
                    low = max(0, (0 if p == 0 else channels) - g * used)
                    if low < used:
                        buf[g * used + low : (g + 1) * used, p * length : (p + 1) * length] = jnp.dot(
                            w_ref[g, low:used], normed, preferred_element_type=jnp.float32
                        ).astype(jnp.bfloat16)
            queries = buf[:channels, :length].astype(jnp.float32) * HEAD_DIM ** (-0.5)
            query_buf[...] = queries.T.astype(jnp.bfloat16)

            @pl.loop(0, heads // 2)
            def _(two):
                lanes = pl.ds(pl.multiple_of(two * LANES, LANES), LANES)
                at = channels + two * LANES
                k_two = buf[pl.ds(pl.multiple_of(at, LANES), LANES)]
                v_two = buf[pl.ds(pl.multiple_of(at + channels, LANES), LANES)]
                q_two = query_buf[:, lanes]
                pair = []
                for h in range(2):
                    cut = slice(h * HEAD_DIM, (h + 1) * HEAD_DIM)
                    scores = jnp.dot(q_two[:, cut], k_two[cut], preferred_element_type=jnp.float32)
                    shifted = jnp.exp(scores - jnp.max(scores, axis=1, keepdims=True))
                    totals = jnp.sum(shifted, axis=1, keepdims=True)
                    mixed = lax.dot_general(
                        shifted.astype(jnp.bfloat16),
                        v_two[cut],
                        NT,
                        preferred_element_type=jnp.float32,
                    )
                    pair.append(mixed / totals)
                mixed_buf[:, lanes] = jnp.concatenate(pair, axis=1).astype(jnp.bfloat16)

            own = c_refs[0][i].astype(jnp.float32).T
            if unpad is not None:
                own = jnp.dot(
                    own.astype(jnp.bfloat16), refs[pieces + 4][...], preferred_element_type=jnp.float32
                )
            if out_weight is None:
                kept = channels // blocks
                v_rows = [w_ref[g, used : used + kept] for g in range(blocks)]
                v_rows = jnp.concatenate(v_rows, axis=0)
            else:
                v_rows = v_ref[...]
            result = own + lax.dot_general(
                mixed_buf[...], v_rows, NT, preferred_element_type=jnp.float32
            )
            result = result.astype(jnp.bfloat16)
            o_ref[i, 0] = result[:width]
            o_ref[i, 1 + inner] = result[width : 2 * width]
            for r in range(inner):
                o_ref[i, 1 + r] = result[(2 + r) * width : (3 + r) * width]

    operands = [*chunks, weights, gain, spread.T, spread]
    if unpad is not None:
        operands.append(unpad)
    if out_weight is not None:
        operands.append(out_weight)
    return call(
        body,
        jax.ShapeDtypeStruct((samples, length // width, width, channels), jnp.bfloat16),
        [
            pltpu.VMEM((3 * channels, keys), jnp.bfloat16),
            pltpu.VMEM((length, channels), jnp.bfloat16),
            pltpu.VMEM((length, channels), jnp.bfloat16),
        ],
    )(*operands)


def pad_rows(values, rows, axis):
    missing = rows - values.shape[axis]
    return jnp.pad(values, [(0, missing if a == axis else 0) for a in range(values.ndim)])


def local(
    features,
    step_index,
    roster,
    time_weight,
    temb_weight,
    norm_gains,
    conv_first,
    conv_second,
    attn_weight,
    out_weight,
):
    samples, height, width, channels = features.shape
    n, planes = lax.axis_size("fsdp"), lax.axis_size("spatial")
    mine, row = lax.axis_index("fsdp"), lax.axis_index("spatial")
    group = channels // GROUPS
    kept = conv_first.shape[1]
    shard = -(-kept // 16) * 16
    length = height * width
    entries = float(length * group)
    count = n * samples
    half = planes // 2
    swap = [(i, i ^ 1) for i in range(planes)]
    ends = jnp.stack([row > 0, row < planes - 1, mine]).astype(jnp.int32)

    def ring(values):
        return [values] + [shift(values, "fsdp", j) for j in range(1, n)]

    def block(values, axis):
        return lax.dynamic_slice_in_dim(values, mine * kept, kept, axis)

    def pad_blocks(values, axis):
        if shard == kept:
            return values
        shape = list(values.shape)
        parts = values.reshape(shape[:axis] + [shape[axis] // kept, kept] + shape[axis + 1 :])
        parts = pad_rows(parts, shard, axis + 1)
        return parts.reshape(shape[:axis] + [shape[axis] // kept * shard] + shape[axis + 1 :])

    def in_plane_stats(values):
        values = values[None]
        size = 1
        while size < planes:
            other = lax.ppermute(values, "spatial", [(i, i ^ size) for i in range(planes)])
            values = jnp.concatenate([values, other], axis=0)
            size *= 2
        return values

    def in_plane(values):
        near = [values] + [shift(values, "spatial", 2 * d) for d in range(1, half)]
        far = [lax.ppermute(c, "spatial", swap) for c in near]
        back = (row - 2 * np.arange(half)) % planes
        return near + far, jnp.concatenate([back, back ^ 1]).astype(jnp.int32)

    flat = features.reshape(samples, length, channels)
    own_stats = local_stats(flat, members(channels, channels, channels, group), group)
    edges = ring(jnp.concatenate([flat[:, :width], flat[:, length - width :]], axis=1))
    above = shift_rows(jnp.concatenate([e[:, width:] for e in edges], axis=0), 1)
    below = shift_rows(jnp.concatenate([e[:, :width] for e in edges], axis=0), -1)
    own_stats = in_plane_stats(own_stats)
    mids = rows_message(own_stats, norm_gains[:1], entries, flat[:, width : length - width])
    mids = ring(mids)

    wide = attn_weight.shape[1]
    part = -(-(wide + kept) // (16 * planes)) * 16
    turned = jnp.concatenate(
        [pad_blocks(attn_weight.T, 1), pad_rows(out_weight.T, n * shard, 1)], axis=0
    )
    turned = lax.dynamic_slice_in_dim(pad_rows(turned, part * planes, 0), row * part, part, 0)
    turned = lax.all_gather(turned, ("fsdp", "spatial"), axis=0)
    turned = turned.reshape(n, planes * part, n * shard)

    projection, used, last_weight = turned, wide, None
    if shard != kept:
        projection = turned[:, :wide].reshape(1, n * wide, n * shard)
        used = n * wide
        last_weight = turned[:, wide : wide + kept, :channels].reshape(channels, channels)
    first_weight = pad_rows(conv_first.T, shard, 0)
    second_weight = pad_rows(pad_blocks(conv_second.T, 1), shard, 0)
    bias = time_bias(step_index, roster, time_weight, block(temb_weight, 1), shard)
    index = jnp.arange(shard)
    pick = jnp.where(index < kept, index + mine * kept, -1)[:, None] == jnp.arange(channels)[None, :]

    edges, mids, own_stats, own_edges, own_mids = first_conv(
        ends,
        edges,
        mids,
        above,
        below,
        first_weight,
        bias,
        same_group(shard, shard, kept, group),
        pick.astype(jnp.bfloat16),
        jnp.asarray(np.eye(-(-count // 8) * 8, LANES, dtype=np.float32)),
        width,
        group,
    )

    edges = ring(edges)
    stacked = jnp.concatenate(edges, axis=0)
    above = shift_rows(stacked, 1)
    below = shift_rows(stacked, -1)
    gain = pad_rows(block(norm_gains[1:2], 1), shard, 1)
    own_stats = in_plane_stats(own_stats)
    mids = columns_message(own_stats, gain, entries, mids)
    mids = ring(mids)
    sums = second_conv(
        ends,
        edges,
        mids,
        above,
        below,
        second_weight,
        own_edges,
        own_mids,
        samples,
        width,
    )

    own = [sums[0]] + [shift(sums[t], "fsdp", -t) for t in range(1, n)]
    own = place(((mine + np.arange(n)) % n).astype(jnp.int32), own, 1)
    chunks, _ = in_plane(own)
    gain = jnp.broadcast_to(pad_blocks(norm_gains[2], 0)[:, None], (n * shard, LANES))
    unpad = None
    if shard != kept:
        at = np.arange(n * shard)
        at = np.where(at % shard < kept, at // shard * kept + at % shard, -1)
        unpad = jnp.asarray(at[:, None] == np.arange(channels)[None, :], jnp.bfloat16)
    return attention(
        chunks,
        projection,
        last_weight,
        gain,
        members(n * shard, shard, kept, group),
        unpad,
        used,
        width,
        group,
    )


def shift_rows(values, step):
    count = lax.axis_size("spatial")
    pairs = [(i, i + step) for i in range(count) if 0 <= i + step < count]
    return lax.ppermute(values, "spatial", pairs)


def solution(mesh):
    in_specs = (
        P("fsdp", "spatial", None, None),
        P(),
        P(),
        P(),
        P(),
        P(),
        P(None, "fsdp"),
        P(None, "fsdp"),
        P(None, "fsdp"),
        P(None, "fsdp"),
    )
    out_specs = P("fsdp", "spatial", None, None)

    return jax.shard_map(local, mesh=mesh, in_specs=in_specs, out_specs=out_specs, check_vma=False)
```

profile of v0, /device:TPU:0, one launch (start us, length us, event | category | flops | bytes accessed | tf_op | source)
XLA Modules:
  0.0 209.4 jit_solution(5265443793971189782)
XLA Ops:
  6.5 1.7 fusion.1
  8.3 0.9 fusion.3
  9.3 0.7 pad_maximum_fusion.2.refs_1_
  10.0 3.1 %collective-permute-start = (bf16[1,128,640]{2,1,0:T(8,128)(2,1)}, bf16[1,128,640]{2,1,0:T(8,128)(2,1)}, u32[]{:S(2)}, u32[]{:S(2)}) collective-permute-start(bf16[1,128,640]{2,1,0:T(8,128)(2,1)} %pad_maximum_fusion.2.refs_1_), channel_id=1, source_target_pairs={{0,1},{1,2},{2,3},{3,0},{4,5},{5,6},{6,7},{7,4},{8,9},{9,10},{10,1... | collective-permute-start | bytes 491528 | tf_op jit(solution)/shard_map/ppermute | solution.py:46
  13.0 2.6 %collective-permute-start.1 = (bf16[1,128,640]{2,1,0:T(8,128)(2,1)}, bf16[1,128,640]{2,1,0:T(8,128)(2,1)}, u32[]{:S(2)}, u32[]{:S(2)}) collective-permute-start(bf16[1,128,640]{2,1,0:T(8,128)(2,1)} %pad_maximum_fusion.2.refs_1_), channel_id=1, source_target_pairs={{0,2},{1,3},{2,0},{3,1},{4,6},{5,7},{6,4},{7,5},{8,10},{9,11},{10,... | collective-permute-start | bytes 491528 | tf_op jit(solution)/shard_map/ppermute | solution.py:46
  15.6 1.3 collective-permute-start.2
  16.9 2.4 %shard_map.145 = f32[2,640]{1,0:T(2,128)} custom-call(bf16[1,256,640]{2,1,0:T(8,128)(2,1)} %bitcast.22, bf16[640,128]{1,0:T(8,128)(2,1)} %constant.44.clone.g_ref.refs_11_), custom_call_target="tpu_custom_call" | custom-call | tf_op jit(solution)/shard_map/pallas_call | solution.py:29
  19.9 1.5 constant_dynamic-slice_fusion.1.t_ref
  21.4 1.6 collective-permute-start.4
  23.6 1.6 slice.66.m_ref
  25.8 3.4 %shard_map.147.refs_12_ = f32[160,128]{1,0:T(8,128)} custom-call(s32[1]{0:T(128)S(6)} %copy.19.i_ref, f32[1,50]{1,0:T(1,128)} %bitcast.34, f32[320,1280]{1,0:T(8,128)} %w_ref.1, f32[1280,160]{1,0:T(8,128)} %constant_dynamic-slice_fusion.1.t_ref), custom_call_target="tpu_custom_call" | custom-call | tf_op jit(solution)/shard_map/pallas_call | solution.py:29
  29.2 1.6 collective-permute-start.5
  30.8 0.9 fusion.4
  31.8 0.9 fusion.5
  32.7 0.9 fusion.6
  33.7 1.3 collective-permute-start.10
  35.0 0.8 pad_maximum_fusion
  35.8 3.0 %collective-permute-start.9 = (bf16[4,64,640]{2,1,0:T(8,128)(2,1)}, bf16[4,64,640]{2,1,0:T(8,128)(2,1)S(1)}, u32[]{:S(2)}, u32[]{:S(2)}) collective-permute-start(bf16[4,64,640]{2,1,0:T(8,128)(2,1)} %pad_maximum_fusion), channel_id=1, source_target_pairs={{0,4},{4,8},{8,12},{12,16},{16,20},{20,24},{24,28},{1,5},{5,9},{9,... | collective-permute-start | bytes 983048 | tf_op jit(solution)/shard_map/ppermute | solution.py:649
  39.5 1.7 shard_map.146.refs_5_
  41.2 0.7 collective-permute-start.6
  41.9 1.4 collective-permute-start.7
  43.2 1.8 collective-permute-start.8
  45.0 0.8 fusion.refs_14_
  45.8 7.2 %collective-permute-done.6.refs_6_ = bf16[1,144,640]{2,1,0:T(8,128)(2,1)S(1)} collective-permute-done((bf16[1,144,640]{2,1,0:T(8,128)(2,1)}, bf16[1,144,640]{2,1,0:T(8,128)(2,1)S(1)}, u32[]{:S(2)}, u32[]{:S(2)}) %collective-permute-start.6) | collective-permute-done | bytes 184352 | tf_op jit(solution)/shard_map/ppermute | solution.py:46
  53.0 7.9 %collective-permute-done.7.refs_7_ = bf16[1,144,640]{2,1,0:T(8,128)(2,1)S(1)} collective-permute-done((bf16[1,144,640]{2,1,0:T(8,128)(2,1)}, bf16[1,144,640]{2,1,0:T(8,128)(2,1)S(1)}, u32[]{:S(2)}, u32[]{:S(2)}) %collective-permute-start.7) | collective-permute-done | bytes 184352 | tf_op jit(solution)/shard_map/ppermute | solution.py:46
  61.0 0.6 copy-done.18
  61.7 0.7 copy-done.15
  62.4 7.8 %shard_map.148 = (bf16[160,512]{1,0:T(8,128)(2,1)}, bf16[160,512]{1,0:T(8,128)(2,1)}, f32[8,160]{1,0:T(8,128)}, bf16[160,512]{1,0:T(8,128)(2,1)}, bf16[160,512]{1,0:T(8,128)(2,1)}) custom-call(s32[3]{0:T(128)} %pad_add_fusion.refs_0_, bf16[1,128,640]{2,1,0:T(8,128)(2,1)} %pad_maximum_fusion.2.refs_1_, bf16[1,128,640]{2,1,0:T(8,128)(2,1)} %collective-permute-done.refs_2_, ...), custom_call_target="tpu_custom_call" | custom-call | flops 1887436800 | tf_op jit(solution)/shard_map/pallas_call | solution.py:29
  70.2 4.2 %collective-permute-start.11 = (bf16[160,512]{1,0:T(8,128)(2,1)}, bf16[160,512]{1,0:T(8,128)(2,1)S(1)}, u32[]{:S(2)}, u32[]{:S(2)}) collective-permute-start(bf16[160,512]{1,0:T(8,128)(2,1)} %get-tuple-element.10.refs_1_), channel_id=1, source_target_pairs={{0,1},{1,2},{2,3},{3,0},{4,5},{5,6},{6,7},{7,4},{8,9},{9,10},{10,1... | collective-permute-start | bytes 491528 | tf_op jit(solution)/shard_map/ppermute | solution.py:46
  74.6 1.6 constant_dynamic-update-slice_fusion.3
  76.2 2.2 %collective-permute-start.13 = (bf16[160,512]{1,0:T(8,128)(2,1)}, bf16[160,512]{1,0:T(8,128)(2,1)S(1)}, u32[]{:S(2)}, u32[]{:S(2)}) collective-permute-start(bf16[160,512]{1,0:T(8,128)(2,1)} %get-tuple-element.10.refs_1_), channel_id=1, source_target_pairs={{0,3},{1,0},{2,1},{3,2},{4,7},{5,4},{6,5},{7,6},{8,11},{9,8},{10,9... | collective-permute-start | bytes 491528 | tf_op jit(solution)/shard_map/ppermute | solution.py:46
  78.5 4.0 %collective-permute-done.11.refs_2_ = bf16[160,512]{1,0:T(8,128)(2,1)S(1)} collective-permute-done((bf16[160,512]{1,0:T(8,128)(2,1)}, bf16[160,512]{1,0:T(8,128)(2,1)S(1)}, u32[]{:S(2)}, u32[]{:S(2)}) %collective-permute-start.11) | collective-permute-done | bytes 163872 | tf_op jit(solution)/shard_map/ppermute | solution.py:46
  82.4 0.7 constant_dynamic-update-slice_fusion.2
  83.1 6.2 %collective-permute-done.12.refs_3_ = bf16[160,512]{1,0:T(8,128)(2,1)S(1)} collective-permute-done((bf16[160,512]{1,0:T(8,128)(2,1)}, bf16[160,512]{1,0:T(8,128)(2,1)S(1)}, u32[]{:S(2)}, u32[]{:S(2)}) %collective-permute-start.12) | collective-permute-done | bytes 163872 | tf_op jit(solution)/shard_map/ppermute | solution.py:46
  89.3 0.7 constant_dynamic-update-slice_fusion.1
  90.1 0.7 constant_dynamic-update-slice_fusion
  90.8 2.7 %collective-permute-start.20 = (bf16[640,512]{1,0:T(8,128)(2,1)}, bf16[640,512]{1,0:T(8,128)(2,1)}, u32[]{:S(2)}, u32[]{:S(2)}) collective-permute-start(bf16[640,512]{1,0:T(8,128)(2,1)} %constant_dynamic-update-slice_fusion), channel_id=1, source_target_pairs={{0,4},{4,8},{8,12},{12,16},{16,20},{20,24},{24,28},{1,5},{5,9},{9,... | collective-permute-start | bytes 1966088 | tf_op jit(solution)/shard_map/ppermute | solution.py:649
  93.6 1.3 collective-permute-start.21
  94.8 0.7 pad_maximum_fusion.7
  95.6 2.5 %collective-permute-start.15 = (f32[2,8,160]{2,1,0:T(8,128)S(1)}, f32[2,8,160]{2,1,0:T(8,128)S(1)}, u32[]{:S(2)}, u32[]{:S(2)}) collective-permute-start(f32[2,8,160]{2,1,0:T(8,128)S(1)} %pad_maximum_fusion.7), channel_id=1, source_target_pairs={{0,8},{4,12},{8,0},{12,4},{16,24},{20,28},{24,16},{28,20},{1,9},{5... | collective-permute-start | bytes 30728 | tf_op jit(solution)/shard_map/ppermute | solution.py:548
  98.1 12.6 %collective-permute-done.15 = f32[2,8,160]{2,1,0:T(8,128)S(1)} collective-permute-done((f32[2,8,160]{2,1,0:T(8,128)S(1)}, f32[2,8,160]{2,1,0:T(8,128)S(1)}, u32[]{:S(2)}, u32[]{:S(2)}) %collective-permute-start.15) | collective-permute-done | bytes 10272 | tf_op jit(solution)/shard_map/ppermute | solution.py:548
  110.7 0.7 pad_maximum_fusion.5
  112.0 3.3 %collective-permute-done.16 = f32[4,8,160]{2,1,0:T(8,128)S(1)} collective-permute-done((f32[4,8,160]{2,1,0:T(8,128)S(1)}, f32[4,8,160]{2,1,0:T(8,128)S(1)}, u32[]{:S(2)}, u32[]{:S(2)}) %collective-permute-start.16) | collective-permute-done | bytes 20512 | tf_op jit(solution)/shard_map/ppermute | solution.py:548
  115.3 1.3 pad_maximum_fusion.3.p_ref
  116.6 1.8 shard_map.149.refs_5_
  118.5 3.3 %collective-permute-start.17 = (bf16[160,640]{1,0:T(8,128)(2,1)}, bf16[160,640]{1,0:T(8,128)(2,1)S(1)}, u32[]{:S(2)}, u32[]{:S(2)}) collective-permute-start(bf16[160,640]{1,0:T(8,128)(2,1)} %shard_map.149.refs_5_), channel_id=1, source_target_pairs={{0,1},{1,2},{2,3},{3,0},{4,5},{5,6},{6,7},{7,4},{8,9},{9,10},{10,1... | collective-permute-start | bytes 614408 | tf_op jit(solution)/shard_map/ppermute | solution.py:46
  121.7 2.8 %collective-permute-start.18 = (bf16[160,640]{1,0:T(8,128)(2,1)}, bf16[160,640]{1,0:T(8,128)(2,1)}, u32[]{:S(2)}, u32[]{:S(2)}) collective-permute-start(bf16[160,640]{1,0:T(8,128)(2,1)} %shard_map.149.refs_5_), channel_id=1, source_target_pairs={{0,2},{1,3},{2,0},{3,1},{4,6},{5,7},{6,4},{7,5},{8,10},{9,11},{10,... | collective-permute-start | bytes 614408 | tf_op jit(solution)/shard_map/ppermute | solution.py:46
  124.5 5.4 %collective-permute-done.17.refs_6_ = bf16[160,640]{1,0:T(8,128)(2,1)S(1)} collective-permute-done((bf16[160,640]{1,0:T(8,128)(2,1)}, bf16[160,640]{1,0:T(8,128)(2,1)S(1)}, u32[]{:S(2)}, u32[]{:S(2)}) %collective-permute-start.17) | collective-permute-done | bytes 204832 | tf_op jit(solution)/shard_map/ppermute | solution.py:46
  129.9 5.0 %collective-permute-done.18.refs_7_ = bf16[160,640]{1,0:T(8,128)(2,1)} collective-permute-done((bf16[160,640]{1,0:T(8,128)(2,1)}, bf16[160,640]{1,0:T(8,128)(2,1)}, u32[]{:S(2)}, u32[]{:S(2)}) %collective-permute-start.18) | collective-permute-done | bytes 204832 | tf_op jit(solution)/shard_map/ppermute | solution.py:46
  135.0 9.1 %shard_map.150 = bf16[4,1,160,256]{3,2,1,0:T(8,128)(2,1)} custom-call(s32[3]{0:T(128)} %pad_add_fusion.refs_0_, bf16[160,512]{1,0:T(8,128)(2,1)} %get-tuple-element.10.refs_1_, bf16[160,512]{1,0:T(8,128)(2,1)} %copy-done.7, bf16[160,512]{1,0:T(8,128)(2,1)} %copy-done.8, bf16[160,512]{1,0:T(8,128)(2,1)} %copy-done.9, bf16[160,640]{1,0:T(8,128)(2,1)} %shard_map.149.refs_5_, ...), custom_call_target="tpu_custom_call" | custom-call | flops 1887436800 | tf_op jit(solution)/shard_map/pallas_call | solution.py:29
  144.1 1.7 slice_bitcast_fusion
  145.8 4.2 %collective-permute-start.22 = (bf16[1,160,256]{2,1,0:T(8,128)(2,1)S(1)}, bf16[1,160,256]{2,1,0:T(8,128)(2,1)S(1)}, u32[]{:S(2)}, u32[]{:S(2)}) collective-permute-start(bf16[1,160,256]{2,1,0:T(8,128)(2,1)S(1)} %get-tuple-element.17), channel_id=1, source_target_pairs={{0,3},{1,0},{2,1},{3,2},{4,7},{5,4},{6,5},{7,6},{8,11},{9,8},{10,9... | collective-permute-start | bytes 245768 | tf_op jit(solution)/shard_map/ppermute | solution.py:46
  150.0 1.5 collective-permute-start.23
  152.1 0.8 collective-permute-done.22.refs_1_
  152.9 5.6 %collective-permute-done.23.refs_2_ = bf16[1,160,256]{2,1,0:T(8,128)(2,1)S(1)} collective-permute-done((bf16[1,160,256]{2,1,0:T(8,128)(2,1)S(1)}, bf16[1,160,256]{2,1,0:T(8,128)(2,1)S(1)}, u32[]{:S(2)}, u32[]{:S(2)}) %collective-permute-start.23) | collective-permute-done | bytes 81952 | tf_op jit(solution)/shard_map/ppermute | solution.py:46
  159.2 1.8 shard_map.151.refs_0_
  161.5 2.9 %collective-permute-start.27 = (bf16[1,640,256]{2,1,0:T(8,128)(2,1)}, bf16[1,640,256]{2,1,0:T(8,128)(2,1)S(1)}, u32[]{:S(2)}, u32[]{:S(2)}) collective-permute-start(bf16[1,640,256]{2,1,0:T(8,128)(2,1)} %shard_map.151.refs_0_), channel_id=1, source_target_pairs={{0,24},{4,28},{8,0},{12,4},{16,8},{20,12},{24,16},{28,20},{1,25},{... | collective-permute-start | bytes 983048 | tf_op jit(solution)/shard_map/ppermute | solution.py:46
  164.5 8.2 %collective-permute-done.25.refs_1_ = bf16[1,640,256]{2,1,0:T(8,128)(2,1)S(1)} collective-permute-done((bf16[1,640,256]{2,1,0:T(8,128)(2,1)}, bf16[1,640,256]{2,1,0:T(8,128)(2,1)S(1)}, u32[]{:S(2)}, u32[]{:S(2)}) %collective-permute-start.25) | collective-permute-done | bytes 327712 | tf_op jit(solution)/shard_map/ppermute | solution.py:46
  172.6 0.7 copy-done.1
  173.4 3.0 %collective-permute-done.26.refs_2_ = bf16[1,640,256]{2,1,0:T(8,128)(2,1)S(1)} collective-permute-done((bf16[1,640,256]{2,1,0:T(8,128)(2,1)}, bf16[1,640,256]{2,1,0:T(8,128)(2,1)S(1)}, u32[]{:S(2)}, u32[]{:S(2)}) %collective-permute-start.26) | collective-permute-done | bytes 327712 | tf_op jit(solution)/shard_map/ppermute | solution.py:46
  177.1 0.9 collective-permute-done.30.refs_6_
  178.0 0.7 copy-done.6
  178.8 0.9 broadcast_in_dim.27.refs_9_
  179.6 22.9 %shard_map.152 = bf16[1,4,64,640]{3,2,1,0:T(8,128)(2,1)} custom-call(bf16[1,640,256]{2,1,0:T(8,128)(2,1)} %shard_map.151.refs_0_, bf16[1,640,256]{2,1,0:T(8,128)(2,1)} %copy-done.1, bf16[1,640,256]{2,1,0:T(8,128)(2,1)} %copy-done.2, bf16[1,640,256]{2,1,0:T(8,128)(2,1)} %copy-done.3, bf16[1,640,256]{2,1,0:T(8,128)(2,1)} %copy-done.4, ...), custom_call_target="tpu_custom_call" | custom-call | tf_op jit(solution)/shard_map/pallas_call | solution.py:29
  (79 shorter events, 5.5 us)
Async XLA Ops:
  6.5 13.4 %copy-start = (f32[1280,640]{1,0:T(8,128)S(1)}, f32[1280,640]{1,0:T(8,128)}, u32[]{:S(2)}) copy-start(f32[1280,640]{1,0:T(8,128)} %param.19) | copy-start | bytes 9830404
  6.5 12.8 %copy-start.14 = (f32[3,640]{1,0:T(4,128)S(1)}, f32[3,640]{1,0:T(4,128)}, u32[]{:S(2)}) copy-start(f32[3,640]{1,0:T(4,128)} %param.20) | copy-start | bytes 23044
  6.5 172.2 %all-gather.3.cloned.1.call-start = ((), (), s32[]{:S(2)}) async-start(), calls=%async_computation | async-start | bytes 3379200 | tf_op jit(solution)/shard_map/all_gather | solution.py:574
  10.0 20.9 %collective-permute-start = (bf16[1,128,640]{2,1,0:T(8,128)(2,1)}, bf16[1,128,640]{2,1,0:T(8,128)(2,1)}, u32[]{:S(2)}, u32[]{:S(2)}) collective-permute-start(bf16[1,128,640]{2,1,0:T(8,128)(2,1)} %pad_maximum_fusion.2.refs_1_), channel_id=1, source_target_pairs={{0,1},{1,2},{2,3},{3,0},{4,5},{5,6},{6,7},{7,4},{8,9},{9,10},{10,1... | collective-permute-start | bytes 491528 | tf_op jit(solution)/shard_map/ppermute | solution.py:46
  13.0 18.8 %collective-permute-start.1 = (bf16[1,128,640]{2,1,0:T(8,128)(2,1)}, bf16[1,128,640]{2,1,0:T(8,128)(2,1)}, u32[]{:S(2)}, u32[]{:S(2)}) collective-permute-start(bf16[1,128,640]{2,1,0:T(8,128)(2,1)} %pad_maximum_fusion.2.refs_1_), channel_id=1, source_target_pairs={{0,2},{1,3},{2,0},{3,1},{4,6},{5,7},{6,4},{7,5},{8,10},{9,11},{10,... | collective-permute-start | bytes 491528 | tf_op jit(solution)/shard_map/ppermute | solution.py:46
  15.6 17.1 %collective-permute-start.2 = (bf16[1,128,640]{2,1,0:T(8,128)(2,1)}, bf16[1,128,640]{2,1,0:T(8,128)(2,1)}, u32[]{:S(2)}, u32[]{:S(2)}) collective-permute-start(bf16[1,128,640]{2,1,0:T(8,128)(2,1)} %pad_maximum_fusion.2.refs_1_), channel_id=1, source_target_pairs={{0,3},{1,0},{2,1},{3,2},{4,7},{5,4},{6,5},{7,6},{8,11},{9,8},{10,9... | collective-permute-start | bytes 491528 | tf_op jit(solution)/shard_map/ppermute | solution.py:46
  19.3 2.1 copy-start.10
  19.3 2.1 collective-permute-start.3
  21.4 7.8 %collective-permute-start.4 = (f32[2,2,640]{2,1,0:T(2,128)S(1)}, f32[2,2,640]{2,1,0:T(2,128)S(1)}, u32[]{:S(2)}, u32[]{:S(2)}) collective-permute-start(f32[2,2,640]{2,1,0:T(2,128)S(1)} %pad_maximum_fusion.8), channel_id=1, source_target_pairs={{0,8},{4,12},{8,0},{12,4},{16,24},{20,28},{24,16},{28,20},{1,9},{5... | collective-permute-start | bytes 30728 | tf_op jit(solution)/shard_map/ppermute | solution.py:548
  29.2 9.6 %collective-permute-start.5 = (f32[4,2,640]{2,1,0:T(2,128)S(1)}, f32[4,2,640]{2,1,0:T(2,128)S(1)}, u32[]{:S(2)}, u32[]{:S(2)}) collective-permute-start(f32[4,2,640]{2,1,0:T(2,128)S(1)} %pad_maximum_fusion.6), channel_id=1, source_target_pairs={{0,16},{4,20},{8,24},{12,28},{16,0},{20,4},{24,8},{28,12},{1,17},{... | collective-permute-start | bytes 61448 | tf_op jit(solution)/shard_map/ppermute | solution.py:548
  33.7 27.2 %collective-permute-start.10 = (bf16[4,64,640]{2,1,0:T(8,128)(2,1)S(1)}, bf16[4,64,640]{2,1,0:T(8,128)(2,1)}, u32[]{:S(2)}, u32[]{:S(2)}) collective-permute-start(bf16[4,64,640]{2,1,0:T(8,128)(2,1)S(1)} %pad_maximum_fusion.1), channel_id=1, source_target_pairs={{4,0},{8,4},{12,8},{16,12},{20,16},{24,20},{28,24},{5,1},{9,5},{13... | collective-permute-start | bytes 983048 | tf_op jit(solution)/shard_map/ppermute | solution.py:649
  35.8 25.1 %collective-permute-start.9 = (bf16[4,64,640]{2,1,0:T(8,128)(2,1)}, bf16[4,64,640]{2,1,0:T(8,128)(2,1)S(1)}, u32[]{:S(2)}, u32[]{:S(2)}) collective-permute-start(bf16[4,64,640]{2,1,0:T(8,128)(2,1)} %pad_maximum_fusion), channel_id=1, source_target_pairs={{0,4},{4,8},{8,12},{12,16},{16,20},{20,24},{24,28},{1,5},{5,9},{9,... | collective-permute-start | bytes 983048 | tf_op jit(solution)/shard_map/ppermute | solution.py:649
  41.2 11.8 %collective-permute-start.6 = (bf16[1,144,640]{2,1,0:T(8,128)(2,1)}, bf16[1,144,640]{2,1,0:T(8,128)(2,1)S(1)}, u32[]{:S(2)}, u32[]{:S(2)}) collective-permute-start(bf16[1,144,640]{2,1,0:T(8,128)(2,1)} %shard_map.146.refs_5_), channel_id=1, source_target_pairs={{0,1},{1,2},{2,3},{3,0},{4,5},{5,6},{6,7},{7,4},{8,9},{9,10},{10,1... | collective-permute-start | bytes 552968 | tf_op jit(solution)/shard_map/ppermute | solution.py:46
  41.9 19.0 %collective-permute-start.7 = (bf16[1,144,640]{2,1,0:T(8,128)(2,1)}, bf16[1,144,640]{2,1,0:T(8,128)(2,1)S(1)}, u32[]{:S(2)}, u32[]{:S(2)}) collective-permute-start(bf16[1,144,640]{2,1,0:T(8,128)(2,1)} %shard_map.146.refs_5_), channel_id=1, source_target_pairs={{0,2},{1,3},{2,0},{3,1},{4,6},{5,7},{6,4},{7,5},{8,10},{9,11},{10,... | collective-permute-start | bytes 552968 | tf_op jit(solution)/shard_map/ppermute | solution.py:46
  43.2 17.7 %collective-permute-start.8 = (bf16[1,144,640]{2,1,0:T(8,128)(2,1)}, bf16[1,144,640]{2,1,0:T(8,128)(2,1)S(1)}, u32[]{:S(2)}, u32[]{:S(2)}) collective-permute-start(bf16[1,144,640]{2,1,0:T(8,128)(2,1)} %shard_map.146.refs_5_), channel_id=1, source_target_pairs={{0,3},{1,0},{2,1},{3,2},{4,7},{5,4},{6,5},{7,6},{8,11},{9,8},{10,9... | collective-permute-start | bytes 552968 | tf_op jit(solution)/shard_map/ppermute | solution.py:46
  53.0 7.9 %copy-start.17 = (bf16[1,144,640]{2,1,0:T(8,128)(2,1)}, bf16[1,144,640]{2,1,0:T(8,128)(2,1)S(1)}, u32[]{:S(2)}) copy-start(bf16[1,144,640]{2,1,0:T(8,128)(2,1)S(1)} %collective-permute-done.6.refs_6_) | copy-start | bytes 552964
  60.9 0.7 copy-start.18
  60.9 0.7 copy-start.19
  61.7 0.7 copy-start.15
  70.2 12.3 %collective-permute-start.11 = (bf16[160,512]{1,0:T(8,128)(2,1)}, bf16[160,512]{1,0:T(8,128)(2,1)S(1)}, u32[]{:S(2)}, u32[]{:S(2)}) collective-permute-start(bf16[160,512]{1,0:T(8,128)(2,1)} %get-tuple-element.10.refs_1_), channel_id=1, source_target_pairs={{0,1},{1,2},{2,3},{3,0},{4,5},{5,6},{6,7},{7,4},{8,9},{9,10},{10,1... | collective-permute-start | bytes 491528 | tf_op jit(solution)/shard_map/ppermute | solution.py:46
  74.4 15.0 %collective-permute-start.12 = (bf16[160,512]{1,0:T(8,128)(2,1)}, bf16[160,512]{1,0:T(8,128)(2,1)S(1)}, u32[]{:S(2)}, u32[]{:S(2)}) collective-permute-start(bf16[160,512]{1,0:T(8,128)(2,1)} %get-tuple-element.10.refs_1_), channel_id=1, source_target_pairs={{0,2},{1,3},{2,0},{3,1},{4,6},{5,7},{6,4},{7,5},{8,10},{9,11},{10,... | collective-permute-start | bytes 491528 | tf_op jit(solution)/shard_map/ppermute | solution.py:46
  76.2 13.8 %collective-permute-start.13 = (bf16[160,512]{1,0:T(8,128)(2,1)}, bf16[160,512]{1,0:T(8,128)(2,1)S(1)}, u32[]{:S(2)}, u32[]{:S(2)}) collective-permute-start(bf16[160,512]{1,0:T(8,128)(2,1)} %get-tuple-element.10.refs_1_), channel_id=1, source_target_pairs={{0,3},{1,0},{2,1},{3,2},{4,7},{5,4},{6,5},{7,6},{8,11},{9,8},{10,9... | collective-permute-start | bytes 491528 | tf_op jit(solution)/shard_map/ppermute | solution.py:46
  78.5 16.4 %collective-permute-start.14 = (f32[1,8,160]{2,1,0:T(8,128)}, f32[1,8,160]{2,1,0:T(8,128)S(1)}, u32[]{:S(2)}, u32[]{:S(2)}) collective-permute-start(f32[1,8,160]{2,1,0:T(8,128)} %bitcast.30), channel_id=1, source_target_pairs={{0,4},{4,0},{8,12},{12,8},{16,20},{20,16},{24,28},{28,24},{1,5},{5... | collective-permute-start | bytes 15368 | tf_op jit(solution)/shard_map/ppermute | solution.py:548
  82.4 52.5 %copy-start.7 = (bf16[160,512]{1,0:T(8,128)(2,1)}, bf16[160,512]{1,0:T(8,128)(2,1)S(1)}, u32[]{:S(2)}) copy-start(bf16[160,512]{1,0:T(8,128)(2,1)S(1)} %collective-permute-done.11.refs_2_) | copy-start | bytes 491524
  89.3 45.6 %copy-start.8 = (bf16[160,512]{1,0:T(8,128)(2,1)}, bf16[160,512]{1,0:T(8,128)(2,1)S(1)}, u32[]{:S(2)}) copy-start(bf16[160,512]{1,0:T(8,128)(2,1)S(1)} %collective-permute-done.12.refs_3_) | copy-start | bytes 491524
  90.1 44.9 %copy-start.9 = (bf16[160,512]{1,0:T(8,128)(2,1)}, bf16[160,512]{1,0:T(8,128)(2,1)S(1)}, u32[]{:S(2)}) copy-start(bf16[160,512]{1,0:T(8,128)(2,1)S(1)} %collective-permute-done.13.refs_4_) | copy-start | bytes 491524
  90.8 44.1 %collective-permute-start.20 = (bf16[640,512]{1,0:T(8,128)(2,1)}, bf16[640,512]{1,0:T(8,128)(2,1)}, u32[]{:S(2)}, u32[]{:S(2)}) collective-permute-start(bf16[640,512]{1,0:T(8,128)(2,1)} %constant_dynamic-update-slice_fusion), channel_id=1, source_target_pairs={{0,4},{4,8},{8,12},{12,16},{16,20},{20,24},{24,28},{1,5},{5,9},{9,... | collective-permute-start | bytes 1966088 | tf_op jit(solution)/shard_map/ppermute | solution.py:649
  93.6 41.4 %collective-permute-start.21 = (bf16[640,512]{1,0:T(8,128)(2,1)}, bf16[640,512]{1,0:T(8,128)(2,1)}, u32[]{:S(2)}, u32[]{:S(2)}) collective-permute-start(bf16[640,512]{1,0:T(8,128)(2,1)} %constant_dynamic-update-slice_fusion), channel_id=1, source_target_pairs={{4,0},{8,4},{12,8},{16,12},{20,16},{24,20},{28,24},{5,1},{9,5},{13... | collective-permute-start | bytes 1966088 | tf_op jit(solution)/shard_map/ppermute | solution.py:649
  95.6 15.1 %collective-permute-start.15 = (f32[2,8,160]{2,1,0:T(8,128)S(1)}, f32[2,8,160]{2,1,0:T(8,128)S(1)}, u32[]{:S(2)}, u32[]{:S(2)}) collective-permute-start(f32[2,8,160]{2,1,0:T(8,128)S(1)} %pad_maximum_fusion.7), channel_id=1, source_target_pairs={{0,8},{4,12},{8,0},{12,4},{16,24},{20,28},{24,16},{28,20},{1,9},{5... | collective-permute-start | bytes 30728 | tf_op jit(solution)/shard_map/ppermute | solution.py:548
  111.4 3.9 %collective-permute-start.16 = (f32[4,8,160]{2,1,0:T(8,128)S(1)}, f32[4,8,160]{2,1,0:T(8,128)S(1)}, u32[]{:S(2)}, u32[]{:S(2)}) collective-permute-start(f32[4,8,160]{2,1,0:T(8,128)S(1)} %pad_maximum_fusion.5), channel_id=1, source_target_pairs={{0,16},{4,20},{8,24},{12,28},{16,0},{20,4},{24,8},{28,12},{1,17},{... | collective-permute-start | bytes 61448 | tf_op jit(solution)/shard_map/ppermute | solution.py:548
  118.5 11.4 %collective-permute-start.17 = (bf16[160,640]{1,0:T(8,128)(2,1)}, bf16[160,640]{1,0:T(8,128)(2,1)S(1)}, u32[]{:S(2)}, u32[]{:S(2)}) collective-permute-start(bf16[160,640]{1,0:T(8,128)(2,1)} %shard_map.149.refs_5_), channel_id=1, source_target_pairs={{0,1},{1,2},{2,3},{3,0},{4,5},{5,6},{6,7},{7,4},{8,9},{9,10},{10,1... | collective-permute-start | bytes 614408 | tf_op jit(solution)/shard_map/ppermute | solution.py:46
  121.7 13.2 %collective-permute-start.18 = (bf16[160,640]{1,0:T(8,128)(2,1)}, bf16[160,640]{1,0:T(8,128)(2,1)}, u32[]{:S(2)}, u32[]{:S(2)}) collective-permute-start(bf16[160,640]{1,0:T(8,128)(2,1)} %shard_map.149.refs_5_), channel_id=1, source_target_pairs={{0,2},{1,3},{2,0},{3,1},{4,6},{5,7},{6,4},{7,5},{8,10},{9,11},{10,... | collective-permute-start | bytes 614408 | tf_op jit(solution)/shard_map/ppermute | solution.py:46
  124.5 10.4 %collective-permute-start.19 = (bf16[160,640]{1,0:T(8,128)(2,1)}, bf16[160,640]{1,0:T(8,128)(2,1)}, u32[]{:S(2)}, u32[]{:S(2)}) collective-permute-start(bf16[160,640]{1,0:T(8,128)(2,1)} %shard_map.149.refs_5_), channel_id=1, source_target_pairs={{0,3},{1,0},{2,1},{3,2},{4,7},{5,4},{6,5},{7,6},{8,11},{9,8},{10,9... | collective-permute-start | bytes 614408 | tf_op jit(solution)/shard_map/ppermute | solution.py:46
  129.9 5.1 %copy-start.16 = (bf16[160,640]{1,0:T(8,128)(2,1)}, bf16[160,640]{1,0:T(8,128)(2,1)S(1)}, u32[]{:S(2)}) copy-start(bf16[160,640]{1,0:T(8,128)(2,1)S(1)} %collective-permute-done.17.refs_6_) | copy-start | bytes 614404
  145.8 7.1 %collective-permute-start.22 = (bf16[1,160,256]{2,1,0:T(8,128)(2,1)S(1)}, bf16[1,160,256]{2,1,0:T(8,128)(2,1)S(1)}, u32[]{:S(2)}, u32[]{:S(2)}) collective-permute-start(bf16[1,160,256]{2,1,0:T(8,128)(2,1)S(1)} %get-tuple-element.17), channel_id=1, source_target_pairs={{0,3},{1,0},{2,1},{3,2},{4,7},{5,4},{6,5},{7,6},{8,11},{9,8},{10,9... | collective-permute-start | bytes 245768 | tf_op jit(solution)/shard_map/ppermute | solution.py:46
  150.0 8.5 %collective-permute-start.23 = (bf16[1,160,256]{2,1,0:T(8,128)(2,1)S(1)}, bf16[1,160,256]{2,1,0:T(8,128)(2,1)S(1)}, u32[]{:S(2)}, u32[]{:S(2)}) collective-permute-start(bf16[1,160,256]{2,1,0:T(8,128)(2,1)S(1)} %get-tuple-element.16), channel_id=1, source_target_pairs={{0,2},{1,3},{2,0},{3,1},{4,6},{5,7},{6,4},{7,5},{8,10},{9,11},{10,... | collective-permute-start | bytes 245768 | tf_op jit(solution)/shard_map/ppermute | solution.py:46
  151.5 7.0 %collective-permute-start.24 = (bf16[1,160,256]{2,1,0:T(8,128)(2,1)S(1)}, bf16[1,160,256]{2,1,0:T(8,128)(2,1)S(1)}, u32[]{:S(2)}, u32[]{:S(2)}) collective-permute-start(bf16[1,160,256]{2,1,0:T(8,128)(2,1)S(1)} %get-tuple-element.15), channel_id=1, source_target_pairs={{0,1},{1,2},{2,3},{3,0},{4,5},{5,6},{6,7},{7,4},{8,9},{9,10},{10,1... | collective-permute-start | bytes 245768 | tf_op jit(solution)/shard_map/ppermute | solution.py:46
  152.9 5.6 %copy-start.11 = (bf16[1,160,256]{2,1,0:T(8,128)(2,1)}, bf16[1,160,256]{2,1,0:T(8,128)(2,1)S(1)}, u32[]{:S(2)}) copy-start(bf16[1,160,256]{2,1,0:T(8,128)(2,1)S(1)} %collective-permute-done.22.refs_1_) | copy-start | bytes 245764
  158.5 0.6 copy-start.12
  158.5 0.7 copy-start.13
  160.9 11.7 %collective-permute-start.25 = (bf16[1,640,256]{2,1,0:T(8,128)(2,1)}, bf16[1,640,256]{2,1,0:T(8,128)(2,1)S(1)}, u32[]{:S(2)}, u32[]{:S(2)}) collective-permute-start(bf16[1,640,256]{2,1,0:T(8,128)(2,1)} %shard_map.151.refs_0_), channel_id=1, source_target_pairs={{0,8},{4,12},{8,16},{12,20},{16,24},{20,28},{24,0},{28,4},{1,9},{5... | collective-permute-start | bytes 983048 | tf_op jit(solution)/shard_map/ppermute | solution.py:46
  161.4 15.0 %collective-permute-start.26 = (bf16[1,640,256]{2,1,0:T(8,128)(2,1)}, bf16[1,640,256]{2,1,0:T(8,128)(2,1)S(1)}, u32[]{:S(2)}, u32[]{:S(2)}) collective-permute-start(bf16[1,640,256]{2,1,0:T(8,128)(2,1)} %shard_map.151.refs_0_), channel_id=1, source_target_pairs={{0,16},{4,20},{8,24},{12,28},{16,0},{20,4},{24,8},{28,12},{1,17},{... | collective-permute-start | bytes 983048 | tf_op jit(solution)/shard_map/ppermute | solution.py:46
  161.5 14.9 %collective-permute-start.27 = (bf16[1,640,256]{2,1,0:T(8,128)(2,1)}, bf16[1,640,256]{2,1,0:T(8,128)(2,1)S(1)}, u32[]{:S(2)}, u32[]{:S(2)}) collective-permute-start(bf16[1,640,256]{2,1,0:T(8,128)(2,1)} %shard_map.151.refs_0_), channel_id=1, source_target_pairs={{0,24},{4,28},{8,0},{12,4},{16,8},{20,12},{24,16},{28,20},{1,25},{... | collective-permute-start | bytes 983048 | tf_op jit(solution)/shard_map/ppermute | solution.py:46
  164.5 12.5 %collective-permute-start.28 = (bf16[1,640,256]{2,1,0:T(8,128)(2,1)}, bf16[1,640,256]{2,1,0:T(8,128)(2,1)S(1)}, u32[]{:S(2)}, u32[]{:S(2)}) collective-permute-start(bf16[1,640,256]{2,1,0:T(8,128)(2,1)} %shard_map.151.refs_0_), channel_id=1, source_target_pairs={{0,4},{4,0},{8,12},{12,8},{16,20},{20,16},{24,28},{28,24},{1,5},{5... | collective-permute-start | bytes 983048 | tf_op jit(solution)/shard_map/ppermute | solution.py:555
  172.6 0.7 copy-start.1
  173.4 3.6 %collective-permute-start.29 = (bf16[1,640,256]{2,1,0:T(8,128)(2,1)S(1)}, bf16[1,640,256]{2,1,0:T(8,128)(2,1)S(1)}, u32[]{:S(2)}, u32[]{:S(2)}) collective-permute-start(bf16[1,640,256]{2,1,0:T(8,128)(2,1)S(1)} %collective-permute-done.25.refs_1_), channel_id=1, source_target_pairs={{0,4},{4,0},{8,12},{12,8},{16,20},{20,16},{24,28},{28,24},{1,5},{5... | collective-permute-start | bytes 983048 | tf_op jit(solution)/shard_map/ppermute | solution.py:555
  176.4 0.7 copy-start.2
  176.4 1.6 collective-permute-start.30
  176.4 1.6 copy-start.3
  176.4 2.3 %collective-permute-start.31 = (bf16[1,640,256]{2,1,0:T(8,128)(2,1)S(1)}, bf16[1,640,256]{2,1,0:T(8,128)(2,1)}, u32[]{:S(2)}, u32[]{:S(2)}) collective-permute-start(bf16[1,640,256]{2,1,0:T(8,128)(2,1)S(1)} %collective-permute-done.27.refs_3_), channel_id=1, source_target_pairs={{0,4},{4,0},{8,12},{12,8},{16,20},{20,16},{24,28},{28,24},{1,5},{5... | collective-permute-start | bytes 983048 | tf_op jit(solution)/shard_map/ppermute | solution.py:555
  176.9 1.1 copy-start.4
  177.1 0.9 copy-start.5
  178.0 0.7 copy-start.6
Sparse Core Ops, SparseCore 0:
  10.2 78.3 all-gather.2
where the time goes:
time: 210 us; the launch traced here: 209 us
  waiting for transfers between devices  70.1 us (33%)
  Pallas kernels  50.8 us (24%)
  starting transfers between devices  47.4 us (23%)
  local copies, waits for them, and re-layouts  18.2 us (9%)
  between operations  14.3 us (7%)
  other arithmetic  8.66 us (4%)
    ppermute x18, waiting for transfers between devices, shift(): lax.ppermute(values, axis, [(i, (i + step) % count) for i in range(count)])  53.3 us
    pallas_call x8, Pallas kernels, run(): pl.pallas_call(body, out_shape=out_shape, in_specs=specs, out_specs=outs,...  50.8 us
    ppermute x18, starting transfers between devices, shift(): lax.ppermute(values, axis, [(i, (i + step) % count) for i in range(count)])  32.8 us
    ppermute x6, waiting for transfers between devices, in_plane_stats(): lax.ppermute(values, 'spatial', [(i, i ^ size) for i in range(planes)])  15.9 us
    ppermute x4, starting transfers between devices, shift_rows(): return lax.ppermute(values, 'spatial', pairs)  8.35 us
    unnamed x43, local copies, waits for them, and re-layouts  6.88 us
    ppermute x6, starting transfers between devices, in_plane_stats(): lax.ppermute(values, 'spatial', [(i, i ^ size) for i in range(planes)])  5.69 us
  transfers between devices with their start and end apart: 33, of which 13 were waited for; matrix products, arithmetic and copies ran while one was open for 10% of the time, Pallas kernels for 13%

commit v1 on v0

--- a/solution.py
+++ b/solution.py
@@ -207,16 +207,56 @@
     return jnp.where(same, 1.0, 0.0).astype(jnp.bfloat16)
 
 
+def halo_rows(edges, width):
+    samples, _, channels = edges[0].shape
+    shape = jax.ShapeDtypeStruct((len(edges) * samples, width, channels), jnp.bfloat16)
+
+    def body(*refs):
+        for j, e in enumerate(refs[:-2]):
+            refs[-2][j * samples : (j + 1) * samples] = e[:, width:]
+            refs[-1][j * samples : (j + 1) * samples] = e[:, :width]
+
+    return call(body, (shape, shape))(*edges)
+
+
+def halo_columns(edges, width):
+    shard, wide = edges[0].shape
+    edge = 2 * width
+    shape = jax.ShapeDtypeStruct((len(edges) * shard, wide // 2), jnp.bfloat16)
+
+    def body(*refs):
+        low = lax.broadcasted_iota(jnp.int32, (shard, edge), 1) < width
+        for j, e in enumerate(refs[:-2]):
+            rows = slice(j * shard, (j + 1) * shard)
+            for p in range(wide // edge // 2):
+                left = e[:, 2 * p * edge : (2 * p + 1) * edge].astype(jnp.float32)
+                right = e[:, (2 * p + 1) * edge : (2 * p + 2) * edge].astype(jnp.float32)
+                cut = slice(p * edge, (p + 1) * edge)
+                last = jnp.where(low, pltpu.roll(left, width, axis=1), right)
+                first = jnp.where(low, left, pltpu.roll(right, width, axis=1))
+                refs[-2][rows, cut] = last.astype(jnp.bfloat16)
+                refs[-1][rows, cut] = first.astype(jnp.bfloat16)
+
+    return call(body, (shape, shape))(*edges)
+
+
 def tap_rows(weight, row, depth):
     return jnp.concatenate(
         [weight[:, (3 * row + b) * depth : (3 * row + b + 1) * depth] for b in range(3)], axis=0
     )
 
 
-def pick_column(values, at, period):
-    lane = lax.broadcasted_iota(jnp.int32, values.shape, 1)
+def spread_column(tail, at, period):
+    lane = lax.broadcasted_iota(jnp.int32, (LANES, LANES), 0)
     chosen = (lane == at) | (lane == at + period) | (lane == at + 2 * period)
-    return jnp.sum(jnp.where(chosen, values, 0.0), axis=1, keepdims=True)
+    chosen = jnp.where(chosen, 1.0, 0.0).astype(jnp.bfloat16)
+    return jnp.dot(tail, chosen, preferred_element_type=jnp.float32)
+
+
+def tile(index, size):
+    if isinstance(index, int):
+        return slice(index * size, (index + 1) * size)
+    return pl.ds(pl.multiple_of(index * size, LANES), size)
 
 
 def column_shift(y, shard, width):
@@ -327,67 +367,92 @@
     edge, mid = edges[0].shape[1] // count, (mids[0].shape[1] - LANES) // count
     length = edge + mid
 
+    unrolled = n <= 4
+    shape = jax.ShapeDtypeStruct((samples, shard, length), jnp.bfloat16)
+    if not unrolled:
+        shape = jax.ShapeDtypeStruct((n, samples, shard, length), jnp.bfloat16)
+
     def body(*refs):
         ends_ref = refs[0]
         e_refs, m_refs = refs[1 : 1 + n], refs[1 + n : 1 + 2 * n]
         a_ref, b_ref, w_ref, fe_ref, fm_ref = refs[1 + 2 * n : 6 + 2 * n]
-        o_ref, buf = refs[6 + 2 * n :]
-        has_above = ends_ref[0].astype(jnp.float32)
-        has_below = ends_ref[1].astype(jnp.float32)
-        lane = lax.broadcasted_iota(jnp.int32, (shard, LANES), 1)
-        low = lane < width
-        columns = [m_refs[j][:, count * mid :].astype(jnp.float32) for j in range(n)]
-
-        def sample(t, i):
+        o_refs, buf = refs[6 + 2 * n : -1], refs[-1]
+        low = lax.broadcasted_iota(jnp.int32, (shard, edge), 1) < width
+        inside = jnp.where(low, ends_ref[0], ends_ref[1]).astype(jnp.float32)
+
+        def sample(t, i, slot):
             for j in range(n):
-                q = lax.rem(t - j + n, n) * samples + i
-                mean, scale = (pick_column(columns[j], at, 2 * count) for at in (q, count + q))
+                q = ((t - j) % n if unrolled else lax.rem(t - j + n, n)) * samples + i
+                tail = m_refs[j][:, count * mid :]
+                mean = spread_column(tail, q, 2 * count)
+                scale = spread_column(tail, q + count, 2 * count)
 
                 def act(x):
-                    return silu((x.astype(jnp.float32) - mean) * scale)
+                    return silu((x - mean) * scale)
 
                 rows = slice(j * shard, (j + 1) * shard)
                 natural = pl.ds(pl.multiple_of(lax.rem(ends_ref[2] + n - j, n) * shard, 16), shard)
-                cut = pl.ds(pl.multiple_of(q * edge, LANES), edge)
-                e = act(e_refs[j][:, cut])
-                m = act(m_refs[j][:, pl.ds(pl.multiple_of(q * mid, LANES), mid)])
-                top = pltpu.roll(act(a_ref[rows, cut]), width, axis=1) * has_above
-                bottom = pltpu.roll(act(b_ref[rows, cut]), width, axis=1) * has_below
-                turned = pltpu.roll(m, width, axis=1)
-                buf[0, natural, :edge] = jnp.where(low, top, m).astype(jnp.bfloat16)
-                buf[0, natural, edge:] = jnp.where(low, e, turned).astype(jnp.bfloat16)
-                buf[1, natural, :edge] = e.astype(jnp.bfloat16)
-                buf[1, natural, edge:] = m.astype(jnp.bfloat16)
-                buf[2, natural, :edge] = jnp.where(low, m, bottom).astype(jnp.bfloat16)
-                buf[2, natural, edge:] = jnp.where(low, turned, e).astype(jnp.bfloat16)
+                half = q // 2 if unrolled else lax.div(q, 2)
+                last = a_ref[rows, tile(half, edge)].astype(jnp.float32)
+                first = b_ref[rows, tile(half, edge)].astype(jnp.float32)
+                if unrolled:
+                    odd = q % 2 == 1
+                    halo = (
+                        jnp.where(low, pltpu.roll(last, width, axis=1), first)
+                        if odd
+                        else jnp.where(low, last, pltpu.roll(first, width, axis=1))
+                    )
+                else:
+                    halo = jnp.where(
+                        lax.rem(q, 2) == 1,
+                        jnp.where(low, pltpu.roll(last, width, axis=1), first),
+                        jnp.where(low, last, pltpu.roll(first, width, axis=1)),
+                    )
+                halo = (act(halo) * inside).astype(jnp.bfloat16)
+                e = act(e_refs[j][:, tile(q, edge)].astype(jnp.float32))
+                m = act(m_refs[j][:, tile(q, mid)].astype(jnp.float32))
+                turned = pltpu.roll(m, width, axis=1).astype(jnp.bfloat16)
+                e = e.astype(jnp.bfloat16)
+                m = m.astype(jnp.bfloat16)
+                buf[slot, 0, natural, :edge] = jnp.where(low, halo, m)
+                buf[slot, 0, natural, edge:] = jnp.where(low, e, turned)
+                buf[slot, 1, natural, :edge] = e
+                buf[slot, 1, natural, edge:] = m
+                buf[slot, 2, natural, :edge] = jnp.where(low, m, halo)
+                buf[slot, 2, natural, edge:] = jnp.where(low, turned, e)
             y = jnp.zeros((3 * shard, length), jnp.float32)
             for a in range(3):
                 y = y + jnp.dot(
-                    tap_rows(w_ref, a, n * shard), buf[a], preferred_element_type=jnp.float32
+                    tap_rows(w_ref, a, n * shard), buf[slot, a], preferred_element_type=jnp.float32
                 )
             out = column_shift(y, shard, width)
             q = t * samples + i
-            cut = pl.ds(pl.multiple_of(q * edge, LANES), edge)
-            o_ref[t, i, :, :edge] = (out[:, :edge] + fe_ref[:, cut].astype(jnp.float32)).astype(
-                jnp.bfloat16
-            )
-            cut = pl.ds(pl.multiple_of(q * mid, LANES), mid)
-            o_ref[t, i, :, edge:] = (out[:, edge:] + fm_ref[:, cut].astype(jnp.float32)).astype(
-                jnp.bfloat16
-            )
-
-        @pl.loop(0, n)
-        def _(t):
-            for i in range(samples):
-                sample(t, i)
-
-    return call(
+            target = o_refs[t].at[i] if unrolled else o_refs[0].at[t, i]
+            target[:, :edge] = (
+                out[:, :edge] + fe_ref[:, tile(q, edge)].astype(jnp.float32)
+            ).astype(jnp.bfloat16)
+            target[:, edge:] = (
+                out[:, edge:] + fm_ref[:, tile(q, mid)].astype(jnp.float32)
+            ).astype(jnp.bfloat16)
+
+        if unrolled:
+            for q in range(count):
+                sample(q // samples, q % samples, q % 2)
+        else:
+
+            @pl.loop(0, n)
+            def _(t):
+                for i in range(samples):
+                    sample(t, i, 0)
+
+    result = call(
         body,
-        jax.ShapeDtypeStruct((n, samples, shard, length), jnp.bfloat16),
-        [pltpu.VMEM((3, n * shard, length), jnp.bfloat16)],
+        (shape,) * n if unrolled else shape,
+        [pltpu.VMEM((2 if unrolled else 1, 3, n * shard, length), jnp.bfloat16)],
         scalars=1,
         flops=6 * count * length * n * shard * 3 * shard,
     )(ends, *edges, *mids, above, below, weight, own_edges, own_mids)
+    return result if unrolled else [result[t] for t in range(n)]
 
 
 def split_dot(ones, column):
@@ -403,48 +468,67 @@
     return jnp.sum(summed, axis=1, keepdims=True)
 
 
-def attention(chunks, weights, out_weight, gain, spread, unpad, used, width, group):
-    pieces = len(chunks)
+def attention(where, chunks, weights, gain, spread, unpad, wide, width, group):
+    pieces, parts = len(chunks), len(weights)
     samples, rows, length = chunks[0].shape
-    channels = gain.shape[0] if unpad is None else unpad.shape[1]
+    channels = rows if unpad is None else unpad.shape[1]
     heads = channels // HEAD_DIM
     keys = pieces * length
     inner = length // width - 2
-    blocks = weights.shape[0]
+    packed = parts > 1
 
     def body(*refs):
-        c_refs = refs[:pieces]
-        w_ref, g_ref, a_ref, b_ref = refs[pieces : pieces + 4]
-        v_ref = None if out_weight is None else refs[-5]
-        o_ref, buf, query_buf, mixed_buf = refs[-4:]
+        where_ref, c_refs = refs[0], refs[1 : 1 + pieces]
+        w_refs = refs[1 + pieces : 1 + pieces + parts]
+        g_ref, a_ref, b_ref = refs[1 + pieces + parts : 4 + pieces + parts]
+        o_ref, buf, query_buf, mixed_buf = refs[-4 - packed : len(refs) - packed]
+        weight = refs[-1] if packed else w_refs[0]
+        if packed:
+            blocks, part, _ = weights[0].shape
+            steps = wide // part
+            for k, w in enumerate(w_refs):
+                at = where_ref[k]
+                for g in range(blocks):
+                    start = jnp.where(
+                        at < steps,
+                        g * wide + at * part,
+                        blocks * wide + g * (channels // blocks) + (at - steps) * part,
+                    )
+                    weight[pl.ds(pl.multiple_of(start, 16), part)] = w[g]
         for i in range(samples):
-            total = jnp.zeros((rows, 1), jnp.float32)
+            total = jnp.zeros((rows, LANES), jnp.float32)
             for c in c_refs:
-                total = total + jnp.sum(c[i].astype(jnp.float32), axis=1, keepdims=True)
+                for start in range(0, length, LANES):
+                    total = total + c[i, :, start : start + LANES].astype(jnp.float32)
+            total = jnp.sum(total, axis=1, keepdims=True)
             mean = split_dot(b_ref[...], split_dot(a_ref[...], total)) / (keys * group)
-            total = jnp.zeros((rows, 1), jnp.float32)
+            total = jnp.zeros((rows, LANES), jnp.float32)
             for c in c_refs:
-                away = c[i].astype(jnp.float32) - mean
-                total = total + jnp.sum(away * away, axis=1, keepdims=True)
+                for start in range(0, length, LANES):
+                    away = c[i, :, start : start + LANES].astype(jnp.float32) - mean
+                    total = total + away * away
+            total = jnp.sum(total, axis=1, keepdims=True)
             spread_of = split_dot(b_ref[...], split_dot(a_ref[...], total)) / (keys * group)
             scale = lax.rsqrt(spread_of + EPSILON) * g_ref[:, :1]
             for p, c in enumerate(c_refs):
                 normed = ((c[i].astype(jnp.float32) - mean) * scale).astype(jnp.bfloat16)
-                for g in range(blocks):
-                    low = max(0, (0 if p == 0 else channels) - g * used)
-                    if low < used:
-                        buf[g * used + low : (g + 1) * used, p * length : (p + 1) * length] = jnp.dot(
-                            w_ref[g, low:used], normed, preferred_element_type=jnp.float32
-                        ).astype(jnp.bfloat16)
-            queries = buf[:channels, :length].astype(jnp.float32) * HEAD_DIM ** (-0.5)
-            query_buf[...] = queries.T.astype(jnp.bfloat16)
+                if p == 0:
+                    queries = jnp.dot(
+                        weight[:channels, :rows], normed, preferred_element_type=jnp.float32
+                    )
+                    queries = queries.astype(jnp.bfloat16).astype(jnp.float32) * HEAD_DIM ** (-0.5)
+                    query_buf[...] = queries.T.astype(jnp.bfloat16)
+                buf[:, p * length : (p + 1) * length] = jnp.dot(
+                    weight[channels : 3 * channels, :rows],
+                    normed,
+                    preferred_element_type=jnp.float32,
+                ).astype(jnp.bfloat16)
 
             @pl.loop(0, heads // 2)
             def _(two):
                 lanes = pl.ds(pl.multiple_of(two * LANES, LANES), LANES)
-                at = channels + two * LANES
-                k_two = buf[pl.ds(pl.multiple_of(at, LANES), LANES)]
-                v_two = buf[pl.ds(pl.multiple_of(at + channels, LANES), LANES)]
+                k_two = buf[pl.ds(pl.multiple_of(two * LANES, LANES), LANES)]
+                v_two = buf[pl.ds(pl.multiple_of(channels + two * LANES, LANES), LANES)]
                 q_two = query_buf[:, lanes]
                 pair = []
                 for h in range(2):
@@ -464,16 +548,15 @@
             own = c_refs[0][i].astype(jnp.float32).T
             if unpad is not None:
                 own = jnp.dot(
-                    own.astype(jnp.bfloat16), refs[pieces + 4][...], preferred_element_type=jnp.float32
+                    own.astype(jnp.bfloat16),
+                    refs[4 + pieces + parts][...],
+                    preferred_element_type=jnp.float32,
                 )
-            if out_weight is None:
-                kept = channels // blocks
-                v_rows = [w_ref[g, used : used + kept] for g in range(blocks)]
-                v_rows = jnp.concatenate(v_rows, axis=0)
-            else:
-                v_rows = v_ref[...]
             result = own + lax.dot_general(
-                mixed_buf[...], v_rows, NT, preferred_element_type=jnp.float32
+                mixed_buf[...],
+                weight[3 * channels :, :channels],
+                NT,
+                preferred_element_type=jnp.float32,
             )
             result = result.astype(jnp.bfloat16)
             o_ref[i, 0] = result[:width]
@@ -481,20 +564,22 @@
             for r in range(inner):
                 o_ref[i, 1 + r] = result[(2 + r) * width : (3 + r) * width]
 
-    operands = [*chunks, weights, gain, spread.T, spread]
+    operands = [*chunks, *weights, gain, spread.T, spread]
     if unpad is not None:
         operands.append(unpad)
-    if out_weight is not None:
-        operands.append(out_weight)
+    scratch = [
+        pltpu.VMEM((2 * channels, keys), jnp.bfloat16),
+        pltpu.VMEM((length, channels), jnp.bfloat16),
+        pltpu.VMEM((length, channels), jnp.bfloat16),
+    ]
+    if packed:
+        scratch.append(pltpu.VMEM((4 * channels, rows), jnp.bfloat16))
     return call(
         body,
         jax.ShapeDtypeStruct((samples, length // width, width, channels), jnp.bfloat16),
-        [
-            pltpu.VMEM((3 * channels, keys), jnp.bfloat16),
-            pltpu.VMEM((length, channels), jnp.bfloat16),
-            pltpu.VMEM((length, channels), jnp.bfloat16),
-        ],
-    )(*operands)
+        scratch,
+        scalars=1,
+    )(where, *operands)
 
 
 def pad_rows(values, rows, axis):
@@ -559,8 +644,9 @@
     flat = features.reshape(samples, length, channels)
     own_stats = local_stats(flat, members(channels, channels, channels, group), group)
     edges = ring(jnp.concatenate([flat[:, :width], flat[:, length - width :]], axis=1))
-    above = shift_rows(jnp.concatenate([e[:, width:] for e in edges], axis=0), 1)
-    below = shift_rows(jnp.concatenate([e[:, :width] for e in edges], axis=0), -1)
+    last, first = halo_rows(edges, width)
+    above = shift_rows(last, 1)
+    below = shift_rows(first, -1)
     own_stats = in_plane_stats(own_stats)
     mids = rows_message(own_stats, norm_gains[:1], entries, flat[:, width : length - width])
     mids = ring(mids)
@@ -571,14 +657,21 @@
         [pad_blocks(attn_weight.T, 1), pad_rows(out_weight.T, n * shard, 1)], axis=0
     )
     turned = lax.dynamic_slice_in_dim(pad_rows(turned, part * planes, 0), row * part, part, 0)
-    turned = lax.all_gather(turned, ("fsdp", "spatial"), axis=0)
-    turned = turned.reshape(n, planes * part, n * shard)
-
-    projection, used, last_weight = turned, wide, None
-    if shard != kept:
-        projection = turned[:, :wide].reshape(1, n * wide, n * shard)
-        used = n * wide
-        last_weight = turned[:, wide : wide + kept, :channels].reshape(channels, channels)
+    places = ((mine - np.arange(n)) % n).astype(jnp.int32)
+    pieces = ring(turned[None])
+    turned = place(places, pieces, 0)
+    projection, from_rows = in_plane(turned)
+    if wide % part or kept % part:
+        turned = place(from_rows, projection, 1)
+        projection = [
+            jnp.concatenate(
+                [
+                    turned[:, :wide].reshape(n * wide, n * shard),
+                    turned[:, wide : wide + kept].reshape(channels, n * shard),
+                ]
+            )
+        ]
+
     first_weight = pad_rows(conv_first.T, shard, 0)
     second_weight = pad_rows(pad_blocks(conv_second.T, 1), shard, 0)
     bias = time_bias(step_index, roster, time_weight, block(temb_weight, 1), shard)
@@ -601,9 +694,9 @@
     )
 
     edges = ring(edges)
-    stacked = jnp.concatenate(edges, axis=0)
-    above = shift_rows(stacked, 1)
-    below = shift_rows(stacked, -1)
+    last, first = halo_columns(edges, width)
+    above = shift_rows(last, 1)
+    below = shift_rows(first, -1)
     gain = pad_rows(block(norm_gains[1:2], 1), shard, 1)
     own_stats = in_plane_stats(own_stats)
     mids = columns_message(own_stats, gain, entries, mids)
@@ -631,13 +724,13 @@
         at = np.where(at % shard < kept, at // shard * kept + at % shard, -1)
         unpad = jnp.asarray(at[:, None] == np.arange(channels)[None, :], jnp.bfloat16)
     return attention(
+        from_rows,
         chunks,
         projection,
-        last_weight,
         gain,
         members(n * shard, shard, kept, group),
         unpad,
-        used,
+        wide,
         width,
         group,
     )

time: 210 us -> 180 us (0.86)
  waiting for transfers between devices: 70.1 us -> 52.5 us
  between operations: 14.3 us -> 0.89 us
  local copies, waits for them, and re-layouts: 18.2 us -> 9.27 us
  starting transfers between devices: 47.4 us -> 54.5 us
  Pallas kernels: 50.8 us -> 55.2 us
    ppermute x6, waiting for transfers between devices: 15.9 us -> 6.86 us  [in_plane_stats(): lax.ppermute(values, 'spatial', [(i, i ^ size) for i in range(planes)])]
    ppermute x18 -> x24, waiting for transfers between devices: 53.3 us -> 44.7 us  [shift(): lax.ppermute(values, axis, [(i, (i + step) % count) for i in range(count)])]
    ppermute x18 -> x24, starting transfers between devices: 32.8 us -> 41.1 us  [shift(): lax.ppermute(values, axis, [(i, (i + step) % count) for i in range(count)])]
    pallas_call x8 -> x11, Pallas kernels: 50.8 us -> 55.2 us  [run(): pl.pallas_call(body, out_shape=out_shape, in_specs=specs, out_specs=outs,...]
    unnamed x43 -> x50, local copies, waits for them, and re-layouts: 6.88 us -> 2.98 us
    slice x3 -> x0, local copies, waits for them, and re-layouts: 2.83 us -> none  [local(): e[:, :width]]
  transfers between devices with their start and end apart: 33 -> 42, of which waited for: 13 -> 16; matrix products, arithmetic and copies ran while one was open for 10% -> 6% of each run, Pallas kernels for 13% -> 14%
where the time goes in v1:
time: 180 us
  Pallas kernels  55.2 us (31%)
  starting transfers between devices  54.5 us (30%)
  waiting for transfers between devices  52.5 us (29%)
  local copies, waits for them, and re-layouts  9.27 us (5%)
  other arithmetic  7.5 us (4%)
    pallas_call x11, Pallas kernels, run(): pl.pallas_call(body, out_shape=out_shape, in_specs=specs, out_specs=outs,...  55.2 us
    ppermute x24, waiting for transfers between devices, shift(): lax.ppermute(values, axis, [(i, (i + step) % count) for i in range(count)])  44.7 us
    ppermute x24, starting transfers between devices, shift(): lax.ppermute(values, axis, [(i, (i + step) % count) for i in range(count)])  41.1 us
    ppermute x4, starting transfers between devices, shift_rows(): return lax.ppermute(values, 'spatial', pairs)  7.63 us
    ppermute x6, waiting for transfers between devices, in_plane_stats(): lax.ppermute(values, 'spatial', [(i, i ^ size) for i in range(planes)])  6.86 us
    ppermute x6, starting transfers between devices, in_plane_stats(): lax.ppermute(values, 'spatial', [(i, i ^ size) for i in range(planes)])  4.63 us
  transfers between devices with their start and end apart: 42, of which 16 were waited for; matrix products, arithmetic and copies ran while one was open for 6% of the time, Pallas kernels for 14%

profile of v1, /device:TPU:0, one launch (start us, length us, event | category | flops | bytes accessed | tf_op | source)
XLA Modules:
  0.0 179.8 jit_solution(14767395334624271398)
XLA Ops:
  0.0 1.1 fusion.6
  1.1 3.1 %collective-permute-start = (bf16[1,128,640]{2,1,0:T(8,128)(2,1)S(1)}, bf16[1,128,640]{2,1,0:T(8,128)(2,1)}, u32[]{:S(2)}, u32[]{:S(2)}) collective-permute-start(bf16[1,128,640]{2,1,0:T(8,128)(2,1)S(1)} %pad_maximum_fusion.refs_0_.refs_1_), channel_id=1, source_target_pairs={{0,1},{1,2},{2,3},{3,0},{4,5},{5,6},{6,7},{7,4},{8,9},{9,10},{10,1... | collective-permute-start | bytes 491528 | tf_op jit(solution)/shard_map/ppermute | solution.py:46
  4.2 2.6 %collective-permute-start.1 = (bf16[1,128,640]{2,1,0:T(8,128)(2,1)S(1)}, bf16[1,128,640]{2,1,0:T(8,128)(2,1)}, u32[]{:S(2)}, u32[]{:S(2)}) collective-permute-start(bf16[1,128,640]{2,1,0:T(8,128)(2,1)S(1)} %pad_maximum_fusion.refs_0_.refs_1_), channel_id=1, source_target_pairs={{0,2},{1,3},{2,0},{3,1},{4,6},{5,7},{6,4},{7,5},{8,10},{9,11},{10,... | collective-permute-start | bytes 491528 | tf_op jit(solution)/shard_map/ppermute | solution.py:46
  6.8 1.3 collective-permute-start.2
  8.2 2.4 %shard_map.163 = f32[2,640]{1,0:T(2,128)} custom-call(bf16[1,256,640]{2,1,0:T(8,128)(2,1)} %bitcast.14, bf16[640,128]{1,0:T(8,128)(2,1)} %constant.64.clone.g_ref.refs_19_), custom_call_target="tpu_custom_call" | custom-call | tf_op jit(solution)/shard_map/pallas_call | solution.py:29
  10.5 1.5 constant_dynamic-slice_fusion.1.t_ref
  12.0 0.6 slice_reduce_fusion
  12.7 1.6 collective-permute-start.4
  14.2 2.2 %collective-permute-done.4 = f32[2,2,640]{2,1,0:T(2,128)S(1)} collective-permute-done((f32[2,2,640]{2,1,0:T(2,128)S(1)}, f32[2,2,640]{2,1,0:T(2,128)S(1)}, u32[]{:S(2)}, u32[]{:S(2)}) %collective-permute-start.4) | collective-permute-done | bytes 10272 | tf_op jit(solution)/shard_map/ppermute | solution.py:633
  16.4 1.6 collective-permute-start.5
  18.0 0.6 pad_add_fusion.1.refs_0_
  18.6 1.6 slice.26.m_ref
  20.9 3.4 %shard_map.166.refs_12_ = f32[160,128]{1,0:T(8,128)} custom-call(s32[1]{0:T(128)S(6)} %copy.18.i_ref, f32[1,50]{1,0:T(1,128)} %bitcast.26, f32[320,1280]{1,0:T(8,128)} %w_ref.1, f32[1280,160]{1,0:T(8,128)} %constant_dynamic-slice_fusion.1.t_ref), custom_call_target="tpu_custom_call" | custom-call | tf_op jit(solution)/shard_map/pallas_call | solution.py:29
  24.3 2.0 %shard_map.165 = (bf16[4,64,640]{2,1,0:T(8,128)(2,1)}, bf16[4,64,640]{2,1,0:T(8,128)(2,1)}) custom-call(bf16[1,128,640]{2,1,0:T(8,128)(2,1)} %copy-done.1, bf16[1,128,640]{2,1,0:T(8,128)(2,1)} %collective-permute-done.refs_1_.refs_2_, bf16[1,128,640]{2,1,0:T(8,128)(2,1)} %collective-permute-done.1.refs_2_.refs_3_, ...), custom_call_target="tpu_custom_call" | custom-call | tf_op jit(solution)/shard_map/pallas_call | solution.py:29
  26.3 1.3 collective-permute-start.10
  27.6 3.0 %collective-permute-start.9 = (bf16[4,64,640]{2,1,0:T(8,128)(2,1)}, bf16[4,64,640]{2,1,0:T(8,128)(2,1)S(1)}, u32[]{:S(2)}, u32[]{:S(2)}) collective-permute-start(bf16[4,64,640]{2,1,0:T(8,128)(2,1)} %get-tuple-element.18), channel_id=1, source_target_pairs={{0,4},{4,8},{8,12},{12,16},{16,20},{20,24},{24,28},{1,5},{5,9},{9,... | collective-permute-start | bytes 983048 | tf_op jit(solution)/shard_map/ppermute | solution.py:742
  30.7 0.6 pad_maximum_fusion.2.p_ref
  31.3 1.7 shard_map.164.refs_5_
  33.0 0.7 collective-permute-start.6
  34.1 2.8 %collective-permute-start.8 = (bf16[1,144,640]{2,1,0:T(8,128)(2,1)}, bf16[1,144,640]{2,1,0:T(8,128)(2,1)S(1)}, u32[]{:S(2)}, u32[]{:S(2)}) collective-permute-start(bf16[1,144,640]{2,1,0:T(8,128)(2,1)} %shard_map.164.refs_5_), channel_id=1, source_target_pairs={{0,3},{1,0},{2,1},{3,2},{4,7},{5,4},{6,5},{7,6},{8,11},{9,8},{10,9... | collective-permute-start | bytes 552968 | tf_op jit(solution)/shard_map/ppermute | solution.py:46
  36.9 0.8 fusion.refs_14_
  37.6 5.0 %collective-permute-done.6.refs_6_ = bf16[1,144,640]{2,1,0:T(8,128)(2,1)S(1)} collective-permute-done((bf16[1,144,640]{2,1,0:T(8,128)(2,1)}, bf16[1,144,640]{2,1,0:T(8,128)(2,1)S(1)}, u32[]{:S(2)}, u32[]{:S(2)}) %collective-permute-start.6) | collective-permute-done | bytes 184352 | tf_op jit(solution)/shard_map/ppermute | solution.py:46
  42.6 7.6 %collective-permute-done.7.refs_7_ = bf16[1,144,640]{2,1,0:T(8,128)(2,1)S(1)} collective-permute-done((bf16[1,144,640]{2,1,0:T(8,128)(2,1)}, bf16[1,144,640]{2,1,0:T(8,128)(2,1)S(1)}, u32[]{:S(2)}, u32[]{:S(2)}) %collective-permute-start.7) | collective-permute-done | bytes 184352 | tf_op jit(solution)/shard_map/ppermute | solution.py:46
  50.3 0.6 copy-done.23
  51.0 0.7 copy-done.21
  51.8 7.7 %shard_map.167 = (bf16[160,512]{1,0:T(8,128)(2,1)}, bf16[160,512]{1,0:T(8,128)(2,1)}, f32[8,160]{1,0:T(8,128)}, bf16[160,512]{1,0:T(8,128)(2,1)}, bf16[160,512]{1,0:T(8,128)(2,1)}) custom-call(s32[3]{0:T(128)} %pad_add_fusion.1.refs_0_, bf16[1,128,640]{2,1,0:T(8,128)(2,1)} %copy-done.1, bf16[1,128,640]{2,1,0:T(8,128)(2,1)} %collective-permute-done.refs_1_.refs_2_, ...), custom_call_target="tpu_custom_call" | custom-call | flops 1887436800 | tf_op jit(solution)/shard_map/pallas_call | solution.py:29
  59.4 1.4 collective-permute-done.14
  60.8 0.7 pad_maximum_fusion.5
  61.5 1.5 collective-permute-start.15
  63.0 0.9 fusion.2.refs_0_
  63.9 4.5 %collective-permute-start.32 = (bf16[1,80,640]{2,1,0:T(8,128)(2,1)S(1)}, bf16[1,80,640]{2,1,0:T(8,128)(2,1)S(1)}, u32[]{:S(2)}, u32[]{:S(2)}) collective-permute-start(bf16[1,80,640]{2,1,0:T(8,128)(2,1)S(1)} %fusion.2.refs_0_), channel_id=1, source_target_pairs={{0,1},{1,2},{2,3},{3,0},{4,5},{5,6},{6,7},{7,4},{8,9},{9,10},{10,1... | collective-permute-start | bytes 307208 | tf_op jit(solution)/shard_map/ppermute | solution.py:46
  68.5 3.8 %collective-permute-start.13 = (bf16[160,512]{1,0:T(8,128)(2,1)}, bf16[160,512]{1,0:T(8,128)(2,1)S(1)}, u32[]{:S(2)}, u32[]{:S(2)}) collective-permute-start(bf16[160,512]{1,0:T(8,128)(2,1)} %get-tuple-element.20.refs_0_.refs_1_), channel_id=1, source_target_pairs={{0,3},{1,0},{2,1},{3,2},{4,7},{5,4},{6,5},{7,6},{8,11},{9,8},{10,9... | collective-permute-start | bytes 491528 | tf_op jit(solution)/shard_map/ppermute | solution.py:46
  72.2 0.7 pad_maximum_fusion.3
  72.9 0.6 constant_dynamic-slice_fusion.g_ref
  73.5 3.3 %collective-permute-done.16 = f32[4,8,160]{2,1,0:T(8,128)S(1)} collective-permute-done((f32[4,8,160]{2,1,0:T(8,128)S(1)}, f32[4,8,160]{2,1,0:T(8,128)S(1)}, u32[]{:S(2)}, u32[]{:S(2)}) %collective-permute-start.16) | collective-permute-done | bytes 20512 | tf_op jit(solution)/shard_map/ppermute | solution.py:633
  76.8 2.0 %collective-permute-start.33 = (bf16[1,80,640]{2,1,0:T(8,128)(2,1)S(1)}, bf16[1,80,640]{2,1,0:T(8,128)(2,1)S(1)}, u32[]{:S(2)}, u32[]{:S(2)}) collective-permute-start(bf16[1,80,640]{2,1,0:T(8,128)(2,1)S(1)} %fusion.2.refs_0_), channel_id=1, source_target_pairs={{0,2},{1,3},{2,0},{3,1},{4,6},{5,7},{6,4},{7,5},{8,10},{9,11},{10,... | collective-permute-start | bytes 307208 | tf_op jit(solution)/shard_map/ppermute | solution.py:46
  78.9 0.9 collective-permute-start.34
  79.8 1.3 pad_maximum_fusion.1.p_ref
  81.1 1.8 %shard_map.168.refs_5_ = bf16[160,640]{1,0:T(8,128)(2,1)} custom-call(f32[8,8,160]{2,1,0:T(8,128)} %pad_maximum_fusion.1.p_ref, f32[1,160]{1,0:T(1,128)} %constant_dynamic-slice_fusion.g_ref, bf16[160,512]{1,0:T(8,128)(2,1)} %get-tuple-element.22.m_ref), custom_call_target="tpu_custom_call" | custom-call | tf_op jit(solution)/shard_map/pallas_call | solution.py:29
  82.9 1.4 collective-permute-done.12.refs_2_.refs_3_
  84.4 5.8 %collective-permute-start.17 = (bf16[160,640]{1,0:T(8,128)(2,1)}, bf16[160,640]{1,0:T(8,128)(2,1)}, u32[]{:S(2)}, u32[]{:S(2)}) collective-permute-start(bf16[160,640]{1,0:T(8,128)(2,1)} %shard_map.168.refs_5_), channel_id=1, source_target_pairs={{0,1},{1,2},{2,3},{3,0},{4,5},{5,6},{6,7},{7,4},{8,9},{9,10},{10,1... | collective-permute-start | bytes 614408 | tf_op jit(solution)/shard_map/ppermute | solution.py:46
  90.2 3.3 %collective-permute-start.18 = (bf16[160,640]{1,0:T(8,128)(2,1)}, bf16[160,640]{1,0:T(8,128)(2,1)}, u32[]{:S(2)}, u32[]{:S(2)}) collective-permute-start(bf16[160,640]{1,0:T(8,128)(2,1)} %shard_map.168.refs_5_), channel_id=1, source_target_pairs={{0,2},{1,3},{2,0},{3,1},{4,6},{5,7},{6,4},{7,5},{8,10},{9,11},{10,... | collective-permute-start | bytes 614408 | tf_op jit(solution)/shard_map/ppermute | solution.py:46
  93.5 2.3 %shard_map.169 = (bf16[640,256]{1,0:T(8,128)(2,1)}, bf16[640,256]{1,0:T(8,128)(2,1)}) custom-call(bf16[160,512]{1,0:T(8,128)(2,1)} %get-tuple-element.20.refs_0_.refs_1_, bf16[160,512]{1,0:T(8,128)(2,1)} %copy-done.13, bf16[160,512]{1,0:T(8,128)(2,1)} %copy-done.14, bf16[160,512]{1,0:T(8,128)(2,1)} %copy-done.15), custom_call_target="tpu_custom_call" | custom-call | tf_op jit(solution)/shard_map/pallas_call | solution.py:29
  95.8 2.0 %collective-permute-start.20 = (bf16[640,256]{1,0:T(8,128)(2,1)}, bf16[640,256]{1,0:T(8,128)(2,1)}, u32[]{:S(2)}, u32[]{:S(2)}) collective-permute-start(bf16[640,256]{1,0:T(8,128)(2,1)} %get-tuple-element.23), channel_id=1, source_target_pairs={{0,4},{4,8},{8,12},{12,16},{16,20},{20,24},{24,28},{1,5},{5,9},{9,... | collective-permute-start | bytes 983048 | tf_op jit(solution)/shard_map/ppermute | solution.py:742
  98.0 1.3 collective-permute-start.21
  99.8 1.9 %shard_map.172.refs_9_ = bf16[4,80,640]{2,1,0:T(8,128)(2,1)} custom-call(s32[4]{0:T(128)} %and_select_fusion.w_ref, bf16[1,80,640]{2,1,0:T(8,128)(2,1)} %copy-done.2, bf16[1,80,640]{2,1,0:T(8,128)(2,1)} %copy-done.16, bf16[1,80,640]{2,1,0:T(8,128)(2,1)} %copy-done.17, bf16[1,80,640]{2,1,0:T(8,128)(2,1)} %collective-permute-done.34.refs_3_), custom_call_target="tpu_custom_call" | custom-call | tf_op jit(solution)/shard_map/pallas_call | solution.py:29
  101.7 2.6 %collective-permute-start.35 = (bf16[4,80,640]{2,1,0:T(8,128)(2,1)}, bf16[4,80,640]{2,1,0:T(8,128)(2,1)S(1)}, u32[]{:S(2)}, u32[]{:S(2)}) collective-permute-start(bf16[4,80,640]{2,1,0:T(8,128)(2,1)} %shard_map.172.refs_9_), channel_id=1, source_target_pairs={{0,8},{4,12},{8,16},{12,20},{16,24},{20,28},{24,0},{28,4},{1,9},{5... | collective-permute-start | bytes 1228808 | tf_op jit(solution)/shard_map/ppermute | solution.py:46
  104.3 1.6 collective-permute-done.18.refs_7_
  105.9 4.0 %collective-permute-done.19.refs_8_ = bf16[160,640]{1,0:T(8,128)(2,1)} collective-permute-done((bf16[160,640]{1,0:T(8,128)(2,1)}, bf16[160,640]{1,0:T(8,128)(2,1)}, u32[]{:S(2)}, u32[]{:S(2)}) %collective-permute-start.19) | collective-permute-done | bytes 204832 | tf_op jit(solution)/shard_map/ppermute | solution.py:46
  109.9 7.5 %shard_map.170 = (bf16[1,160,256]{2,1,0:T(8,128)(2,1)}, bf16[1,160,256]{2,1,0:T(8,128)(2,1)}, bf16[1,160,256]{2,1,0:T(8,128)(2,1)}, bf16[1,160,256]{2,1,0:T(8,128)(2,1)}) custom-call(s32[3]{0:T(128)} %pad_add_fusion.1.refs_0_, bf16[160,512]{1,0:T(8,128)(2,1)} %get-tuple-element.20.refs_0_.refs_1_, bf16[160,512]{1,0:T(8,128)(2,1)} %copy-done.13, ...), custom_call_target="tpu_custom_call" | custom-call | flops 1887436800 | tf_op jit(solution)/shard_map/pallas_call | solution.py:29
  117.5 4.0 %collective-permute-start.22 = (bf16[1,160,256]{2,1,0:T(8,128)(2,1)}, bf16[1,160,256]{2,1,0:T(8,128)(2,1)}, u32[]{:S(2)}, u32[]{:S(2)}) collective-permute-start(bf16[1,160,256]{2,1,0:T(8,128)(2,1)} %get-tuple-element.28), channel_id=1, source_target_pairs={{0,3},{1,0},{2,1},{3,2},{4,7},{5,4},{6,5},{7,6},{8,11},{9,8},{10,9... | collective-permute-start | bytes 245768 | tf_op jit(solution)/shard_map/ppermute | solution.py:46
  121.4 2.5 %collective-permute-done.36.refs_11_ = bf16[4,80,640]{2,1,0:T(8,128)(2,1)S(1)} collective-permute-done((bf16[4,80,640]{2,1,0:T(8,128)(2,1)}, bf16[4,80,640]{2,1,0:T(8,128)(2,1)S(1)}, u32[]{:S(2)}, u32[]{:S(2)}) %collective-permute-start.36) | collective-permute-done | bytes 409632 | tf_op jit(solution)/shard_map/ppermute | solution.py:46
  124.6 3.7 %collective-permute-done.23.refs_2_ = bf16[1,160,256]{2,1,0:T(8,128)(2,1)} collective-permute-done((bf16[1,160,256]{2,1,0:T(8,128)(2,1)}, bf16[1,160,256]{2,1,0:T(8,128)(2,1)}, u32[]{:S(2)}, u32[]{:S(2)}) %collective-permute-start.23) | collective-permute-done | bytes 81952 | tf_op jit(solution)/shard_map/ppermute | solution.py:46
  128.9 6.0 %collective-permute-done.24.refs_3_ = bf16[1,160,256]{2,1,0:T(8,128)(2,1)} collective-permute-done((bf16[1,160,256]{2,1,0:T(8,128)(2,1)}, bf16[1,160,256]{2,1,0:T(8,128)(2,1)}, u32[]{:S(2)}, u32[]{:S(2)}) %collective-permute-start.24) | collective-permute-done | bytes 81952 | tf_op jit(solution)/shard_map/ppermute | solution.py:46
  134.9 1.8 shard_map.171.refs_1_
  136.7 0.7 collective-permute-start.25
  137.4 1.5 collective-permute-start.26
  138.9 1.0 collective-permute-start.27
  140.3 8.0 %collective-permute-done.25.refs_2_ = bf16[1,640,256]{2,1,0:T(8,128)(2,1)S(1)} collective-permute-done((bf16[1,640,256]{2,1,0:T(8,128)(2,1)}, bf16[1,640,256]{2,1,0:T(8,128)(2,1)S(1)}, u32[]{:S(2)}, u32[]{:S(2)}) %collective-permute-start.25) | collective-permute-done | bytes 327712 | tf_op jit(solution)/shard_map/ppermute | solution.py:46
  148.4 0.7 copy-done.5
  149.1 4.2 %collective-permute-done.26.refs_3_ = bf16[1,640,256]{2,1,0:T(8,128)(2,1)S(1)} collective-permute-done((bf16[1,640,256]{2,1,0:T(8,128)(2,1)}, bf16[1,640,256]{2,1,0:T(8,128)(2,1)S(1)}, u32[]{:S(2)}, u32[]{:S(2)}) %collective-permute-start.26) | collective-permute-done | bytes 327712 | tf_op jit(solution)/shard_map/ppermute | solution.py:46
  153.9 0.7 pad_add_fusion.refs_0_
  156.2 0.9 broadcast_in_dim.31.refs_17_
  157.1 22.7 %shard_map.173 = bf16[1,4,64,640]{3,2,1,0:T(8,128)(2,1)} custom-call(s32[8]{0:T(128)} %pad_add_fusion.refs_0_, bf16[1,640,256]{2,1,0:T(8,128)(2,1)} %shard_map.171.refs_1_, bf16[1,640,256]{2,1,0:T(8,128)(2,1)} %copy-done.5, bf16[1,640,256]{2,1,0:T(8,128)(2,1)} %copy-done.6, bf16[1,640,256]{2,1,0:T(8,128)(2,1)} %copy-done.7, bf16[1,640,256]{2,1,0:T(8,128)(2,1)} %copy-done.8, ...), custom_call_target="tpu_custom_call" | custom-call | tf_op jit(solution)/shard_map/pallas_call | solution.py:29
  (102 shorter events, 5.3 us)
Async XLA Ops:
  0.0 10.5 %copy-start = (f32[1280,640]{1,0:T(8,128)S(1)}, f32[1280,640]{1,0:T(8,128)}, u32[]{:S(2)}) copy-start(f32[1280,640]{1,0:T(8,128)} %param.21) | copy-start | bytes 9830404
  0.0 12.0 %copy-start.19 = (f32[3,640]{1,0:T(4,128)S(1)}, f32[3,640]{1,0:T(4,128)}, u32[]{:S(2)}) copy-start(f32[3,640]{1,0:T(4,128)} %param.22) | copy-start | bytes 23044
  1.1 23.2 %copy-start.1 = (bf16[1,128,640]{2,1,0:T(8,128)(2,1)}, bf16[1,128,640]{2,1,0:T(8,128)(2,1)S(1)}, u32[]{:S(2)}) copy-start(bf16[1,128,640]{2,1,0:T(8,128)(2,1)S(1)} %pad_maximum_fusion.refs_0_.refs_1_) | copy-start | bytes 491524
  1.1 23.1 %collective-permute-start = (bf16[1,128,640]{2,1,0:T(8,128)(2,1)S(1)}, bf16[1,128,640]{2,1,0:T(8,128)(2,1)}, u32[]{:S(2)}, u32[]{:S(2)}) collective-permute-start(bf16[1,128,640]{2,1,0:T(8,128)(2,1)S(1)} %pad_maximum_fusion.refs_0_.refs_1_), channel_id=1, source_target_pairs={{0,1},{1,2},{2,3},{3,0},{4,5},{5,6},{6,7},{7,4},{8,9},{9,10},{10,1... | collective-permute-start | bytes 491528 | tf_op jit(solution)/shard_map/ppermute | solution.py:46
  4.2 20.0 %collective-permute-start.1 = (bf16[1,128,640]{2,1,0:T(8,128)(2,1)S(1)}, bf16[1,128,640]{2,1,0:T(8,128)(2,1)}, u32[]{:S(2)}, u32[]{:S(2)}) collective-permute-start(bf16[1,128,640]{2,1,0:T(8,128)(2,1)S(1)} %pad_maximum_fusion.refs_0_.refs_1_), channel_id=1, source_target_pairs={{0,2},{1,3},{2,0},{3,1},{4,6},{5,7},{6,4},{7,5},{8,10},{9,11},{10,... | collective-permute-start | bytes 491528 | tf_op jit(solution)/shard_map/ppermute | solution.py:46
  6.8 17.5 %collective-permute-start.2 = (bf16[1,128,640]{2,1,0:T(8,128)(2,1)S(1)}, bf16[1,128,640]{2,1,0:T(8,128)(2,1)}, u32[]{:S(2)}, u32[]{:S(2)}) collective-permute-start(bf16[1,128,640]{2,1,0:T(8,128)(2,1)S(1)} %pad_maximum_fusion.refs_0_.refs_1_), channel_id=1, source_target_pairs={{0,3},{1,0},{2,1},{3,2},{4,7},{5,4},{6,5},{7,6},{8,11},{9,8},{10,9... | collective-permute-start | bytes 491528 | tf_op jit(solution)/shard_map/ppermute | solution.py:46
  10.5 2.1 %copy-start.18 = (f32[2,640]{1,0:T(2,128)S(1)}, f32[2,640]{1,0:T(2,128)}, u32[]{:S(2)}) copy-start(f32[2,640]{1,0:T(2,128)} %shard_map.163) | copy-start | bytes 15364
  10.5 2.1 %collective-permute-start.3 = (f32[1,2,640]{2,1,0:T(2,128)}, f32[1,2,640]{2,1,0:T(2,128)S(1)}, u32[]{:S(2)}, u32[]{:S(2)}) collective-permute-start(f32[1,2,640]{2,1,0:T(2,128)} %bitcast.18), channel_id=1, source_target_pairs={{0,4},{4,0},{8,12},{12,8},{16,20},{20,16},{24,28},{28,24},{1,5},{5... | collective-permute-start | bytes 15368 | tf_op jit(solution)/shard_map/ppermute | solution.py:633
  12.7 3.7 %collective-permute-start.4 = (f32[2,2,640]{2,1,0:T(2,128)S(1)}, f32[2,2,640]{2,1,0:T(2,128)S(1)}, u32[]{:S(2)}, u32[]{:S(2)}) collective-permute-start(f32[2,2,640]{2,1,0:T(2,128)S(1)} %pad_maximum_fusion.6), channel_id=1, source_target_pairs={{0,8},{4,12},{8,0},{12,4},{16,24},{20,28},{24,16},{28,20},{1,9},{5... | collective-permute-start | bytes 30728 | tf_op jit(solution)/shard_map/ppermute | solution.py:633
  16.4 14.3 %collective-permute-start.5 = (f32[4,2,640]{2,1,0:T(2,128)S(1)}, f32[4,2,640]{2,1,0:T(2,128)S(1)}, u32[]{:S(2)}, u32[]{:S(2)}) collective-permute-start(f32[4,2,640]{2,1,0:T(2,128)S(1)} %pad_maximum_fusion.4), channel_id=1, source_target_pairs={{0,16},{4,20},{8,24},{12,28},{16,0},{20,4},{24,8},{28,12},{1,17},{... | collective-permute-start | bytes 61448 | tf_op jit(solution)/shard_map/ppermute | solution.py:633
  26.3 23.9 %collective-permute-start.10 = (bf16[4,64,640]{2,1,0:T(8,128)(2,1)}, bf16[4,64,640]{2,1,0:T(8,128)(2,1)S(1)}, u32[]{:S(2)}, u32[]{:S(2)}) collective-permute-start(bf16[4,64,640]{2,1,0:T(8,128)(2,1)} %get-tuple-element.19), channel_id=1, source_target_pairs={{4,0},{8,4},{12,8},{16,12},{20,16},{24,20},{28,24},{5,1},{9,5},{13... | collective-permute-start | bytes 983048 | tf_op jit(solution)/shard_map/ppermute | solution.py:742
  27.6 22.7 %collective-permute-start.9 = (bf16[4,64,640]{2,1,0:T(8,128)(2,1)}, bf16[4,64,640]{2,1,0:T(8,128)(2,1)S(1)}, u32[]{:S(2)}, u32[]{:S(2)}) collective-permute-start(bf16[4,64,640]{2,1,0:T(8,128)(2,1)} %get-tuple-element.18), channel_id=1, source_target_pairs={{0,4},{4,8},{8,12},{12,16},{16,20},{20,24},{24,28},{1,5},{5,9},{9,... | collective-permute-start | bytes 983048 | tf_op jit(solution)/shard_map/ppermute | solution.py:742
  33.0 9.6 %collective-permute-start.6 = (bf16[1,144,640]{2,1,0:T(8,128)(2,1)}, bf16[1,144,640]{2,1,0:T(8,128)(2,1)S(1)}, u32[]{:S(2)}, u32[]{:S(2)}) collective-permute-start(bf16[1,144,640]{2,1,0:T(8,128)(2,1)} %shard_map.164.refs_5_), channel_id=1, source_target_pairs={{0,1},{1,2},{2,3},{3,0},{4,5},{5,6},{6,7},{7,4},{8,9},{9,10},{10,1... | collective-permute-start | bytes 552968 | tf_op jit(solution)/shard_map/ppermute | solution.py:46
  33.7 16.6 %collective-permute-start.7 = (bf16[1,144,640]{2,1,0:T(8,128)(2,1)}, bf16[1,144,640]{2,1,0:T(8,128)(2,1)S(1)}, u32[]{:S(2)}, u32[]{:S(2)}) collective-permute-start(bf16[1,144,640]{2,1,0:T(8,128)(2,1)} %shard_map.164.refs_5_), channel_id=1, source_target_pairs={{0,2},{1,3},{2,0},{3,1},{4,6},{5,7},{6,4},{7,5},{8,10},{9,11},{10,... | collective-permute-start | bytes 552968 | tf_op jit(solution)/shard_map/ppermute | solution.py:46
  34.1 16.2 %collective-permute-start.8 = (bf16[1,144,640]{2,1,0:T(8,128)(2,1)}, bf16[1,144,640]{2,1,0:T(8,128)(2,1)S(1)}, u32[]{:S(2)}, u32[]{:S(2)}) collective-permute-start(bf16[1,144,640]{2,1,0:T(8,128)(2,1)} %shard_map.164.refs_5_), channel_id=1, source_target_pairs={{0,3},{1,0},{2,1},{3,2},{4,7},{5,4},{6,5},{7,6},{8,11},{9,8},{10,9... | collective-permute-start | bytes 552968 | tf_op jit(solution)/shard_map/ppermute | solution.py:46
  42.6 7.7 %copy-start.22 = (bf16[1,144,640]{2,1,0:T(8,128)(2,1)}, bf16[1,144,640]{2,1,0:T(8,128)(2,1)S(1)}, u32[]{:S(2)}) copy-start(bf16[1,144,640]{2,1,0:T(8,128)(2,1)S(1)} %collective-permute-done.6.refs_6_) | copy-start | bytes 552964
  50.3 0.7 copy-start.24
  50.3 1.5 copy-start.20
  51.7 11.2 %copy-start.12 = (bf16[640,160]{0,1:T(8,128)(2,1)S(1)}, bf16[640,160]{0,1:T(8,128)(2,1)}, u32[]{:S(2)}) copy-start(bf16[640,160]{0,1:T(8,128)(2,1)} %param.26) | copy-start | bytes 614404
  59.4 1.4 collective-permute-start.14
  61.5 10.7 %collective-permute-start.15 = (f32[2,8,160]{2,1,0:T(8,128)S(1)}, f32[2,8,160]{2,1,0:T(8,128)S(1)}, u32[]{:S(2)}, u32[]{:S(2)}) collective-permute-start(f32[2,8,160]{2,1,0:T(8,128)S(1)} %pad_maximum_fusion.5), channel_id=1, source_target_pairs={{0,8},{4,12},{8,0},{12,4},{16,24},{20,28},{24,16},{28,20},{1,9},{5... | collective-permute-start | bytes 30728 | tf_op jit(solution)/shard_map/ppermute | solution.py:633
  63.9 35.9 %copy-start.2 = (bf16[1,80,640]{2,1,0:T(8,128)(2,1)}, bf16[1,80,640]{2,1,0:T(8,128)(2,1)S(1)}, u32[]{:S(2)}) copy-start(bf16[1,80,640]{2,1,0:T(8,128)(2,1)S(1)} %fusion.2.refs_0_) | copy-start | bytes 307204
  63.9 31.8 %collective-permute-start.32 = (bf16[1,80,640]{2,1,0:T(8,128)(2,1)S(1)}, bf16[1,80,640]{2,1,0:T(8,128)(2,1)S(1)}, u32[]{:S(2)}, u32[]{:S(2)}) collective-permute-start(bf16[1,80,640]{2,1,0:T(8,128)(2,1)S(1)} %fusion.2.refs_0_), channel_id=1, source_target_pairs={{0,1},{1,2},{2,3},{3,0},{4,5},{5,6},{6,7},{7,4},{8,9},{9,10},{10,1... | collective-permute-start | bytes 307208 | tf_op jit(solution)/shard_map/ppermute | solution.py:46
  68.4 10.5 %collective-permute-start.11 = (bf16[160,512]{1,0:T(8,128)(2,1)}, bf16[160,512]{1,0:T(8,128)(2,1)S(1)}, u32[]{:S(2)}, u32[]{:S(2)}) collective-permute-start(bf16[160,512]{1,0:T(8,128)(2,1)} %get-tuple-element.20.refs_0_.refs_1_), channel_id=1, source_target_pairs={{0,1},{1,2},{2,3},{3,0},{4,5},{5,6},{6,7},{7,4},{8,9},{9,10},{10,1... | collective-permute-start | bytes 491528 | tf_op jit(solution)/shard_map/ppermute | solution.py:46
  68.5 15.9 %collective-permute-start.12 = (bf16[160,512]{1,0:T(8,128)(2,1)}, bf16[160,512]{1,0:T(8,128)(2,1)S(1)}, u32[]{:S(2)}, u32[]{:S(2)}) collective-permute-start(bf16[160,512]{1,0:T(8,128)(2,1)} %get-tuple-element.20.refs_0_.refs_1_), channel_id=1, source_target_pairs={{0,2},{1,3},{2,0},{3,1},{4,6},{5,7},{6,4},{7,5},{8,10},{9,11},{10,... | collective-permute-start | bytes 491528 | tf_op jit(solution)/shard_map/ppermute | solution.py:46
  68.5 21.8 %collective-permute-start.13 = (bf16[160,512]{1,0:T(8,128)(2,1)}, bf16[160,512]{1,0:T(8,128)(2,1)S(1)}, u32[]{:S(2)}, u32[]{:S(2)}) collective-permute-start(bf16[160,512]{1,0:T(8,128)(2,1)} %get-tuple-element.20.refs_0_.refs_1_), channel_id=1, source_target_pairs={{0,3},{1,0},{2,1},{3,2},{4,7},{5,4},{6,5},{7,6},{8,11},{9,8},{10,9... | collective-permute-start | bytes 491528 | tf_op jit(solution)/shard_map/ppermute | solution.py:46
  72.9 3.9 %collective-permute-start.16 = (f32[4,8,160]{2,1,0:T(8,128)S(1)}, f32[4,8,160]{2,1,0:T(8,128)S(1)}, u32[]{:S(2)}, u32[]{:S(2)}) collective-permute-start(f32[4,8,160]{2,1,0:T(8,128)S(1)} %pad_maximum_fusion.3), channel_id=1, source_target_pairs={{0,16},{4,20},{8,24},{12,28},{16,0},{20,4},{24,8},{28,12},{1,17},{... | collective-permute-start | bytes 61448 | tf_op jit(solution)/shard_map/ppermute | solution.py:633
  76.8 21.0 %collective-permute-start.33 = (bf16[1,80,640]{2,1,0:T(8,128)(2,1)S(1)}, bf16[1,80,640]{2,1,0:T(8,128)(2,1)S(1)}, u32[]{:S(2)}, u32[]{:S(2)}) collective-permute-start(bf16[1,80,640]{2,1,0:T(8,128)(2,1)S(1)} %fusion.2.refs_0_), channel_id=1, source_target_pairs={{0,2},{1,3},{2,0},{3,1},{4,6},{5,7},{6,4},{7,5},{8,10},{9,11},{10,... | collective-permute-start | bytes 307208 | tf_op jit(solution)/shard_map/ppermute | solution.py:46
  78.9 14.6 %copy-start.13 = (bf16[160,512]{1,0:T(8,128)(2,1)}, bf16[160,512]{1,0:T(8,128)(2,1)S(1)}, u32[]{:S(2)}) copy-start(bf16[160,512]{1,0:T(8,128)(2,1)S(1)} %collective-permute-done.11.refs_1_.refs_2_) | copy-start | bytes 491524
  78.9 19.1 %collective-permute-start.34 = (bf16[1,80,640]{2,1,0:T(8,128)(2,1)S(1)}, bf16[1,80,640]{2,1,0:T(8,128)(2,1)}, u32[]{:S(2)}, u32[]{:S(2)}) collective-permute-start(bf16[1,80,640]{2,1,0:T(8,128)(2,1)S(1)} %fusion.2.refs_0_), channel_id=1, source_target_pairs={{0,3},{1,0},{2,1},{3,2},{4,7},{5,4},{6,5},{7,6},{8,11},{9,8},{10,9... | collective-permute-start | bytes 307208 | tf_op jit(solution)/shard_map/ppermute | solution.py:46
  84.4 9.1 %copy-start.14 = (bf16[160,512]{1,0:T(8,128)(2,1)}, bf16[160,512]{1,0:T(8,128)(2,1)S(1)}, u32[]{:S(2)}) copy-start(bf16[160,512]{1,0:T(8,128)(2,1)S(1)} %collective-permute-done.12.refs_2_.refs_3_) | copy-start | bytes 491524
  84.4 17.3 %collective-permute-start.17 = (bf16[160,640]{1,0:T(8,128)(2,1)}, bf16[160,640]{1,0:T(8,128)(2,1)}, u32[]{:S(2)}, u32[]{:S(2)}) collective-permute-start(bf16[160,640]{1,0:T(8,128)(2,1)} %shard_map.168.refs_5_), channel_id=1, source_target_pairs={{0,1},{1,2},{2,3},{3,0},{4,5},{5,6},{6,7},{7,4},{8,9},{9,10},{10,1... | collective-permute-start | bytes 614408 | tf_op jit(solution)/shard_map/ppermute | solution.py:46
  90.2 3.3 %copy-start.15 = (bf16[160,512]{1,0:T(8,128)(2,1)}, bf16[160,512]{1,0:T(8,128)(2,1)S(1)}, u32[]{:S(2)}) copy-start(bf16[160,512]{1,0:T(8,128)(2,1)S(1)} %collective-permute-done.13.refs_3_.refs_4_) | copy-start | bytes 491524
  90.2 15.7 %collective-permute-start.18 = (bf16[160,640]{1,0:T(8,128)(2,1)}, bf16[160,640]{1,0:T(8,128)(2,1)}, u32[]{:S(2)}, u32[]{:S(2)}) collective-permute-start(bf16[160,640]{1,0:T(8,128)(2,1)} %shard_map.168.refs_5_), channel_id=1, source_target_pairs={{0,2},{1,3},{2,0},{3,1},{4,6},{5,7},{6,4},{7,5},{8,10},{9,11},{10,... | collective-permute-start | bytes 614408 | tf_op jit(solution)/shard_map/ppermute | solution.py:46
  95.8 4.0 %copy-start.16 = (bf16[1,80,640]{2,1,0:T(8,128)(2,1)}, bf16[1,80,640]{2,1,0:T(8,128)(2,1)S(1)}, u32[]{:S(2)}) copy-start(bf16[1,80,640]{2,1,0:T(8,128)(2,1)S(1)} %collective-permute-done.32.refs_1_) | copy-start | bytes 307204
  95.8 14.1 %collective-permute-start.20 = (bf16[640,256]{1,0:T(8,128)(2,1)}, bf16[640,256]{1,0:T(8,128)(2,1)}, u32[]{:S(2)}, u32[]{:S(2)}) collective-permute-start(bf16[640,256]{1,0:T(8,128)(2,1)} %get-tuple-element.23), channel_id=1, source_target_pairs={{0,4},{4,8},{8,12},{12,16},{16,20},{20,24},{24,28},{1,5},{5,9},{9,... | collective-permute-start | bytes 983048 | tf_op jit(solution)/shard_map/ppermute | solution.py:742
  97.8 2.0 %copy-start.17 = (bf16[1,80,640]{2,1,0:T(8,128)(2,1)}, bf16[1,80,640]{2,1,0:T(8,128)(2,1)S(1)}, u32[]{:S(2)}) copy-start(bf16[1,80,640]{2,1,0:T(8,128)(2,1)S(1)} %collective-permute-done.33.refs_2_) | copy-start | bytes 307204
  97.8 12.1 %collective-permute-start.19 = (bf16[160,640]{1,0:T(8,128)(2,1)}, bf16[160,640]{1,0:T(8,128)(2,1)}, u32[]{:S(2)}, u32[]{:S(2)}) collective-permute-start(bf16[160,640]{1,0:T(8,128)(2,1)} %shard_map.168.refs_5_), channel_id=1, source_target_pairs={{0,3},{1,0},{2,1},{3,2},{4,7},{5,4},{6,5},{7,6},{8,11},{9,8},{10,9... | collective-permute-start | bytes 614408 | tf_op jit(solution)/shard_map/ppermute | solution.py:46
  98.0 11.9 %collective-permute-start.21 = (bf16[640,256]{1,0:T(8,128)(2,1)}, bf16[640,256]{1,0:T(8,128)(2,1)}, u32[]{:S(2)}, u32[]{:S(2)}) collective-permute-start(bf16[640,256]{1,0:T(8,128)(2,1)} %get-tuple-element.24), channel_id=1, source_target_pairs={{4,0},{8,4},{12,8},{16,12},{20,16},{24,20},{28,24},{5,1},{9,5},{13... | collective-permute-start | bytes 983048 | tf_op jit(solution)/shard_map/ppermute | solution.py:742
  101.7 19.7 %collective-permute-start.35 = (bf16[4,80,640]{2,1,0:T(8,128)(2,1)}, bf16[4,80,640]{2,1,0:T(8,128)(2,1)S(1)}, u32[]{:S(2)}, u32[]{:S(2)}) collective-permute-start(bf16[4,80,640]{2,1,0:T(8,128)(2,1)} %shard_map.172.refs_9_), channel_id=1, source_target_pairs={{0,8},{4,12},{8,16},{12,20},{16,24},{20,28},{24,0},{28,4},{1,9},{5... | collective-permute-start | bytes 1228808 | tf_op jit(solution)/shard_map/ppermute | solution.py:46
  105.9 18.0 %collective-permute-start.36 = (bf16[4,80,640]{2,1,0:T(8,128)(2,1)}, bf16[4,80,640]{2,1,0:T(8,128)(2,1)S(1)}, u32[]{:S(2)}, u32[]{:S(2)}) collective-permute-start(bf16[4,80,640]{2,1,0:T(8,128)(2,1)} %shard_map.172.refs_9_), channel_id=1, source_target_pairs={{0,16},{4,20},{8,24},{12,28},{16,0},{20,4},{24,8},{28,12},{1,17},{... | collective-permute-start | bytes 1228808 | tf_op jit(solution)/shard_map/ppermute | solution.py:46
  109.9 27.5 %collective-permute-start.37 = (bf16[4,80,640]{2,1,0:T(8,128)(2,1)}, bf16[4,80,640]{2,1,0:T(8,128)(2,1)}, u32[]{:S(2)}, u32[]{:S(2)}) collective-permute-start(bf16[4,80,640]{2,1,0:T(8,128)(2,1)} %shard_map.172.refs_9_), channel_id=1, source_target_pairs={{0,24},{4,28},{8,0},{12,4},{16,8},{20,12},{24,16},{28,20},{1,25},{... | collective-permute-start | bytes 1228808 | tf_op jit(solution)/shard_map/ppermute | solution.py:46
  109.9 28.9 %collective-permute-start.38 = (bf16[4,80,640]{2,1,0:T(8,128)(2,1)}, bf16[4,80,640]{2,1,0:T(8,128)(2,1)}, u32[]{:S(2)}, u32[]{:S(2)}) collective-permute-start(bf16[4,80,640]{2,1,0:T(8,128)(2,1)} %shard_map.172.refs_9_), channel_id=1, source_target_pairs={{0,4},{4,0},{8,12},{12,8},{16,20},{20,16},{24,28},{28,24},{1,5},{5... | collective-permute-start | bytes 1228808 | tf_op jit(solution)/shard_map/ppermute | solution.py:640
  117.5 7.2 %collective-permute-start.22 = (bf16[1,160,256]{2,1,0:T(8,128)(2,1)}, bf16[1,160,256]{2,1,0:T(8,128)(2,1)}, u32[]{:S(2)}, u32[]{:S(2)}) collective-permute-start(bf16[1,160,256]{2,1,0:T(8,128)(2,1)} %get-tuple-element.28), channel_id=1, source_target_pairs={{0,3},{1,0},{2,1},{3,2},{4,7},{5,4},{6,5},{7,6},{8,11},{9,8},{10,9... | collective-permute-start | bytes 245768 | tf_op jit(solution)/shard_map/ppermute | solution.py:46
  121.4 35.6 %copy-start.3 = (bf16[4,80,640]{2,1,0:T(8,128)(2,1)}, bf16[4,80,640]{2,1,0:T(8,128)(2,1)S(1)}, u32[]{:S(2)}) copy-start(bf16[4,80,640]{2,1,0:T(8,128)(2,1)S(1)} %collective-permute-done.35.refs_10_) | copy-start | bytes 1228804
  121.4 6.9 %collective-permute-start.23 = (bf16[1,160,256]{2,1,0:T(8,128)(2,1)}, bf16[1,160,256]{2,1,0:T(8,128)(2,1)}, u32[]{:S(2)}, u32[]{:S(2)}) collective-permute-start(bf16[1,160,256]{2,1,0:T(8,128)(2,1)} %get-tuple-element.29), channel_id=1, source_target_pairs={{0,2},{1,3},{2,0},{3,1},{4,6},{5,7},{6,4},{7,5},{8,10},{9,11},{10,... | collective-permute-start | bytes 245768 | tf_op jit(solution)/shard_map/ppermute | solution.py:46
  123.9 33.2 %copy-start.4 = (bf16[4,80,640]{2,1,0:T(8,128)(2,1)}, bf16[4,80,640]{2,1,0:T(8,128)(2,1)S(1)}, u32[]{:S(2)}) copy-start(bf16[4,80,640]{2,1,0:T(8,128)(2,1)S(1)} %collective-permute-done.36.refs_11_) | copy-start | bytes 1228804
  123.9 15.9 %collective-permute-start.39 = (bf16[4,80,640]{2,1,0:T(8,128)(2,1)S(1)}, bf16[4,80,640]{2,1,0:T(8,128)(2,1)}, u32[]{:S(2)}, u32[]{:S(2)}) collective-permute-start(bf16[4,80,640]{2,1,0:T(8,128)(2,1)S(1)} %collective-permute-done.35.refs_10_), channel_id=1, source_target_pairs={{0,4},{4,0},{8,12},{12,8},{16,20},{20,16},{24,28},{28,24},{1,5},{5... | collective-permute-start | bytes 1228808 | tf_op jit(solution)/shard_map/ppermute | solution.py:640
  124.6 15.2 %collective-permute-start.40 = (bf16[4,80,640]{2,1,0:T(8,128)(2,1)S(1)}, bf16[4,80,640]{2,1,0:T(8,128)(2,1)}, u32[]{:S(2)}, u32[]{:S(2)}) collective-permute-start(bf16[4,80,640]{2,1,0:T(8,128)(2,1)S(1)} %collective-permute-done.36.refs_11_), channel_id=1, source_target_pairs={{0,4},{4,0},{8,12},{12,8},{16,20},{20,16},{24,28},{28,24},{1,5},{5... | collective-permute-start | bytes 1228808 | tf_op jit(solution)/shard_map/ppermute | solution.py:640
  128.4 6.6 %collective-permute-start.24 = (bf16[1,160,256]{2,1,0:T(8,128)(2,1)}, bf16[1,160,256]{2,1,0:T(8,128)(2,1)}, u32[]{:S(2)}, u32[]{:S(2)}) collective-permute-start(bf16[1,160,256]{2,1,0:T(8,128)(2,1)} %get-tuple-element.30), channel_id=1, source_target_pairs={{0,1},{1,2},{2,3},{3,0},{4,5},{5,6},{6,7},{7,4},{8,9},{9,10},{10,1... | collective-permute-start | bytes 245768 | tf_op jit(solution)/shard_map/ppermute | solution.py:46
  136.7 11.7 %collective-permute-start.25 = (bf16[1,640,256]{2,1,0:T(8,128)(2,1)}, bf16[1,640,256]{2,1,0:T(8,128)(2,1)S(1)}, u32[]{:S(2)}, u32[]{:S(2)}) collective-permute-start(bf16[1,640,256]{2,1,0:T(8,128)(2,1)} %shard_map.171.refs_1_), channel_id=1, source_target_pairs={{0,8},{4,12},{8,16},{12,20},{16,24},{20,28},{24,0},{28,4},{1,9},{5... | collective-permute-start | bytes 983048 | tf_op jit(solution)/shard_map/ppermute | solution.py:46
  137.4 16.0 %collective-permute-start.26 = (bf16[1,640,256]{2,1,0:T(8,128)(2,1)}, bf16[1,640,256]{2,1,0:T(8,128)(2,1)S(1)}, u32[]{:S(2)}, u32[]{:S(2)}) collective-permute-start(bf16[1,640,256]{2,1,0:T(8,128)(2,1)} %shard_map.171.refs_1_), channel_id=1, source_target_pairs={{0,16},{4,20},{8,24},{12,28},{16,0},{20,4},{24,8},{28,12},{1,17},{... | collective-permute-start | bytes 983048 | tf_op jit(solution)/shard_map/ppermute | solution.py:46
  138.9 14.5 %collective-permute-start.27 = (bf16[1,640,256]{2,1,0:T(8,128)(2,1)}, bf16[1,640,256]{2,1,0:T(8,128)(2,1)S(1)}, u32[]{:S(2)}, u32[]{:S(2)}) collective-permute-start(bf16[1,640,256]{2,1,0:T(8,128)(2,1)} %shard_map.171.refs_1_), channel_id=1, source_target_pairs={{0,24},{4,28},{8,0},{12,4},{16,8},{20,12},{24,16},{28,20},{1,25},{... | collective-permute-start | bytes 983048 | tf_op jit(solution)/shard_map/ppermute | solution.py:46
  139.8 14.7 %collective-permute-start.41 = (bf16[4,80,640]{2,1,0:T(8,128)(2,1)}, bf16[4,80,640]{2,1,0:T(8,128)(2,1)}, u32[]{:S(2)}, u32[]{:S(2)}) collective-permute-start(bf16[4,80,640]{2,1,0:T(8,128)(2,1)} %collective-permute-done.37.refs_12_), channel_id=1, source_target_pairs={{0,4},{4,0},{8,12},{12,8},{16,20},{20,16},{24,28},{28,24},{1,5},{5... | collective-permute-start | bytes 1228808 | tf_op jit(solution)/shard_map/ppermute | solution.py:640
  139.8 14.7 %collective-permute-start.28 = (bf16[1,640,256]{2,1,0:T(8,128)(2,1)}, bf16[1,640,256]{2,1,0:T(8,128)(2,1)S(1)}, u32[]{:S(2)}, u32[]{:S(2)}) collective-permute-start(bf16[1,640,256]{2,1,0:T(8,128)(2,1)} %shard_map.171.refs_1_), channel_id=1, source_target_pairs={{0,4},{4,0},{8,12},{12,8},{16,20},{20,16},{24,28},{28,24},{1,5},{5... | collective-permute-start | bytes 983048 | tf_op jit(solution)/shard_map/ppermute | solution.py:640
  148.4 0.7 copy-start.5
  149.1 5.4 %collective-permute-start.29 = (bf16[1,640,256]{2,1,0:T(8,128)(2,1)S(1)}, bf16[1,640,256]{2,1,0:T(8,128)(2,1)S(1)}, u32[]{:S(2)}, u32[]{:S(2)}) collective-permute-start(bf16[1,640,256]{2,1,0:T(8,128)(2,1)S(1)} %collective-permute-done.25.refs_2_), channel_id=1, source_target_pairs={{0,4},{4,0},{8,12},{12,8},{16,20},{20,16},{24,28},{28,24},{1,5},{5... | collective-permute-start | bytes 983048 | tf_op jit(solution)/shard_map/ppermute | solution.py:640
  153.3 1.2 copy-start.6
  153.3 1.6 collective-permute-start.30
  153.4 1.6 copy-start.7
  153.4 2.1 %collective-permute-start.31 = (bf16[1,640,256]{2,1,0:T(8,128)(2,1)S(1)}, bf16[1,640,256]{2,1,0:T(8,128)(2,1)S(1)}, u32[]{:S(2)}, u32[]{:S(2)}) collective-permute-start(bf16[1,640,256]{2,1,0:T(8,128)(2,1)S(1)} %collective-permute-done.27.refs_4_), channel_id=1, source_target_pairs={{0,4},{4,0},{8,12},{12,8},{16,20},{20,16},{24,28},{28,24},{1,5},{5... | collective-permute-start | bytes 983048 | tf_op jit(solution)/shard_map/ppermute | solution.py:640
  154.5 0.9 copy-start.8
  154.6 0.9 copy-start.9
  155.4 0.7 copy-start.11
  (3 other events, 2.1 us)

commit v2 on v1

--- a/solution.py
+++ b/solution.py
@@ -51,37 +51,59 @@
     return half + half * jnp.tanh(half)
 
 
-def time_bias(step_index, roster, time_weight, temb_columns, rows):
+def own_channels(where, rows, kept, channels):
+    row = lax.broadcasted_iota(jnp.int32, (rows, channels), 0)
+    column = lax.broadcasted_iota(jnp.int32, (rows, channels), 1)
+    chosen = (row + where * kept == column) & (row < kept)
+    return jnp.where(chosen, 1.0, 0.0).astype(jnp.bfloat16)
+
+
+def part_rows(row):
+    at = lax.broadcasted_iota(jnp.int32, (8, row.shape[1]), 0)
+    high, middle, low = three_parts(row)
+    parts = jnp.where(at == 0, high, jnp.where(at == 1, middle, jnp.where(at == 2, low, 0.0)))
+    return parts.astype(jnp.bfloat16)
+
+
+def time_bias(ends, step_index, roster, time_weight, temb_weight, rows, kept):
     freqs, hidden = time_weight.shape
-    kept = temb_columns.shape[1]
+    channels = temb_weight.shape[1]
     half_len = freqs // 2
     steps = roster.shape[0]
 
-    def body(i_ref, r_ref, w_ref, t_ref, o_ref):
+    def column(row):
+        tiles = [
+            jnp.broadcast_to(row[:, start : start + LANES], (LANES, LANES)).T
+            for start in range(0, row.shape[1], LANES)
+        ]
+        return jnp.concatenate(tiles, axis=0)[:, :1]
+
+    def body(n_ref, i_ref, r_ref, w_ref, t_ref, o_ref):
         at = lax.broadcasted_iota(jnp.int32, (1, steps), 1)
         moment = jnp.sum(jnp.where(at == i_ref[0], r_ref[...], 0.0), axis=1, keepdims=True)
-        row = lax.broadcasted_iota(jnp.int32, (half_len, 1), 0).astype(jnp.float32)
-        angles = moment * jnp.exp(-math.log(10000.0) * row / half_len)
-        time_hidden = jnp.sum(jnp.cos(angles) * w_ref[:half_len], axis=0, keepdims=True) + jnp.sum(
-            jnp.sin(angles) * w_ref[half_len:], axis=0, keepdims=True
+        padded = -(-half_len // LANES) * LANES
+        place = lax.broadcasted_iota(jnp.int32, (1, padded), 1).astype(jnp.float32)
+        angles = moment * jnp.exp(-math.log(10000.0) * place / half_len)
+        time_hidden = jnp.zeros((1, hidden), jnp.float32)
+        for start, wave in ((0, jnp.cos(angles)), (half_len, jnp.sin(angles))):
+            time_hidden = time_hidden + jnp.sum(
+                column(wave)[:half_len] * w_ref[start : start + half_len], axis=0, keepdims=True
+            )
+        time_hidden = time_hidden / (1.0 + jnp.exp(-time_hidden))
+        summed = jnp.zeros((LANES, channels), jnp.float32)
+        turned = column(time_hidden)
+        for start in range(0, hidden, LANES):
+            summed = summed + turned[start : start + LANES] * t_ref[start : start + LANES]
+        parts = lax.dot_general(
+            own_channels(n_ref[2], rows, kept, channels),
+            part_rows(jnp.sum(summed, axis=0, keepdims=True)),
+            NT,
+            preferred_element_type=jnp.float32,
         )
-        time_hidden = time_hidden / (1.0 + jnp.exp(-time_hidden))
-        parts = []
-        for start in range(0, hidden, LANES):
-            piece = jnp.broadcast_to(time_hidden[:, start : start + LANES], (LANES, LANES))
-            parts.append(piece.T[:, :1] * t_ref[start : start + LANES])
-        summed = jnp.sum(sum(parts[1:], parts[0]), axis=0, keepdims=True)
-        o_ref[...] = jnp.zeros((rows, LANES), jnp.float32)
-        for start in range(0, kept, LANES):
-            size = min(LANES, kept - start)
-            cut = summed[:, start : start + size]
-            if size < LANES:
-                cut = jnp.concatenate([cut, jnp.zeros((1, LANES - size), jnp.float32)], axis=1)
-            turned = jnp.broadcast_to(cut, (LANES, LANES)).T
-            o_ref[start : start + size] = turned[:size]
-
-    return call(body, jax.ShapeDtypeStruct((rows, LANES), jnp.float32), scalars=1)(
-        step_index, roster[None, :], time_weight, temb_columns
+        o_ref[...] = jnp.broadcast_to(jnp.sum(parts, axis=1, keepdims=True), (rows, LANES))
+
+    return call(body, jax.ShapeDtypeStruct((rows, LANES), jnp.float32), scalars=2)(
+        ends, step_index, roster[None, :], time_weight, temb_weight
     )
 
 
@@ -110,21 +132,20 @@
 
 def group_sums(row, member):
     for dims in ((((1,), (0,)), ((), ())), NT):
-        at = lax.broadcasted_iota(jnp.int32, (8, row.shape[1]), 0)
-        high, middle, low = three_parts(row)
-        parts = jnp.where(at == 0, high, jnp.where(at == 1, middle, jnp.where(at == 2, low, 0.0)))
         summed = lax.dot_general(
-            parts.astype(jnp.bfloat16), member, dims, preferred_element_type=jnp.float32
+            part_rows(row), member, dims, preferred_element_type=jnp.float32
         )
         row = jnp.sum(summed, axis=0, keepdims=True)
     return row
 
 
-def local_stats(features, member, width):
+def local_stats(features, member, width, columns):
     samples, length, channels = features.shape
 
-    def body(x_ref, g_ref, o_ref):
+    def body(x_ref, g_ref, o_ref, e_ref):
         for i in range(samples):
+            e_ref[i, :columns] = x_ref[i, :columns]
+            e_ref[i, columns:] = x_ref[i, length - columns :]
             v = x_ref[i].astype(jnp.float32)
             mean = group_sums(jnp.sum(v, axis=0, keepdims=True), g_ref[...]) / (length * width)
             c = v - mean
@@ -133,7 +154,30 @@
                 jnp.sum(c * c, axis=0, keepdims=True), g_ref[...]
             )
 
-    return call(body, jax.ShapeDtypeStruct((2 * samples, channels), jnp.float32))(features, member)
+    shapes = (
+        jax.ShapeDtypeStruct((2 * samples, channels), jnp.float32),
+        jax.ShapeDtypeStruct((samples, 2 * columns, channels), jnp.bfloat16),
+    )
+    return call(body, shapes)(features, member)
+
+
+def place_weights(where, pieces, wide, channels):
+    blocks, part, depth = pieces[0].shape
+    steps = wide // part
+
+    def body(w_ref, *refs):
+        for k, piece in enumerate(refs[:-1]):
+            at = w_ref[k]
+            for g in range(blocks):
+                start = jnp.where(
+                    at < steps,
+                    g * wide + at * part,
+                    blocks * wide + g * (channels // blocks) + (at - steps) * part,
+                )
+                refs[-1][pl.ds(pl.multiple_of(start, 16), part)] = piece[g]
+
+    shape = jax.ShapeDtypeStruct((4 * channels, depth), jnp.bfloat16)
+    return call(body, shape, scalars=1)(where, *pieces)
 
 
 def place(where, pieces, axis, flops=0):
@@ -152,53 +196,45 @@
     )
 
 
-def merge_stats(p_ref, gain, entries):
-    devices, rows, _ = p_ref.shape
-    count = rows // 2
-    mean = p_ref[0, :count]
-    for d in range(1, devices):
-        mean = mean + p_ref[d, :count]
-    mean = mean / devices
-    squares = jnp.zeros_like(mean)
-    for d in range(devices):
-        away = p_ref[d, :count] - mean
-        squares = squares + p_ref[d, count:] + entries * (away * away)
-    return mean, lax.rsqrt(squares / (entries * devices) + EPSILON) * gain
+def norm_terms(figures, gain, entries):
+    count = figures.shape[0] // 2
+    return figures[:count], lax.rsqrt(figures[count:] / entries + EPSILON) * gain
 
 
 TAIL = 16
 
 
-def rows_message(parts, gain, entries, mids):
-    samples, mid, channels = mids.shape
+def rows_message(figures, gain, entries, flat, width):
+    samples, length, channels = flat.shape
+    mid = length - 2 * width
 
     def body(p_ref, g_ref, m_ref, o_ref):
-        mean, scale = merge_stats(p_ref, g_ref[...], entries)
+        mean, scale = norm_terms(p_ref[...], g_ref[...], entries)
         for i in range(samples):
-            o_ref[i, :mid] = m_ref[i]
+            o_ref[i, :mid] = m_ref[i, width : width + mid]
             rows = [*three_parts(mean[i : i + 1]), *three_parts(scale[i : i + 1])]
             rows.append(jnp.zeros((TAIL - len(rows), channels), jnp.float32))
             o_ref[i, mid:] = jnp.concatenate(rows, axis=0).astype(jnp.bfloat16)
 
     shape = jax.ShapeDtypeStruct((samples, mid + TAIL, channels), jnp.bfloat16)
-    return call(body, shape)(parts, gain, mids)
-
-
-def columns_message(parts, gain, entries, mids):
+    return call(body, shape)(figures, gain, flat)
+
+
+def columns_message(figures, gain, entries, mids):
     shard, wide = mids.shape
 
     def body(p_ref, g_ref, m_ref, o_ref):
         o_ref[:, :wide] = m_ref[...]
-        figures = jnp.concatenate(merge_stats(p_ref, g_ref[...], entries), axis=0)
-        rows = [*three_parts(figures)]
-        rows.append(jnp.zeros((LANES - 3 * figures.shape[0], shard), jnp.float32))
+        terms = jnp.concatenate(norm_terms(p_ref[...], g_ref[...], entries), axis=0)
+        rows = [*three_parts(terms)]
+        rows.append(jnp.zeros((LANES - 3 * terms.shape[0], shard), jnp.float32))
         rows = jnp.concatenate(rows, axis=0).astype(jnp.bfloat16)
         o_ref[:, wide:] = lax.dot_general(
             identity(shard, shard), rows, NT, preferred_element_type=jnp.float32
         ).astype(jnp.bfloat16)
 
     shape = jax.ShapeDtypeStruct((shard, wide + LANES), jnp.bfloat16)
-    return call(body, shape)(parts, gain, mids)
+    return call(body, shape)(figures, gain, mids)
 
 
 def identity(rows, columns):
@@ -273,7 +309,7 @@
     return jnp.concatenate(tiles, axis=1)
 
 
-def first_conv(ends, edges, mids, above, below, weight, bias, groups, pick, eye, width, group):
+def first_conv(ends, edges, mids, above, below, weight, bias, groups, gain, eye, kept, width, group):
     n = len(edges)
     samples, edge, channels = edges[0].shape
     mid = mids[0].shape[1] - TAIL
@@ -286,7 +322,10 @@
         ends_ref = refs[0]
         e_refs, m_refs = refs[1 : 1 + n], refs[1 + n : 1 + 2 * n]
         a_ref, b_ref, w_ref, t_ref, g_ref, p_ref, i_ref = refs[1 + 2 * n : 8 + 2 * n]
-        eo_ref, mo_ref, so_ref, fe_ref, fm_ref, buf, out_buf = refs[8 + 2 * n :]
+        eo_ref, mo_ref, so_ref, fe_ref, fm_ref, go_ref, buf, out_buf = refs[8 + 2 * n :]
+        pick = own_channels(ends_ref[2], shard, kept, channels)
+        parts = lax.dot_general(part_rows(p_ref[...]), pick, NT, preferred_element_type=jnp.float32)
+        go_ref[...] = jnp.sum(parts, axis=0, keepdims=True)
         has_above = ends_ref[0].astype(jnp.float32)
         has_below = ends_ref[1].astype(jnp.float32)
         lane = lax.broadcasted_iota(jnp.int32, (shard, LANES), 1)
@@ -304,18 +343,18 @@
                 e = e_refs[j][i]
                 m = m_refs[j][i, :mid]
                 ea = act(e).astype(jnp.bfloat16)
-                buf[:width] = (act(a_ref[q]) * has_above).astype(jnp.bfloat16)
-                buf[width : 2 * width] = ea[:width]
-                buf[2 * width : 2 * width + mid] = act(m).astype(jnp.bfloat16)
-                buf[2 * width + mid : 3 * width + mid] = ea[width:]
-                buf[3 * width + mid :] = (act(b_ref[q]) * has_below).astype(jnp.bfloat16)
+                buf[q % 2, :width] = (act(a_ref[q]) * has_above).astype(jnp.bfloat16)
+                buf[q % 2, width : 2 * width] = ea[:width]
+                buf[q % 2, 2 * width : 2 * width + mid] = act(m).astype(jnp.bfloat16)
+                buf[q % 2, 2 * width + mid : 3 * width + mid] = ea[width:]
+                buf[q % 2, 3 * width + mid :] = (act(b_ref[q]) * has_below).astype(jnp.bfloat16)
                 y = jnp.zeros((3 * shard, length), jnp.float32)
                 for a in range(3):
                     window = jnp.concatenate(
                         [
-                            buf[a * width : (a + 1) * width],
-                            buf[(a + 1 + inner) * width : (a + 2 + inner) * width],
-                            buf[(a + 1) * width : (a + 1 + inner) * width],
+                            buf[q % 2, a * width : (a + 1) * width],
+                            buf[q % 2, (a + 1 + inner) * width : (a + 2 + inner) * width],
+                            buf[q % 2, (a + 1) * width : (a + 1 + inner) * width],
                         ],
                         axis=0,
                     )
@@ -326,10 +365,10 @@
                 eo_ref[:, q * edge : (q + 1) * edge] = out[:, :edge].astype(jnp.bfloat16)
                 mo_ref[:, q * mid : (q + 1) * mid] = out[:, edge:].astype(jnp.bfloat16)
                 fe_ref[:, q * edge : (q + 1) * edge] = lax.dot_general(
-                    p_ref[...], e, NT, preferred_element_type=jnp.float32
+                    pick, e, NT, preferred_element_type=jnp.float32
                 ).astype(jnp.bfloat16)
                 fm_ref[:, q * mid : (q + 1) * mid] = lax.dot_general(
-                    p_ref[...], m, NT, preferred_element_type=jnp.float32
+                    pick, m, NT, preferred_element_type=jnp.float32
                 ).astype(jnp.bfloat16)
                 out_buf[q] = out
                 sums = jnp.where(lane == q, jnp.sum(out, axis=1, keepdims=True), sums)
@@ -350,13 +389,14 @@
         jax.ShapeDtypeStruct((2 * count, shard), jnp.float32),
         jax.ShapeDtypeStruct((shard, count * edge), jnp.bfloat16),
         jax.ShapeDtypeStruct((shard, count * mid), jnp.bfloat16),
+        jax.ShapeDtypeStruct((1, shard), jnp.float32),
     )
     scratch = [
-        pltpu.VMEM((length + 2 * width, channels), jnp.bfloat16),
+        pltpu.VMEM((2, length + 2 * width, channels), jnp.bfloat16),
         pltpu.VMEM((count, shard, length), jnp.float32),
     ]
     return call(body, out_shape, scratch, scalars=1, flops=6 * count * length * channels * 3 * shard)(
-        ends, *edges, *mids, above, below, weight, bias, groups, pick, eye
+        ends, *edges, *mids, above, below, weight, bias, groups, gain, eye
     )
 
 
@@ -468,33 +508,17 @@
     return jnp.sum(summed, axis=1, keepdims=True)
 
 
-def attention(where, chunks, weights, gain, spread, unpad, wide, width, group):
-    pieces, parts = len(chunks), len(weights)
+def attention(chunks, weights, gain, spread, unpad, width, group):
+    pieces = len(chunks)
     samples, rows, length = chunks[0].shape
     channels = rows if unpad is None else unpad.shape[1]
     heads = channels // HEAD_DIM
     keys = pieces * length
     inner = length // width - 2
-    packed = parts > 1
 
     def body(*refs):
-        where_ref, c_refs = refs[0], refs[1 : 1 + pieces]
-        w_refs = refs[1 + pieces : 1 + pieces + parts]
-        g_ref, a_ref, b_ref = refs[1 + pieces + parts : 4 + pieces + parts]
-        o_ref, buf, query_buf, mixed_buf = refs[-4 - packed : len(refs) - packed]
-        weight = refs[-1] if packed else w_refs[0]
-        if packed:
-            blocks, part, _ = weights[0].shape
-            steps = wide // part
-            for k, w in enumerate(w_refs):
-                at = where_ref[k]
-                for g in range(blocks):
-                    start = jnp.where(
-                        at < steps,
-                        g * wide + at * part,
-                        blocks * wide + g * (channels // blocks) + (at - steps) * part,
-                    )
-                    weight[pl.ds(pl.multiple_of(start, 16), part)] = w[g]
+        c_refs, weight, g_ref, a_ref, b_ref = refs[:pieces], *refs[pieces : pieces + 4]
+        o_ref, buf, query_buf, mixed_buf = refs[-4:]
         for i in range(samples):
             total = jnp.zeros((rows, LANES), jnp.float32)
             for c in c_refs:
@@ -524,32 +548,32 @@
                     preferred_element_type=jnp.float32,
                 ).astype(jnp.bfloat16)
 
-            @pl.loop(0, heads // 2)
-            def _(two):
-                lanes = pl.ds(pl.multiple_of(two * LANES, LANES), LANES)
-                k_two = buf[pl.ds(pl.multiple_of(two * LANES, LANES), LANES)]
-                v_two = buf[pl.ds(pl.multiple_of(channels + two * LANES, LANES), LANES)]
+            for two in range(heads // 2):
+                lanes = slice(two * LANES, (two + 1) * LANES)
+                k_two = buf[lanes]
+                v_two = buf[channels + two * LANES : channels + (two + 1) * LANES]
                 q_two = query_buf[:, lanes]
+                ones = jnp.ones((16, keys), jnp.bfloat16)
                 pair = []
                 for h in range(2):
                     cut = slice(h * HEAD_DIM, (h + 1) * HEAD_DIM)
                     scores = jnp.dot(q_two[:, cut], k_two[cut], preferred_element_type=jnp.float32)
-                    shifted = jnp.exp(scores - jnp.max(scores, axis=1, keepdims=True))
-                    totals = jnp.sum(shifted, axis=1, keepdims=True)
+                    below = scores - jnp.max(scores, axis=1, keepdims=True)
+                    shifted = jnp.exp(below.astype(jnp.bfloat16))
                     mixed = lax.dot_general(
-                        shifted.astype(jnp.bfloat16),
-                        v_two[cut],
+                        shifted,
+                        jnp.concatenate([v_two[cut], ones], axis=0),
                         NT,
                         preferred_element_type=jnp.float32,
                     )
-                    pair.append(mixed / totals)
+                    pair.append(mixed[:, :HEAD_DIM] / mixed[:, HEAD_DIM : HEAD_DIM + 1])
                 mixed_buf[:, lanes] = jnp.concatenate(pair, axis=1).astype(jnp.bfloat16)
 
             own = c_refs[0][i].astype(jnp.float32).T
             if unpad is not None:
                 own = jnp.dot(
                     own.astype(jnp.bfloat16),
-                    refs[4 + pieces + parts][...],
+                    refs[pieces + 4][...],
                     preferred_element_type=jnp.float32,
                 )
             result = own + lax.dot_general(
@@ -564,22 +588,29 @@
             for r in range(inner):
                 o_ref[i, 1 + r] = result[(2 + r) * width : (3 + r) * width]
 
-    operands = [*chunks, *weights, gain, spread.T, spread]
+    operands = [*chunks, weights, gain, spread.T, spread]
     if unpad is not None:
         operands.append(unpad)
-    scratch = [
-        pltpu.VMEM((2 * channels, keys), jnp.bfloat16),
-        pltpu.VMEM((length, channels), jnp.bfloat16),
-        pltpu.VMEM((length, channels), jnp.bfloat16),
-    ]
-    if packed:
-        scratch.append(pltpu.VMEM((4 * channels, rows), jnp.bfloat16))
     return call(
         body,
         jax.ShapeDtypeStruct((samples, length // width, width, channels), jnp.bfloat16),
-        scratch,
-        scalars=1,
-    )(where, *operands)
+        [
+            pltpu.VMEM((2 * channels, keys), jnp.bfloat16),
+            pltpu.VMEM((length, channels), jnp.bfloat16),
+            pltpu.VMEM((length, channels), jnp.bfloat16),
+        ],
+    )(*operands)
+
+
+def gain_column(gain):
+    channels = gain.shape[1]
+
+    def body(g_ref, o_ref):
+        for start in range(0, channels, LANES):
+            row = g_ref[:, start : start + LANES]
+            o_ref[start : start + LANES] = jnp.broadcast_to(row, (LANES, LANES)).T
+
+    return call(body, jax.ShapeDtypeStruct((channels, LANES), jnp.float32))(gain)
 
 
 def pad_rows(values, rows, axis):
@@ -615,9 +646,6 @@
     def ring(values):
         return [values] + [shift(values, "fsdp", j) for j in range(1, n)]
 
-    def block(values, axis):
-        return lax.dynamic_slice_in_dim(values, mine * kept, kept, axis)
-
     def pad_blocks(values, axis):
         if shard == kept:
             return values
@@ -627,11 +655,14 @@
         return parts.reshape(shape[:axis] + [shape[axis] // kept * shard] + shape[axis + 1 :])
 
     def in_plane_stats(values):
-        values = values[None]
+        rows = values.shape[0] // 2
         size = 1
         while size < planes:
             other = lax.ppermute(values, "spatial", [(i, i ^ size) for i in range(planes)])
-            values = jnp.concatenate([values, other], axis=0)
+            away = values[:rows] - other[:rows]
+            mean = 0.5 * (values[:rows] + other[:rows])
+            squares = values[rows:] + other[rows:] + (0.5 * size * entries) * (away * away)
+            values = jnp.concatenate([mean, squares], axis=0)
             size *= 2
         return values
 
@@ -642,13 +673,13 @@
         return near + far, jnp.concatenate([back, back ^ 1]).astype(jnp.int32)
 
     flat = features.reshape(samples, length, channels)
-    own_stats = local_stats(flat, members(channels, channels, channels, group), group)
-    edges = ring(jnp.concatenate([flat[:, :width], flat[:, length - width :]], axis=1))
+    own_stats, edges = local_stats(flat, members(channels, channels, channels, group), group, width)
+    edges = ring(edges)
     last, first = halo_rows(edges, width)
     above = shift_rows(last, 1)
     below = shift_rows(first, -1)
     own_stats = in_plane_stats(own_stats)
-    mids = rows_message(own_stats, norm_gains[:1], entries, flat[:, width : length - width])
+    mids = rows_message(own_stats, norm_gains[:1], entries * planes, flat, width)
     mids = ring(mids)
 
     wide = attn_weight.shape[1]
@@ -663,22 +694,20 @@
     projection, from_rows = in_plane(turned)
     if wide % part or kept % part:
         turned = place(from_rows, projection, 1)
-        projection = [
-            jnp.concatenate(
-                [
-                    turned[:, :wide].reshape(n * wide, n * shard),
-                    turned[:, wide : wide + kept].reshape(channels, n * shard),
-                ]
-            )
-        ]
+        projection = jnp.concatenate(
+            [
+                turned[:, :wide].reshape(n * wide, n * shard),
+                turned[:, wide : wide + kept].reshape(channels, n * shard),
+            ]
+        )
+    else:
+        projection = place_weights(from_rows, projection, wide, channels)
 
     first_weight = pad_rows(conv_first.T, shard, 0)
     second_weight = pad_rows(pad_blocks(conv_second.T, 1), shard, 0)
-    bias = time_bias(step_index, roster, time_weight, block(temb_weight, 1), shard)
-    index = jnp.arange(shard)
-    pick = jnp.where(index < kept, index + mine * kept, -1)[:, None] == jnp.arange(channels)[None, :]
-
-    edges, mids, own_stats, own_edges, own_mids = first_conv(
+    bias = time_bias(ends, step_index, roster, time_weight, temb_weight, shard, kept)
+
+    edges, mids, own_stats, own_edges, own_mids, gain = first_conv(
         ends,
         edges,
         mids,
@@ -687,8 +716,9 @@
         first_weight,
         bias,
         same_group(shard, shard, kept, group),
-        pick.astype(jnp.bfloat16),
+        norm_gains[1:2],
         jnp.asarray(np.eye(-(-count // 8) * 8, LANES, dtype=np.float32)),
+        kept,
         width,
         group,
     )
@@ -697,9 +727,8 @@
     last, first = halo_columns(edges, width)
     above = shift_rows(last, 1)
     below = shift_rows(first, -1)
-    gain = pad_rows(block(norm_gains[1:2], 1), shard, 1)
     own_stats = in_plane_stats(own_stats)
-    mids = columns_message(own_stats, gain, entries, mids)
+    mids = columns_message(own_stats, gain, entries * planes, mids)
     mids = ring(mids)
     sums = second_conv(
         ends,
@@ -717,20 +746,18 @@
     own = [sums[0]] + [shift(sums[t], "fsdp", -t) for t in range(1, n)]
     own = place(((mine + np.arange(n)) % n).astype(jnp.int32), own, 1)
     chunks, _ = in_plane(own)
-    gain = jnp.broadcast_to(pad_blocks(norm_gains[2], 0)[:, None], (n * shard, LANES))
+    gain = gain_column(pad_blocks(norm_gains[2:3], 1))
     unpad = None
     if shard != kept:
         at = np.arange(n * shard)
         at = np.where(at % shard < kept, at // shard * kept + at % shard, -1)
         unpad = jnp.asarray(at[:, None] == np.arange(channels)[None, :], jnp.bfloat16)
     return attention(
-        from_rows,
         chunks,
         projection,
         gain,
         members(n * shard, shard, kept, group),
         unpad,
-        wide,
         width,
         group,
     )

time: 180 us -> 182 us (1.011)
  starting transfers between devices: 54.5 us -> 58.8 us
  local copies, waits for them, and re-layouts: 9.27 us -> 5.79 us
  waiting for transfers between devices: 52.5 us -> 54.8 us
  other arithmetic: 7.5 us -> 5.21 us
    ppermute x24, waiting for transfers between devices: 44.7 us -> 49.7 us  [shift(): lax.ppermute(values, axis, [(i, (i + step) % count) for i in range(count)])]
    ppermute x6, starting transfers between devices: 4.63 us -> 7.68 us  [in_plane_stats(): lax.ppermute(values, 'spatial', [(i, i ^ size) for i in range(planes)])]
    concatenate x7 -> x6, other arithmetic: 3.41 us -> 1.29 us  [in_plane_stats(): values = jnp.concatenate([mean, squares], axis=0)]
    dynamic_slice x2 -> x0, local copies, waits for them, and re-layouts: 2.11 us -> none  [block(): return lax.dynamic_slice_in_dim(values, mine * kept, kept, axis)]
    slice x3 -> x1, local copies, waits for them, and re-layouts: 3.28 us -> 1.42 us  [local(): gain = gain_column(pad_blocks(norm_gains[2:3], 1))]
    unnamed x50 -> x70, local copies, waits for them, and re-layouts: 2.98 us -> 4.37 us
    pallas_call x11 -> x13, Pallas kernels: 55.2 us -> 56 us  [run(): pl.pallas_call(body, out_shape=out_shape, in_specs=specs, out_specs=outs,...]
  transfers between devices with their start and end apart: 42 -> 42, of which waited for: 16 -> 15; matrix products, arithmetic and copies ran while one was open for 6% -> 3% of each run, Pallas kernels for 14% -> 16%
where the time goes in v2:
time: 182 us
  starting transfers between devices  58.8 us (32%)
  Pallas kernels  56 us (31%)
  waiting for transfers between devices  54.8 us (30%)
  local copies, waits for them, and re-layouts  5.79 us (3%)
  other arithmetic  5.21 us (3%)
    pallas_call x13, Pallas kernels, run(): pl.pallas_call(body, out_shape=out_shape, in_specs=specs, out_specs=outs,...  56 us
    ppermute x24, waiting for transfers between devices, shift(): lax.ppermute(values, axis, [(i, (i + step) % count) for i in range(count)])  49.7 us
    ppermute x24, starting transfers between devices, shift(): lax.ppermute(values, axis, [(i, (i + step) % count) for i in range(count)])  42.6 us
    ppermute x6, starting transfers between devices, in_plane_stats(): lax.ppermute(values, 'spatial', [(i, i ^ size) for i in range(planes)])  7.68 us
    ppermute x4, starting transfers between devices, shift_rows(): return lax.ppermute(values, 'spatial', pairs)  6.91 us
    ppermute x6, waiting for transfers between devices, in_plane_stats(): lax.ppermute(values, 'spatial', [(i, i ^ size) for i in range(planes)])  5.07 us
    unnamed x70, local copies, waits for them, and re-layouts  4.37 us
  transfers between devices with their start and end apart: 42, of which 15 were waited for; matrix products, arithmetic and copies ran while one was open for 3% of the time, Pallas kernels for 16%

profile of v2, /device:TPU:0, one launch (start us, length us, event | category | flops | bytes accessed | tf_op | source)
XLA Modules:
  0.0 181.6 jit_solution(3243383386190939803)
XLA Ops:
  0.0 2.4 %shard_map.163 = (f32[2,640]{1,0:T(2,128)}, bf16[1,128,640]{2,1,0:T(8,128)(2,1)}) custom-call(bf16[1,256,640]{2,1,0:T(8,128)(2,1)} %bitcast.11, bf16[640,128]{1,0:T(8,128)(2,1)} %constant.71.clone.g_ref.refs_11_), custom_call_target="tpu_custom_call" | custom-call | tf_op jit(solution)/shard_map/pallas_call | solution.py:29
  2.9 1.0 collective-permute-done.3
  3.9 0.8 add_multiply_fusion.5
  4.7 2.9 %collective-permute-start.4 = (f32[2,640]{1,0:T(2,128)S(1)}, f32[2,640]{1,0:T(2,128)S(1)}, u32[]{:S(2)}, u32[]{:S(2)}) collective-permute-start(f32[2,640]{1,0:T(2,128)S(1)} %pad_maximum_fusion.3), channel_id=1, source_target_pairs={{0,8},{4,12},{8,0},{12,4},{16,24},{20,28},{24,16},{28,20},{1,9},{5... | collective-permute-start | bytes 15368 | tf_op jit(solution)/shard_map/ppermute | solution.py:661
  7.6 1.6 collective-permute-start
  9.1 2.6 %collective-permute-start.1 = (bf16[1,128,640]{2,1,0:T(8,128)(2,1)}, bf16[1,128,640]{2,1,0:T(8,128)(2,1)S(1)}, u32[]{:S(2)}, u32[]{:S(2)}) collective-permute-start(bf16[1,128,640]{2,1,0:T(8,128)(2,1)} %get-tuple-element.21.refs_0_.refs_1_), channel_id=1, source_target_pairs={{0,2},{1,3},{2,0},{3,1},{4,6},{5,7},{6,4},{7,5},{8,10},{9,11},{10,... | collective-permute-start | bytes 491528 | tf_op jit(solution)/shard_map/ppermute | solution.py:46
  11.7 1.3 collective-permute-start.2
  13.1 1.6 collective-permute-start.5
  14.7 1.4 fusion.11
  16.1 0.6 collective-permute-done.refs_1_.refs_2_
  16.7 6.0 %collective-permute-done.1.refs_2_.refs_3_ = bf16[1,128,640]{2,1,0:T(8,128)(2,1)S(1)} collective-permute-done((bf16[1,128,640]{2,1,0:T(8,128)(2,1)}, bf16[1,128,640]{2,1,0:T(8,128)(2,1)S(1)}, u32[]{:S(2)}, u32[]{:S(2)}) %collective-permute-start.1) | collective-permute-done | bytes 163872 | tf_op jit(solution)/shard_map/ppermute | solution.py:46
  22.8 0.6 copy-done.14
  23.4 0.6 copy-done.15
  24.0 2.0 %shard_map.165 = (bf16[4,64,640]{2,1,0:T(8,128)(2,1)}, bf16[4,64,640]{2,1,0:T(8,128)(2,1)}) custom-call(bf16[1,128,640]{2,1,0:T(8,128)(2,1)} %get-tuple-element.21.refs_0_.refs_1_, bf16[1,128,640]{2,1,0:T(8,128)(2,1)} %copy-done.13, bf16[1,128,640]{2,1,0:T(8,128)(2,1)} %copy-done.14, bf16[1,128,640]{2,1,0:T(8,128)(2,1)} %copy-done.15), custom_call_target="tpu_custom_call" | custom-call | tf_op jit(solution)/shard_map/pallas_call | solution.py:29
  26.1 1.3 collective-permute-start.10
  27.4 3.0 %collective-permute-start.9 = (bf16[4,64,640]{2,1,0:T(8,128)(2,1)}, bf16[4,64,640]{2,1,0:T(8,128)(2,1)S(1)}, u32[]{:S(2)}, u32[]{:S(2)}) collective-permute-start(bf16[4,64,640]{2,1,0:T(8,128)(2,1)} %get-tuple-element.23), channel_id=1, source_target_pairs={{0,4},{4,8},{8,12},{12,16},{16,20},{20,24},{24,28},{1,5},{5,9},{9,... | collective-permute-start | bytes 983048 | tf_op jit(solution)/shard_map/ppermute | solution.py:769
  30.5 0.6 pad_maximum_fusion.5.p_ref
  31.0 1.7 shard_map.164.refs_5_
  32.7 3.3 %collective-permute-start.6 = (bf16[1,144,640]{2,1,0:T(8,128)(2,1)}, bf16[1,144,640]{2,1,0:T(8,128)(2,1)S(1)}, u32[]{:S(2)}, u32[]{:S(2)}) collective-permute-start(bf16[1,144,640]{2,1,0:T(8,128)(2,1)} %shard_map.164.refs_5_), channel_id=1, source_target_pairs={{0,1},{1,2},{2,3},{3,0},{4,5},{5,6},{6,7},{7,4},{8,9},{9,10},{10,1... | collective-permute-start | bytes 552968 | tf_op jit(solution)/shard_map/ppermute | solution.py:46
  36.1 2.3 %collective-permute-start.7 = (bf16[1,144,640]{2,1,0:T(8,128)(2,1)}, bf16[1,144,640]{2,1,0:T(8,128)(2,1)S(1)}, u32[]{:S(2)}, u32[]{:S(2)}) collective-permute-start(bf16[1,144,640]{2,1,0:T(8,128)(2,1)} %shard_map.164.refs_5_), channel_id=1, source_target_pairs={{0,2},{1,3},{2,0},{3,1},{4,6},{5,7},{6,4},{7,5},{8,10},{9,11},{10,... | collective-permute-start | bytes 552968 | tf_op jit(solution)/shard_map/ppermute | solution.py:46
  39.1 0.7 pad_add_fusion.n_ref.refs_0_
  39.8 4.2 %shard_map.166.refs_12_ = f32[160,128]{1,0:T(8,128)} custom-call(s32[3]{0:T(128)} %pad_add_fusion.n_ref.refs_0_, s32[1]{0:T(128)S(6)} %copy.18.i_ref, f32[1,50]{1,0:T(1,128)} %bitcast.15, f32[320,1280]{1,0:T(8,128)} %w_ref.1, f32[1280,640]{1,0:T(8,128)} %t_ref.1), custom_call_target="tpu_custom_call" | custom-call | tf_op jit(solution)/shard_map/pallas_call | solution.py:29
  44.0 7.0 %collective-permute-done.7.refs_7_ = bf16[1,144,640]{2,1,0:T(8,128)(2,1)S(1)} collective-permute-done((bf16[1,144,640]{2,1,0:T(8,128)(2,1)}, bf16[1,144,640]{2,1,0:T(8,128)(2,1)S(1)}, u32[]{:S(2)}, u32[]{:S(2)}) %collective-permute-start.7) | collective-permute-done | bytes 184352 | tf_op jit(solution)/shard_map/ppermute | solution.py:46
  51.0 0.6 copy-done.33
  52.0 7.8 %shard_map.167 = (bf16[160,512]{1,0:T(8,128)(2,1)}, bf16[160,512]{1,0:T(8,128)(2,1)}, f32[8,160]{1,0:T(8,128)}, bf16[160,512]{1,0:T(8,128)(2,1)}, bf16[160,512]{1,0:T(8,128)(2,1)}, /*index=5*/f32[1,160]{1,0:T(1,128)}) custom-call(s32[3]{0:T(128)} %pad_add_fusion.n_ref.refs_0_, bf16[1,128,640]{2,1,0:T(8,128)(2,1)} %get-tuple-element.21.refs_0_.refs_1_, ...), custom_call_target="tpu_custom_call" | custom-call | flops 1887436800 | tf_op jit(solution)/shard_map/pallas_call | solution.py:29
  59.9 1.3 collective-permute-done.14
  61.2 0.8 add_multiply_fusion.2
  62.0 1.0 collective-permute-start.15
  62.9 2.8 %collective-permute-done.15 = f32[8,160]{1,0:T(8,128)S(1)} collective-permute-done((f32[8,160]{1,0:T(8,128)S(1)}, f32[8,160]{1,0:T(8,128)S(1)}, u32[]{:S(2)}, u32[]{:S(2)}) %collective-permute-start.15) | collective-permute-done | bytes 5152 | tf_op jit(solution)/shard_map/ppermute | solution.py:661
  65.7 1.6 collective-permute-start.16
  67.4 4.5 %collective-permute-start.32 = (bf16[1,80,640]{2,1,0:T(8,128)(2,1)S(1)}, bf16[1,80,640]{2,1,0:T(8,128)(2,1)S(1)}, u32[]{:S(2)}, u32[]{:S(2)}) collective-permute-start(bf16[1,80,640]{2,1,0:T(8,128)(2,1)S(1)} %fusion.1.refs_0_), channel_id=1, source_target_pairs={{0,1},{1,2},{2,3},{3,0},{4,5},{5,6},{6,7},{7,4},{8,9},{9,10},{10,1... | collective-permute-start | bytes 307208 | tf_op jit(solution)/shard_map/ppermute | solution.py:46
  72.6 2.4 %collective-permute-start.12 = (bf16[160,512]{1,0:T(8,128)(2,1)}, bf16[160,512]{1,0:T(8,128)(2,1)S(1)}, u32[]{:S(2)}, u32[]{:S(2)}) collective-permute-start(bf16[160,512]{1,0:T(8,128)(2,1)} %get-tuple-element.25.refs_0_.refs_1_), channel_id=1, source_target_pairs={{0,2},{1,3},{2,0},{3,1},{4,6},{5,7},{6,4},{7,5},{8,10},{9,11},{10,... | collective-permute-start | bytes 491528 | tf_op jit(solution)/shard_map/ppermute | solution.py:46
  74.9 2.8 %collective-permute-start.13 = (bf16[160,512]{1,0:T(8,128)(2,1)}, bf16[160,512]{1,0:T(8,128)(2,1)S(1)}, u32[]{:S(2)}, u32[]{:S(2)}) collective-permute-start(bf16[160,512]{1,0:T(8,128)(2,1)} %get-tuple-element.25.refs_0_.refs_1_), channel_id=1, source_target_pairs={{0,3},{1,0},{2,1},{3,2},{4,7},{5,4},{6,5},{7,6},{8,11},{9,8},{10,9... | collective-permute-start | bytes 491528 | tf_op jit(solution)/shard_map/ppermute | solution.py:46
  77.8 3.9 %collective-permute-done.11.refs_1_.refs_2_ = bf16[160,512]{1,0:T(8,128)(2,1)S(1)} collective-permute-done((bf16[160,512]{1,0:T(8,128)(2,1)}, bf16[160,512]{1,0:T(8,128)(2,1)S(1)}, u32[]{:S(2)}, u32[]{:S(2)}) %collective-permute-start.11) | collective-permute-done | bytes 163872 | tf_op jit(solution)/shard_map/ppermute | solution.py:46
  81.7 0.7 pad_maximum_fusion.2.p_ref
  82.3 1.8 shard_map.168.refs_5_
  84.1 5.5 %collective-permute-done.12.refs_2_.refs_3_ = bf16[160,512]{1,0:T(8,128)(2,1)S(1)} collective-permute-done((bf16[160,512]{1,0:T(8,128)(2,1)}, bf16[160,512]{1,0:T(8,128)(2,1)S(1)}, u32[]{:S(2)}, u32[]{:S(2)}) %collective-permute-start.12) | collective-permute-done | bytes 163872 | tf_op jit(solution)/shard_map/ppermute | solution.py:46
  89.6 5.5 %collective-permute-start.17 = (bf16[160,640]{1,0:T(8,128)(2,1)}, bf16[160,640]{1,0:T(8,128)(2,1)S(1)}, u32[]{:S(2)}, u32[]{:S(2)}) collective-permute-start(bf16[160,640]{1,0:T(8,128)(2,1)} %shard_map.168.refs_5_), channel_id=1, source_target_pairs={{0,1},{1,2},{2,3},{3,0},{4,5},{5,6},{6,7},{7,4},{8,9},{9,10},{10,1... | collective-permute-start | bytes 614408 | tf_op jit(solution)/shard_map/ppermute | solution.py:46
  95.1 3.4 %collective-permute-start.18 = (bf16[160,640]{1,0:T(8,128)(2,1)}, bf16[160,640]{1,0:T(8,128)(2,1)S(1)}, u32[]{:S(2)}, u32[]{:S(2)}) collective-permute-start(bf16[160,640]{1,0:T(8,128)(2,1)} %shard_map.168.refs_5_), channel_id=1, source_target_pairs={{0,2},{1,3},{2,0},{3,1},{4,6},{5,7},{6,4},{7,5},{8,10},{9,11},{10,... | collective-permute-start | bytes 614408 | tf_op jit(solution)/shard_map/ppermute | solution.py:46
  98.5 2.3 %shard_map.169 = (bf16[640,256]{1,0:T(8,128)(2,1)}, bf16[640,256]{1,0:T(8,128)(2,1)}) custom-call(bf16[160,512]{1,0:T(8,128)(2,1)} %get-tuple-element.25.refs_0_.refs_1_, bf16[160,512]{1,0:T(8,128)(2,1)} %copy-done.16, bf16[160,512]{1,0:T(8,128)(2,1)} %copy-done.17, bf16[160,512]{1,0:T(8,128)(2,1)} %copy-done.18), custom_call_target="tpu_custom_call" | custom-call | tf_op jit(solution)/shard_map/pallas_call | solution.py:29
  100.7 1.3 collective-permute-start.20
  102.1 1.0 collective-permute-start.19
  103.1 1.3 collective-permute-start.21
  104.9 1.8 %shard_map.172.refs_0_ = bf16[4,80,640]{2,1,0:T(8,128)(2,1)} custom-call(s32[4]{0:T(128)} %and_select_fusion.w_ref, bf16[1,80,640]{2,1,0:T(8,128)(2,1)} %copy-done.1, bf16[1,80,640]{2,1,0:T(8,128)(2,1)} %copy-done.19, bf16[1,80,640]{2,1,0:T(8,128)(2,1)} %copy-done.20, bf16[1,80,640]{2,1,0:T(8,128)(2,1)} %copy-done.21), custom_call_target="tpu_custom_call" | custom-call | tf_op jit(solution)/shard_map/pallas_call | solution.py:29
  106.7 2.9 %collective-permute-start.35 = (bf16[4,80,640]{2,1,0:T(8,128)(2,1)}, bf16[4,80,640]{2,1,0:T(8,128)(2,1)S(1)}, u32[]{:S(2)}, u32[]{:S(2)}) collective-permute-start(bf16[4,80,640]{2,1,0:T(8,128)(2,1)} %shard_map.172.refs_0_), channel_id=1, source_target_pairs={{0,8},{4,12},{8,16},{12,20},{16,24},{20,28},{24,0},{28,4},{1,9},{5... | collective-permute-start | bytes 1228808 | tf_op jit(solution)/shard_map/ppermute | solution.py:46
  109.6 1.2 collective-permute-done.18.refs_7_
  111.4 2.6 %collective-permute-done.19.refs_8_ = bf16[160,640]{1,0:T(8,128)(2,1)S(1)} collective-permute-done((bf16[160,640]{1,0:T(8,128)(2,1)}, bf16[160,640]{1,0:T(8,128)(2,1)S(1)}, u32[]{:S(2)}, u32[]{:S(2)}) %collective-permute-start.19) | collective-permute-done | bytes 204832 | tf_op jit(solution)/shard_map/ppermute | solution.py:46
  114.9 7.5 %shard_map.170 = (bf16[1,160,256]{2,1,0:T(8,128)(2,1)}, bf16[1,160,256]{2,1,0:T(8,128)(2,1)}, bf16[1,160,256]{2,1,0:T(8,128)(2,1)}, bf16[1,160,256]{2,1,0:T(8,128)(2,1)}) custom-call(s32[3]{0:T(128)} %pad_add_fusion.n_ref.refs_0_, bf16[160,512]{1,0:T(8,128)(2,1)} %get-tuple-element.25.refs_0_.refs_1_, bf16[160,512]{1,0:T(8,128)(2,1)} %copy-done.16, ...), custom_call_target="tpu_custom_call" | custom-call | flops 1887436800 | tf_op jit(solution)/shard_map/pallas_call | solution.py:29
  122.4 2.1 %collective-permute-start.22 = (bf16[1,160,256]{2,1,0:T(8,128)(2,1)}, bf16[1,160,256]{2,1,0:T(8,128)(2,1)S(1)}, u32[]{:S(2)}, u32[]{:S(2)}) collective-permute-start(bf16[1,160,256]{2,1,0:T(8,128)(2,1)} %get-tuple-element.34), channel_id=1, source_target_pairs={{0,3},{1,0},{2,1},{3,2},{4,7},{5,4},{6,5},{7,6},{8,11},{9,8},{10,9... | collective-permute-start | bytes 245768 | tf_op jit(solution)/shard_map/ppermute | solution.py:46
  124.5 1.1 collective-permute-start.23
  125.5 4.0 %collective-permute-done.36.refs_2_ = bf16[4,80,640]{2,1,0:T(8,128)(2,1)S(1)} collective-permute-done((bf16[4,80,640]{2,1,0:T(8,128)(2,1)}, bf16[4,80,640]{2,1,0:T(8,128)(2,1)S(1)}, u32[]{:S(2)}, u32[]{:S(2)}) %collective-permute-start.36) | collective-permute-done | bytes 409632 | tf_op jit(solution)/shard_map/ppermute | solution.py:46
  130.1 1.9 %collective-permute-done.23.refs_2_ = bf16[1,160,256]{2,1,0:T(8,128)(2,1)S(1)} collective-permute-done((bf16[1,160,256]{2,1,0:T(8,128)(2,1)}, bf16[1,160,256]{2,1,0:T(8,128)(2,1)S(1)}, u32[]{:S(2)}, u32[]{:S(2)}) %collective-permute-start.23) | collective-permute-done | bytes 81952 | tf_op jit(solution)/shard_map/ppermute | solution.py:46
  132.0 0.8 collective-permute-start.24
  133.3 5.2 %collective-permute-done.24.refs_3_ = bf16[1,160,256]{2,1,0:T(8,128)(2,1)S(1)} collective-permute-done((bf16[1,160,256]{2,1,0:T(8,128)(2,1)}, bf16[1,160,256]{2,1,0:T(8,128)(2,1)S(1)}, u32[]{:S(2)}, u32[]{:S(2)}) %collective-permute-start.24) | collective-permute-done | bytes 81952 | tf_op jit(solution)/shard_map/ppermute | solution.py:46
  138.4 0.6 copy-done.24
  139.0 1.8 shard_map.171.refs_0_
  140.8 1.8 collective-permute-start.25
  142.8 1.8 %collective-permute-start.27 = (bf16[1,640,256]{2,1,0:T(8,128)(2,1)}, bf16[1,640,256]{2,1,0:T(8,128)(2,1)S(1)}, u32[]{:S(2)}, u32[]{:S(2)}) collective-permute-start(bf16[1,640,256]{2,1,0:T(8,128)(2,1)} %shard_map.171.refs_0_), channel_id=1, source_target_pairs={{0,24},{4,28},{8,0},{12,4},{16,8},{20,12},{24,16},{28,20},{1,25},{... | collective-permute-start | bytes 983048 | tf_op jit(solution)/shard_map/ppermute | solution.py:46
  145.1 7.4 %collective-permute-done.25.refs_1_ = bf16[1,640,256]{2,1,0:T(8,128)(2,1)S(1)} collective-permute-done((bf16[1,640,256]{2,1,0:T(8,128)(2,1)}, bf16[1,640,256]{2,1,0:T(8,128)(2,1)S(1)}, u32[]{:S(2)}, u32[]{:S(2)}) %collective-permute-start.25) | collective-permute-done | bytes 327712 | tf_op jit(solution)/shard_map/ppermute | solution.py:46
  152.6 4.4 %collective-permute-done.26.refs_2_ = bf16[1,640,256]{2,1,0:T(8,128)(2,1)S(1)} collective-permute-done((bf16[1,640,256]{2,1,0:T(8,128)(2,1)}, bf16[1,640,256]{2,1,0:T(8,128)(2,1)S(1)}, u32[]{:S(2)}, u32[]{:S(2)}) %collective-permute-start.26) | collective-permute-done | bytes 327712 | tf_op jit(solution)/shard_map/ppermute | solution.py:46
  157.5 1.6 shard_map.174.refs_9_
  159.7 0.7 copy-done.8
  160.5 3.8 %shard_map.173.refs_8_ = bf16[2560,640]{1,0:T(8,128)(2,1)} custom-call(s32[8]{0:T(128)} %pad_add_fusion.1.w_ref, bf16[4,80,640]{2,1,0:T(8,128)(2,1)} %shard_map.172.refs_0_, bf16[4,80,640]{2,1,0:T(8,128)(2,1)} %copy-done.2, bf16[4,80,640]{2,1,0:T(8,128)(2,1)} %copy-done.3, bf16[4,80,640]{2,1,0:T(8,128)(2,1)} %copy-done.4, bf16[4,80,640]{2,1,0:T(8,128)(2,1)} %copy-done.5, ...), custom_call_target="tpu_custom_call" | custom-call | tf_op jit(solution)/shard_map/pallas_call | solution.py:29
  164.3 17.3 %shard_map.175 = bf16[1,4,64,640]{3,2,1,0:T(8,128)(2,1)} custom-call(bf16[1,640,256]{2,1,0:T(8,128)(2,1)} %shard_map.171.refs_0_, bf16[1,640,256]{2,1,0:T(8,128)(2,1)} %copy-done.9, bf16[1,640,256]{2,1,0:T(8,128)(2,1)} %copy-done.10, bf16[1,640,256]{2,1,0:T(8,128)(2,1)} %copy-done.11, bf16[1,640,256]{2,1,0:T(8,128)(2,1)} %collective-permute-done.28.refs_4_, ...), custom_call_target="tpu_custom_call" | custom-call | tf_op jit(solution)/shard_map/pallas_call | solution.py:29
  (122 shorter events, 6.7 us)
Async XLA Ops:
  2.4 1.5 collective-permute-start.3
  4.7 8.4 %collective-permute-start.4 = (f32[2,640]{1,0:T(2,128)S(1)}, f32[2,640]{1,0:T(2,128)S(1)}, u32[]{:S(2)}, u32[]{:S(2)}) collective-permute-start(f32[2,640]{1,0:T(2,128)S(1)} %pad_maximum_fusion.3), channel_id=1, source_target_pairs={{0,8},{4,12},{8,0},{12,4},{16,24},{20,28},{24,16},{28,20},{1,9},{5... | collective-permute-start | bytes 15368 | tf_op jit(solution)/shard_map/ppermute | solution.py:661
  7.6 9.2 %collective-permute-start = (bf16[1,128,640]{2,1,0:T(8,128)(2,1)}, bf16[1,128,640]{2,1,0:T(8,128)(2,1)S(1)}, u32[]{:S(2)}, u32[]{:S(2)}) collective-permute-start(bf16[1,128,640]{2,1,0:T(8,128)(2,1)} %get-tuple-element.21.refs_0_.refs_1_), channel_id=1, source_target_pairs={{0,1},{1,2},{2,3},{3,0},{4,5},{5,6},{6,7},{7,4},{8,9},{9,10},{10,1... | collective-permute-start | bytes 491528 | tf_op jit(solution)/shard_map/ppermute | solution.py:46
  9.1 13.6 %collective-permute-start.1 = (bf16[1,128,640]{2,1,0:T(8,128)(2,1)}, bf16[1,128,640]{2,1,0:T(8,128)(2,1)S(1)}, u32[]{:S(2)}, u32[]{:S(2)}) collective-permute-start(bf16[1,128,640]{2,1,0:T(8,128)(2,1)} %get-tuple-element.21.refs_0_.refs_1_), channel_id=1, source_target_pairs={{0,2},{1,3},{2,0},{3,1},{4,6},{5,7},{6,4},{7,5},{8,10},{9,11},{10,... | collective-permute-start | bytes 491528 | tf_op jit(solution)/shard_map/ppermute | solution.py:46
  11.7 11.0 %collective-permute-start.2 = (bf16[1,128,640]{2,1,0:T(8,128)(2,1)}, bf16[1,128,640]{2,1,0:T(8,128)(2,1)S(1)}, u32[]{:S(2)}, u32[]{:S(2)}) collective-permute-start(bf16[1,128,640]{2,1,0:T(8,128)(2,1)} %get-tuple-element.21.refs_0_.refs_1_), channel_id=1, source_target_pairs={{0,3},{1,0},{2,1},{3,2},{4,7},{5,4},{6,5},{7,6},{8,11},{9,8},{10,9... | collective-permute-start | bytes 491528 | tf_op jit(solution)/shard_map/ppermute | solution.py:46
  13.1 17.3 %collective-permute-start.5 = (f32[2,640]{1,0:T(2,128)S(1)}, f32[2,640]{1,0:T(2,128)S(1)}, u32[]{:S(2)}, u32[]{:S(2)}) collective-permute-start(f32[2,640]{1,0:T(2,128)S(1)} %pad_maximum_fusion.4), channel_id=1, source_target_pairs={{0,16},{4,20},{8,24},{12,28},{16,0},{20,4},{24,8},{28,12},{1,17},{... | collective-permute-start | bytes 15368 | tf_op jit(solution)/shard_map/ppermute | solution.py:661
  16.7 6.0 %copy-start.13 = (bf16[1,128,640]{2,1,0:T(8,128)(2,1)}, bf16[1,128,640]{2,1,0:T(8,128)(2,1)S(1)}, u32[]{:S(2)}) copy-start(bf16[1,128,640]{2,1,0:T(8,128)(2,1)S(1)} %collective-permute-done.refs_1_.refs_2_) | copy-start | bytes 491524
  26.1 24.9 %collective-permute-start.10 = (bf16[4,64,640]{2,1,0:T(8,128)(2,1)}, bf16[4,64,640]{2,1,0:T(8,128)(2,1)S(1)}, u32[]{:S(2)}, u32[]{:S(2)}) collective-permute-start(bf16[4,64,640]{2,1,0:T(8,128)(2,1)} %get-tuple-element.24), channel_id=1, source_target_pairs={{4,0},{8,4},{12,8},{16,12},{20,16},{24,20},{28,24},{5,1},{9,5},{13... | collective-permute-start | bytes 983048 | tf_op jit(solution)/shard_map/ppermute | solution.py:769
  27.4 23.7 %collective-permute-start.9 = (bf16[4,64,640]{2,1,0:T(8,128)(2,1)}, bf16[4,64,640]{2,1,0:T(8,128)(2,1)S(1)}, u32[]{:S(2)}, u32[]{:S(2)}) collective-permute-start(bf16[4,64,640]{2,1,0:T(8,128)(2,1)} %get-tuple-element.23), channel_id=1, source_target_pairs={{0,4},{4,8},{8,12},{12,16},{16,20},{20,24},{24,28},{1,5},{5,9},{9,... | collective-permute-start | bytes 983048 | tf_op jit(solution)/shard_map/ppermute | solution.py:769
  32.7 11.3 %collective-permute-start.6 = (bf16[1,144,640]{2,1,0:T(8,128)(2,1)}, bf16[1,144,640]{2,1,0:T(8,128)(2,1)S(1)}, u32[]{:S(2)}, u32[]{:S(2)}) collective-permute-start(bf16[1,144,640]{2,1,0:T(8,128)(2,1)} %shard_map.164.refs_5_), channel_id=1, source_target_pairs={{0,1},{1,2},{2,3},{3,0},{4,5},{5,6},{6,7},{7,4},{8,9},{9,10},{10,1... | collective-permute-start | bytes 552968 | tf_op jit(solution)/shard_map/ppermute | solution.py:46
  36.1 14.9 %collective-permute-start.7 = (bf16[1,144,640]{2,1,0:T(8,128)(2,1)}, bf16[1,144,640]{2,1,0:T(8,128)(2,1)S(1)}, u32[]{:S(2)}, u32[]{:S(2)}) collective-permute-start(bf16[1,144,640]{2,1,0:T(8,128)(2,1)} %shard_map.164.refs_5_), channel_id=1, source_target_pairs={{0,2},{1,3},{2,0},{3,1},{4,6},{5,7},{6,4},{7,5},{8,10},{9,11},{10,... | collective-permute-start | bytes 552968 | tf_op jit(solution)/shard_map/ppermute | solution.py:46
  38.4 12.6 %collective-permute-start.8 = (bf16[1,144,640]{2,1,0:T(8,128)(2,1)}, bf16[1,144,640]{2,1,0:T(8,128)(2,1)S(1)}, u32[]{:S(2)}, u32[]{:S(2)}) collective-permute-start(bf16[1,144,640]{2,1,0:T(8,128)(2,1)} %shard_map.164.refs_5_), channel_id=1, source_target_pairs={{0,3},{1,0},{2,1},{3,2},{4,7},{5,4},{6,5},{7,6},{8,11},{9,8},{10,9... | collective-permute-start | bytes 552968 | tf_op jit(solution)/shard_map/ppermute | solution.py:46
  44.0 7.0 %copy-start.32 = (bf16[1,144,640]{2,1,0:T(8,128)(2,1)}, bf16[1,144,640]{2,1,0:T(8,128)(2,1)S(1)}, u32[]{:S(2)}) copy-start(bf16[1,144,640]{2,1,0:T(8,128)(2,1)S(1)} %collective-permute-done.6.refs_6_) | copy-start | bytes 552964
  51.9 15.4 %copy-start = (bf16[640,480]{0,1:T(8,128)(2,1)S(1)}, bf16[640,480]{0,1:T(8,128)(2,1)}, u32[]{:S(2)}) copy-start(bf16[640,480]{0,1:T(8,128)(2,1)} %param.25) | copy-start | bytes 1843204
  51.9 15.4 %copy-start.12 = (bf16[640,160]{0,1:T(8,128)(2,1)S(1)}, bf16[640,160]{0,1:T(8,128)(2,1)}, u32[]{:S(2)}) copy-start(bf16[640,160]{0,1:T(8,128)(2,1)} %param.26) | copy-start | bytes 614404
  59.7 1.4 collective-permute-start.14
  62.0 3.7 %collective-permute-start.15 = (f32[8,160]{1,0:T(8,128)S(1)}, f32[8,160]{1,0:T(8,128)S(1)}, u32[]{:S(2)}, u32[]{:S(2)}) collective-permute-start(f32[8,160]{1,0:T(8,128)S(1)} %pad_maximum_fusion), channel_id=1, source_target_pairs={{0,8},{4,12},{8,0},{12,4},{16,24},{20,28},{24,16},{28,20},{1,9},{5... | collective-permute-start | bytes 15368 | tf_op jit(solution)/shard_map/ppermute | solution.py:661
  65.7 9.2 %collective-permute-start.16 = (f32[8,160]{1,0:T(8,128)S(1)}, f32[8,160]{1,0:T(8,128)S(1)}, u32[]{:S(2)}, u32[]{:S(2)}) collective-permute-start(f32[8,160]{1,0:T(8,128)S(1)} %pad_maximum_fusion.1), channel_id=1, source_target_pairs={{0,16},{4,20},{8,24},{12,28},{16,0},{20,4},{24,8},{28,12},{1,17},{... | collective-permute-start | bytes 15368 | tf_op jit(solution)/shard_map/ppermute | solution.py:661
  67.4 37.5 %copy-start.1 = (bf16[1,80,640]{2,1,0:T(8,128)(2,1)}, bf16[1,80,640]{2,1,0:T(8,128)(2,1)S(1)}, u32[]{:S(2)}) copy-start(bf16[1,80,640]{2,1,0:T(8,128)(2,1)S(1)} %fusion.1.refs_0_) | copy-start | bytes 307204
  67.4 33.3 %collective-permute-start.32 = (bf16[1,80,640]{2,1,0:T(8,128)(2,1)S(1)}, bf16[1,80,640]{2,1,0:T(8,128)(2,1)S(1)}, u32[]{:S(2)}, u32[]{:S(2)}) collective-permute-start(bf16[1,80,640]{2,1,0:T(8,128)(2,1)S(1)} %fusion.1.refs_0_), channel_id=1, source_target_pairs={{0,1},{1,2},{2,3},{3,0},{4,5},{5,6},{6,7},{7,4},{8,9},{9,10},{10,1... | collective-permute-start | bytes 307208 | tf_op jit(solution)/shard_map/ppermute | solution.py:46
  71.9 30.1 %collective-permute-start.33 = (bf16[1,80,640]{2,1,0:T(8,128)(2,1)S(1)}, bf16[1,80,640]{2,1,0:T(8,128)(2,1)S(1)}, u32[]{:S(2)}, u32[]{:S(2)}) collective-permute-start(bf16[1,80,640]{2,1,0:T(8,128)(2,1)S(1)} %fusion.1.refs_0_), channel_id=1, source_target_pairs={{0,2},{1,3},{2,0},{3,1},{4,6},{5,7},{6,4},{7,5},{8,10},{9,11},{10,... | collective-permute-start | bytes 307208 | tf_op jit(solution)/shard_map/ppermute | solution.py:46
  72.5 9.2 %collective-permute-start.11 = (bf16[160,512]{1,0:T(8,128)(2,1)}, bf16[160,512]{1,0:T(8,128)(2,1)S(1)}, u32[]{:S(2)}, u32[]{:S(2)}) collective-permute-start(bf16[160,512]{1,0:T(8,128)(2,1)} %get-tuple-element.25.refs_0_.refs_1_), channel_id=1, source_target_pairs={{0,1},{1,2},{2,3},{3,0},{4,5},{5,6},{6,7},{7,4},{8,9},{9,10},{10,1... | collective-permute-start | bytes 491528 | tf_op jit(solution)/shard_map/ppermute | solution.py:46
  72.6 17.0 %collective-permute-start.12 = (bf16[160,512]{1,0:T(8,128)(2,1)}, bf16[160,512]{1,0:T(8,128)(2,1)S(1)}, u32[]{:S(2)}, u32[]{:S(2)}) collective-permute-start(bf16[160,512]{1,0:T(8,128)(2,1)} %get-tuple-element.25.refs_0_.refs_1_), channel_id=1, source_target_pairs={{0,2},{1,3},{2,0},{3,1},{4,6},{5,7},{6,4},{7,5},{8,10},{9,11},{10,... | collective-permute-start | bytes 491528 | tf_op jit(solution)/shard_map/ppermute | solution.py:46
  74.9 20.2 %collective-permute-start.13 = (bf16[160,512]{1,0:T(8,128)(2,1)}, bf16[160,512]{1,0:T(8,128)(2,1)S(1)}, u32[]{:S(2)}, u32[]{:S(2)}) collective-permute-start(bf16[160,512]{1,0:T(8,128)(2,1)} %get-tuple-element.25.refs_0_.refs_1_), channel_id=1, source_target_pairs={{0,3},{1,0},{2,1},{3,2},{4,7},{5,4},{6,5},{7,6},{8,11},{9,8},{10,9... | collective-permute-start | bytes 491528 | tf_op jit(solution)/shard_map/ppermute | solution.py:46
  81.7 16.8 %copy-start.16 = (bf16[160,512]{1,0:T(8,128)(2,1)}, bf16[160,512]{1,0:T(8,128)(2,1)S(1)}, u32[]{:S(2)}) copy-start(bf16[160,512]{1,0:T(8,128)(2,1)S(1)} %collective-permute-done.11.refs_1_.refs_2_) | copy-start | bytes 491524
  81.7 21.4 %collective-permute-start.34 = (bf16[1,80,640]{2,1,0:T(8,128)(2,1)S(1)}, bf16[1,80,640]{2,1,0:T(8,128)(2,1)S(1)}, u32[]{:S(2)}, u32[]{:S(2)}) collective-permute-start(bf16[1,80,640]{2,1,0:T(8,128)(2,1)S(1)} %fusion.1.refs_0_), channel_id=1, source_target_pairs={{0,3},{1,0},{2,1},{3,2},{4,7},{5,4},{6,5},{7,6},{8,11},{9,8},{10,9... | collective-permute-start | bytes 307208 | tf_op jit(solution)/shard_map/ppermute | solution.py:46
  89.6 8.9 %copy-start.17 = (bf16[160,512]{1,0:T(8,128)(2,1)}, bf16[160,512]{1,0:T(8,128)(2,1)S(1)}, u32[]{:S(2)}) copy-start(bf16[160,512]{1,0:T(8,128)(2,1)S(1)} %collective-permute-done.12.refs_2_.refs_3_) | copy-start | bytes 491524
  89.6 17.2 %collective-permute-start.17 = (bf16[160,640]{1,0:T(8,128)(2,1)}, bf16[160,640]{1,0:T(8,128)(2,1)S(1)}, u32[]{:S(2)}, u32[]{:S(2)}) collective-permute-start(bf16[160,640]{1,0:T(8,128)(2,1)} %shard_map.168.refs_5_), channel_id=1, source_target_pairs={{0,1},{1,2},{2,3},{3,0},{4,5},{5,6},{6,7},{7,4},{8,9},{9,10},{10,1... | collective-permute-start | bytes 614408 | tf_op jit(solution)/shard_map/ppermute | solution.py:46
  95.1 3.4 %copy-start.18 = (bf16[160,512]{1,0:T(8,128)(2,1)}, bf16[160,512]{1,0:T(8,128)(2,1)S(1)}, u32[]{:S(2)}) copy-start(bf16[160,512]{1,0:T(8,128)(2,1)S(1)} %collective-permute-done.13.refs_3_.refs_4_) | copy-start | bytes 491524
  95.1 15.7 %collective-permute-start.18 = (bf16[160,640]{1,0:T(8,128)(2,1)}, bf16[160,640]{1,0:T(8,128)(2,1)S(1)}, u32[]{:S(2)}, u32[]{:S(2)}) collective-permute-start(bf16[160,640]{1,0:T(8,128)(2,1)} %shard_map.168.refs_5_), channel_id=1, source_target_pairs={{0,2},{1,3},{2,0},{3,1},{4,6},{5,7},{6,4},{7,5},{8,10},{9,11},{10,... | collective-permute-start | bytes 614408 | tf_op jit(solution)/shard_map/ppermute | solution.py:46
  100.7 4.1 %copy-start.19 = (bf16[1,80,640]{2,1,0:T(8,128)(2,1)}, bf16[1,80,640]{2,1,0:T(8,128)(2,1)S(1)}, u32[]{:S(2)}) copy-start(bf16[1,80,640]{2,1,0:T(8,128)(2,1)S(1)} %collective-permute-done.32.refs_1_) | copy-start | bytes 307204
  100.7 13.2 %collective-permute-start.20 = (bf16[640,256]{1,0:T(8,128)(2,1)}, bf16[640,256]{1,0:T(8,128)(2,1)S(1)}, u32[]{:S(2)}, u32[]{:S(2)}) collective-permute-start(bf16[640,256]{1,0:T(8,128)(2,1)} %get-tuple-element.29), channel_id=1, source_target_pairs={{0,4},{4,8},{8,12},{12,16},{16,20},{20,24},{24,28},{1,5},{5,9},{9,... | collective-permute-start | bytes 983048 | tf_op jit(solution)/shard_map/ppermute | solution.py:769
  102.1 11.9 %collective-permute-start.19 = (bf16[160,640]{1,0:T(8,128)(2,1)}, bf16[160,640]{1,0:T(8,128)(2,1)S(1)}, u32[]{:S(2)}, u32[]{:S(2)}) collective-permute-start(bf16[160,640]{1,0:T(8,128)(2,1)} %shard_map.168.refs_5_), channel_id=1, source_target_pairs={{0,3},{1,0},{2,1},{3,2},{4,7},{5,4},{6,5},{7,6},{8,11},{9,8},{10,9... | collective-permute-start | bytes 614408 | tf_op jit(solution)/shard_map/ppermute | solution.py:46
  103.1 11.1 %collective-permute-start.21 = (bf16[640,256]{1,0:T(8,128)(2,1)}, bf16[640,256]{1,0:T(8,128)(2,1)S(1)}, u32[]{:S(2)}, u32[]{:S(2)}) collective-permute-start(bf16[640,256]{1,0:T(8,128)(2,1)} %get-tuple-element.30), channel_id=1, source_target_pairs={{4,0},{8,4},{12,8},{16,12},{20,16},{24,20},{28,24},{5,1},{9,5},{13... | collective-permute-start | bytes 983048 | tf_op jit(solution)/shard_map/ppermute | solution.py:769
  106.7 7.4 %copy-start.29 = (bf16[160,640]{1,0:T(8,128)(2,1)}, bf16[160,640]{1,0:T(8,128)(2,1)S(1)}, u32[]{:S(2)}) copy-start(bf16[160,640]{1,0:T(8,128)(2,1)S(1)} %collective-permute-done.17.refs_6_) | copy-start | bytes 614404
  106.7 17.7 %collective-permute-start.35 = (bf16[4,80,640]{2,1,0:T(8,128)(2,1)}, bf16[4,80,640]{2,1,0:T(8,128)(2,1)S(1)}, u32[]{:S(2)}, u32[]{:S(2)}) collective-permute-start(bf16[4,80,640]{2,1,0:T(8,128)(2,1)} %shard_map.172.refs_0_), channel_id=1, source_target_pairs={{0,8},{4,12},{8,16},{12,20},{16,24},{20,28},{24,0},{28,4},{1,9},{5... | collective-permute-start | bytes 1228808 | tf_op jit(solution)/shard_map/ppermute | solution.py:46
  110.9 3.3 %copy-start.30 = (bf16[160,640]{1,0:T(8,128)(2,1)}, bf16[160,640]{1,0:T(8,128)(2,1)S(1)}, u32[]{:S(2)}) copy-start(bf16[160,640]{1,0:T(8,128)(2,1)S(1)} %collective-permute-done.18.refs_7_) | copy-start | bytes 614404
  110.9 18.7 %collective-permute-start.36 = (bf16[4,80,640]{2,1,0:T(8,128)(2,1)}, bf16[4,80,640]{2,1,0:T(8,128)(2,1)S(1)}, u32[]{:S(2)}, u32[]{:S(2)}) collective-permute-start(bf16[4,80,640]{2,1,0:T(8,128)(2,1)} %shard_map.172.refs_0_), channel_id=1, source_target_pairs={{0,16},{4,20},{8,24},{12,28},{16,0},{20,4},{24,8},{28,12},{1,17},{... | collective-permute-start | bytes 1228808 | tf_op jit(solution)/shard_map/ppermute | solution.py:46
  114.0 28.7 %collective-permute-start.37 = (bf16[4,80,640]{2,1,0:T(8,128)(2,1)}, bf16[4,80,640]{2,1,0:T(8,128)(2,1)S(1)}, u32[]{:S(2)}, u32[]{:S(2)}) collective-permute-start(bf16[4,80,640]{2,1,0:T(8,128)(2,1)} %shard_map.172.refs_0_), channel_id=1, source_target_pairs={{0,24},{4,28},{8,0},{12,4},{16,8},{20,12},{24,16},{28,20},{1,25},{... | collective-permute-start | bytes 1228808 | tf_op jit(solution)/shard_map/ppermute | solution.py:46
  114.0 28.8 %collective-permute-start.38 = (bf16[4,80,640]{2,1,0:T(8,128)(2,1)}, bf16[4,80,640]{2,1,0:T(8,128)(2,1)S(1)}, u32[]{:S(2)}, u32[]{:S(2)}) collective-permute-start(bf16[4,80,640]{2,1,0:T(8,128)(2,1)} %shard_map.172.refs_0_), channel_id=1, source_target_pairs={{0,4},{4,0},{8,12},{12,8},{16,20},{20,16},{24,28},{28,24},{1,5},{5... | collective-permute-start | bytes 1228808 | tf_op jit(solution)/shard_map/ppermute | solution.py:671
  122.4 7.2 %collective-permute-start.22 = (bf16[1,160,256]{2,1,0:T(8,128)(2,1)}, bf16[1,160,256]{2,1,0:T(8,128)(2,1)S(1)}, u32[]{:S(2)}, u32[]{:S(2)}) collective-permute-start(bf16[1,160,256]{2,1,0:T(8,128)(2,1)} %get-tuple-element.34), channel_id=1, source_target_pairs={{0,3},{1,0},{2,1},{3,2},{4,7},{5,4},{6,5},{7,6},{8,11},{9,8},{10,9... | collective-permute-start | bytes 245768 | tf_op jit(solution)/shard_map/ppermute | solution.py:46
  124.5 35.2 %copy-start.2 = (bf16[4,80,640]{2,1,0:T(8,128)(2,1)}, bf16[4,80,640]{2,1,0:T(8,128)(2,1)S(1)}, u32[]{:S(2)}) copy-start(bf16[4,80,640]{2,1,0:T(8,128)(2,1)S(1)} %collective-permute-done.35.refs_1_) | copy-start | bytes 1228804
  124.5 7.5 %collective-permute-start.23 = (bf16[1,160,256]{2,1,0:T(8,128)(2,1)}, bf16[1,160,256]{2,1,0:T(8,128)(2,1)S(1)}, u32[]{:S(2)}, u32[]{:S(2)}) collective-permute-start(bf16[1,160,256]{2,1,0:T(8,128)(2,1)} %get-tuple-element.35), channel_id=1, source_target_pairs={{0,2},{1,3},{2,0},{3,1},{4,6},{5,7},{6,4},{7,5},{8,10},{9,11},{10,... | collective-permute-start | bytes 245768 | tf_op jit(solution)/shard_map/ppermute | solution.py:46
  129.6 30.1 %copy-start.3 = (bf16[4,80,640]{2,1,0:T(8,128)(2,1)}, bf16[4,80,640]{2,1,0:T(8,128)(2,1)S(1)}, u32[]{:S(2)}) copy-start(bf16[4,80,640]{2,1,0:T(8,128)(2,1)S(1)} %collective-permute-done.36.refs_2_) | copy-start | bytes 1228804
  129.6 15.1 %collective-permute-start.39 = (bf16[4,80,640]{2,1,0:T(8,128)(2,1)S(1)}, bf16[4,80,640]{2,1,0:T(8,128)(2,1)S(1)}, u32[]{:S(2)}, u32[]{:S(2)}) collective-permute-start(bf16[4,80,640]{2,1,0:T(8,128)(2,1)S(1)} %collective-permute-done.35.refs_1_), channel_id=1, source_target_pairs={{0,4},{4,0},{8,12},{12,8},{16,20},{20,16},{24,28},{28,24},{1,5},{5... | collective-permute-start | bytes 1228808 | tf_op jit(solution)/shard_map/ppermute | solution.py:671
  129.6 8.8 %copy-start.22 = (bf16[1,160,256]{2,1,0:T(8,128)(2,1)}, bf16[1,160,256]{2,1,0:T(8,128)(2,1)S(1)}, u32[]{:S(2)}) copy-start(bf16[1,160,256]{2,1,0:T(8,128)(2,1)S(1)} %collective-permute-done.22.refs_1_) | copy-start | bytes 245764
  129.6 15.0 %collective-permute-start.40 = (bf16[4,80,640]{2,1,0:T(8,128)(2,1)S(1)}, bf16[4,80,640]{2,1,0:T(8,128)(2,1)S(1)}, u32[]{:S(2)}, u32[]{:S(2)}) collective-permute-start(bf16[4,80,640]{2,1,0:T(8,128)(2,1)S(1)} %collective-permute-done.36.refs_2_), channel_id=1, source_target_pairs={{0,4},{4,0},{8,12},{12,8},{16,20},{20,16},{24,28},{28,24},{1,5},{5... | collective-permute-start | bytes 1228808 | tf_op jit(solution)/shard_map/ppermute | solution.py:671
  132.0 6.5 %copy-start.23 = (bf16[1,160,256]{2,1,0:T(8,128)(2,1)}, bf16[1,160,256]{2,1,0:T(8,128)(2,1)S(1)}, u32[]{:S(2)}) copy-start(bf16[1,160,256]{2,1,0:T(8,128)(2,1)S(1)} %collective-permute-done.23.refs_2_) | copy-start | bytes 245764
  132.0 6.4 %collective-permute-start.24 = (bf16[1,160,256]{2,1,0:T(8,128)(2,1)}, bf16[1,160,256]{2,1,0:T(8,128)(2,1)S(1)}, u32[]{:S(2)}, u32[]{:S(2)}) collective-permute-start(bf16[1,160,256]{2,1,0:T(8,128)(2,1)} %get-tuple-element.36), channel_id=1, source_target_pairs={{0,1},{1,2},{2,3},{3,0},{4,5},{5,6},{6,7},{7,4},{8,9},{9,10},{10,1... | collective-permute-start | bytes 245768 | tf_op jit(solution)/shard_map/ppermute | solution.py:46
  140.8 11.7 %collective-permute-start.25 = (bf16[1,640,256]{2,1,0:T(8,128)(2,1)}, bf16[1,640,256]{2,1,0:T(8,128)(2,1)S(1)}, u32[]{:S(2)}, u32[]{:S(2)}) collective-permute-start(bf16[1,640,256]{2,1,0:T(8,128)(2,1)} %shard_map.171.refs_0_), channel_id=1, source_target_pairs={{0,8},{4,12},{8,16},{12,20},{16,24},{20,28},{24,0},{28,4},{1,9},{5... | collective-permute-start | bytes 983048 | tf_op jit(solution)/shard_map/ppermute | solution.py:46
  142.6 17.1 %copy-start.4 = (bf16[4,80,640]{2,1,0:T(8,128)(2,1)}, bf16[4,80,640]{2,1,0:T(8,128)(2,1)S(1)}, u32[]{:S(2)}) copy-start(bf16[4,80,640]{2,1,0:T(8,128)(2,1)S(1)} %collective-permute-done.37.refs_3_) | copy-start | bytes 1228804
  142.6 14.4 %collective-permute-start.26 = (bf16[1,640,256]{2,1,0:T(8,128)(2,1)}, bf16[1,640,256]{2,1,0:T(8,128)(2,1)S(1)}, u32[]{:S(2)}, u32[]{:S(2)}) collective-permute-start(bf16[1,640,256]{2,1,0:T(8,128)(2,1)} %shard_map.171.refs_0_), channel_id=1, source_target_pairs={{0,16},{4,20},{8,24},{12,28},{16,0},{20,4},{24,8},{28,12},{1,17},{... | collective-permute-start | bytes 983048 | tf_op jit(solution)/shard_map/ppermute | solution.py:46
  142.8 16.9 %copy-start.5 = (bf16[4,80,640]{2,1,0:T(8,128)(2,1)}, bf16[4,80,640]{2,1,0:T(8,128)(2,1)S(1)}, u32[]{:S(2)}) copy-start(bf16[4,80,640]{2,1,0:T(8,128)(2,1)S(1)} %collective-permute-done.38.refs_4_) | copy-start | bytes 1228804
  142.8 14.2 %collective-permute-start.27 = (bf16[1,640,256]{2,1,0:T(8,128)(2,1)}, bf16[1,640,256]{2,1,0:T(8,128)(2,1)S(1)}, u32[]{:S(2)}, u32[]{:S(2)}) collective-permute-start(bf16[1,640,256]{2,1,0:T(8,128)(2,1)} %shard_map.171.refs_0_), channel_id=1, source_target_pairs={{0,24},{4,28},{8,0},{12,4},{16,8},{20,12},{24,16},{28,20},{1,25},{... | collective-permute-start | bytes 983048 | tf_op jit(solution)/shard_map/ppermute | solution.py:46
  144.6 15.1 %copy-start.6 = (bf16[4,80,640]{2,1,0:T(8,128)(2,1)}, bf16[4,80,640]{2,1,0:T(8,128)(2,1)S(1)}, u32[]{:S(2)}) copy-start(bf16[4,80,640]{2,1,0:T(8,128)(2,1)S(1)} %collective-permute-done.39.refs_5_) | copy-start | bytes 1228804
  144.6 15.0 %collective-permute-start.41 = (bf16[4,80,640]{2,1,0:T(8,128)(2,1)S(1)}, bf16[4,80,640]{2,1,0:T(8,128)(2,1)S(1)}, u32[]{:S(2)}, u32[]{:S(2)}) collective-permute-start(bf16[4,80,640]{2,1,0:T(8,128)(2,1)S(1)} %collective-permute-done.37.refs_3_), channel_id=1, source_target_pairs={{0,4},{4,0},{8,12},{12,8},{16,20},{20,16},{24,28},{28,24},{1,5},{5... | collective-permute-start | bytes 1228808 | tf_op jit(solution)/shard_map/ppermute | solution.py:671
  144.6 15.1 %copy-start.7 = (bf16[4,80,640]{2,1,0:T(8,128)(2,1)}, bf16[4,80,640]{2,1,0:T(8,128)(2,1)S(1)}, u32[]{:S(2)}) copy-start(bf16[4,80,640]{2,1,0:T(8,128)(2,1)S(1)} %collective-permute-done.40.refs_6_) | copy-start | bytes 1228804
  144.7 19.6 %collective-permute-start.28 = (bf16[1,640,256]{2,1,0:T(8,128)(2,1)}, bf16[1,640,256]{2,1,0:T(8,128)(2,1)}, u32[]{:S(2)}, u32[]{:S(2)}) collective-permute-start(bf16[1,640,256]{2,1,0:T(8,128)(2,1)} %shard_map.171.refs_0_), channel_id=1, source_target_pairs={{0,4},{4,0},{8,12},{12,8},{16,20},{20,16},{24,28},{28,24},{1,5},{5... | collective-permute-start | bytes 983048 | tf_op jit(solution)/shard_map/ppermute | solution.py:671
  152.6 11.8 %copy-start.9 = (bf16[1,640,256]{2,1,0:T(8,128)(2,1)}, bf16[1,640,256]{2,1,0:T(8,128)(2,1)S(1)}, u32[]{:S(2)}) copy-start(bf16[1,640,256]{2,1,0:T(8,128)(2,1)S(1)} %collective-permute-done.25.refs_1_) | copy-start | bytes 983044
  152.6 11.7 %collective-permute-start.29 = (bf16[1,640,256]{2,1,0:T(8,128)(2,1)S(1)}, bf16[1,640,256]{2,1,0:T(8,128)(2,1)}, u32[]{:S(2)}, u32[]{:S(2)}) collective-permute-start(bf16[1,640,256]{2,1,0:T(8,128)(2,1)S(1)} %collective-permute-done.25.refs_1_), channel_id=1, source_target_pairs={{0,4},{4,0},{8,12},{12,8},{16,20},{20,16},{24,28},{28,24},{1,5},{5... | collective-permute-start | bytes 983048 | tf_op jit(solution)/shard_map/ppermute | solution.py:671
  157.0 7.3 %copy-start.10 = (bf16[1,640,256]{2,1,0:T(8,128)(2,1)}, bf16[1,640,256]{2,1,0:T(8,128)(2,1)S(1)}, u32[]{:S(2)}) copy-start(bf16[1,640,256]{2,1,0:T(8,128)(2,1)S(1)} %collective-permute-done.26.refs_2_) | copy-start | bytes 983044
  157.0 7.3 %collective-permute-start.30 = (bf16[1,640,256]{2,1,0:T(8,128)(2,1)S(1)}, bf16[1,640,256]{2,1,0:T(8,128)(2,1)}, u32[]{:S(2)}, u32[]{:S(2)}) collective-permute-start(bf16[1,640,256]{2,1,0:T(8,128)(2,1)S(1)} %collective-permute-done.26.refs_2_), channel_id=1, source_target_pairs={{0,4},{4,0},{8,12},{12,8},{16,20},{20,16},{24,28},{28,24},{1,5},{5... | collective-permute-start | bytes 983048 | tf_op jit(solution)/shard_map/ppermute | solution.py:671
  157.0 7.3 %copy-start.11 = (bf16[1,640,256]{2,1,0:T(8,128)(2,1)}, bf16[1,640,256]{2,1,0:T(8,128)(2,1)S(1)}, u32[]{:S(2)}) copy-start(bf16[1,640,256]{2,1,0:T(8,128)(2,1)S(1)} %collective-permute-done.27.refs_3_) | copy-start | bytes 983044
  157.0 7.3 %collective-permute-start.31 = (bf16[1,640,256]{2,1,0:T(8,128)(2,1)S(1)}, bf16[1,640,256]{2,1,0:T(8,128)(2,1)}, u32[]{:S(2)}, u32[]{:S(2)}) collective-permute-start(bf16[1,640,256]{2,1,0:T(8,128)(2,1)S(1)} %collective-permute-done.27.refs_3_), channel_id=1, source_target_pairs={{0,4},{4,0},{8,12},{12,8},{16,20},{20,16},{24,28},{28,24},{1,5},{5... | collective-permute-start | bytes 983048 | tf_op jit(solution)/shard_map/ppermute | solution.py:671
  (13 other events, 12.7 us)

commit v3 on v2

--- a/solution.py
+++ b/solution.py
@@ -19,8 +19,13 @@
 NT = (((1,), (1,)), ((), ()))
 
 
-def call(body, out_shape, scratch=(), scalars=0, flops=0):
+def call(body, out_shape, scratch=(), scalars=0, flops=0, near=(), limit=16):
     def run(*operands):
+        near_ones = set(range(len(operands))) if near is True else set(near)
+        placed = [
+            pltpu.with_memory_space_constraint(x, pltpu.VMEM) if i in near_ones and i >= scalars else x
+            for i, x in enumerate(operands)
+        ]
         specs = [
             pl.BlockSpec(memory_space=pltpu.SMEM if i < scalars else pltpu.VMEM)
             for i in range(len(operands))
@@ -32,11 +37,11 @@
             in_specs=specs,
             out_specs=outs,
             scratch_shapes=list(scratch),
-            compiler_params=pltpu.CompilerParams(vmem_limit_bytes=60 * 2**20),
+            compiler_params=pltpu.CompilerParams(vmem_limit_bytes=limit * 2**20),
             cost_estimate=pl.CostEstimate(flops=flops, transcendentals=0, bytes_accessed=0)
             if flops
             else None,
-        )(*operands)
+        )(*placed)
 
     return run
 
@@ -252,7 +257,7 @@
             refs[-2][j * samples : (j + 1) * samples] = e[:, width:]
             refs[-1][j * samples : (j + 1) * samples] = e[:, :width]
 
-    return call(body, (shape, shape))(*edges)
+    return call(body, (shape, shape), near=True)(*edges)
 
 
 def halo_columns(edges, width):
@@ -273,7 +278,7 @@
                 refs[-2][rows, cut] = last.astype(jnp.bfloat16)
                 refs[-1][rows, cut] = first.astype(jnp.bfloat16)
 
-    return call(body, (shape, shape))(*edges)
+    return call(body, (shape, shape), near=True)(*edges)
 
 
 def tap_rows(weight, row, depth):
@@ -395,12 +400,14 @@
         pltpu.VMEM((2, length + 2 * width, channels), jnp.bfloat16),
         pltpu.VMEM((count, shard, length), jnp.float32),
     ]
-    return call(body, out_shape, scratch, scalars=1, flops=6 * count * length * channels * 3 * shard)(
+    return call(body, out_shape, scratch, scalars=1, flops=6 * count * length * channels * 3 * shard, limit=32)(
         ends, *edges, *mids, above, below, weight, bias, groups, gain, eye
     )
 
 
-def second_conv(ends, edges, mids, above, below, weight, own_edges, own_mids, samples, width):
+def second_conv(
+    ends, edges, mids, above, below, weight, own_edges, own_mids, samples, width, begin, end
+):
     n = len(edges)
     shard = edges[0].shape[0]
     count = n * samples
@@ -467,7 +474,7 @@
                 )
             out = column_shift(y, shard, width)
             q = t * samples + i
-            target = o_refs[t].at[i] if unrolled else o_refs[0].at[t, i]
+            target = o_refs[t - begin].at[i] if unrolled else o_refs[0].at[t, i]
             target[:, :edge] = (
                 out[:, :edge] + fe_ref[:, tile(q, edge)].astype(jnp.float32)
             ).astype(jnp.bfloat16)
@@ -476,7 +483,7 @@
             ).astype(jnp.bfloat16)
 
         if unrolled:
-            for q in range(count):
+            for q in range(begin * samples, end * samples):
                 sample(q // samples, q % samples, q % 2)
         else:
 
@@ -487,12 +494,13 @@
 
     result = call(
         body,
-        (shape,) * n if unrolled else shape,
+        (shape,) * (end - begin) if unrolled else shape,
         [pltpu.VMEM((2 if unrolled else 1, 3, n * shard, length), jnp.bfloat16)],
         scalars=1,
         flops=6 * count * length * n * shard * 3 * shard,
+        limit=32,
     )(ends, *edges, *mids, above, below, weight, own_edges, own_mids)
-    return result if unrolled else [result[t] for t in range(n)]
+    return list(result) if unrolled else [result[t] for t in range(n)]
 
 
 def split_dot(ones, column):
@@ -599,6 +607,7 @@
             pltpu.VMEM((length, channels), jnp.bfloat16),
             pltpu.VMEM((length, channels), jnp.bfloat16),
         ],
+        limit=48,
     )(*operands)
 
 
@@ -644,7 +653,10 @@
     ends = jnp.stack([row > 0, row < planes - 1, mine]).astype(jnp.int32)
 
     def ring(values):
-        return [values] + [shift(values, "fsdp", j) for j in range(1, n)]
+        found = [values]
+        for j in range(1, n):
+            found.append(shift(values, "fsdp", j))
+        return found
 
     def pad_blocks(values, axis):
         if shard == kept:
@@ -730,20 +742,27 @@
     own_stats = in_plane_stats(own_stats)
     mids = columns_message(own_stats, gain, entries * planes, mids)
     mids = ring(mids)
-    sums = second_conv(
-        ends,
-        edges,
-        mids,
-        above,
-        below,
-        second_weight,
-        own_edges,
-        own_mids,
-        samples,
-        width,
-    )
-
-    own = [sums[0]] + [shift(sums[t], "fsdp", -t) for t in range(1, n)]
+    own = {}
+    turns = [(n // 2, n), (0, n // 2)] if n <= 4 else [(0, n)]
+    for first, last in turns:
+        sums = second_conv(
+            ends,
+            edges,
+            mids,
+            above,
+            below,
+            second_weight,
+            own_edges,
+            own_mids,
+            samples,
+            width,
+            first,
+            last,
+        )
+
+        for t, found in zip(range(first, last), sums):
+            own[t] = shift(found, "fsdp", -t) if t > 0 else found
+    own = [own[t] for t in range(n)]
     own = place(((mine + np.arange(n)) % n).astype(jnp.int32), own, 1)
     chunks, _ = in_plane(own)
     gain = gain_column(pad_blocks(norm_gains[2:3], 1))

time: 182 us -> 167 us (0.918)
  Pallas kernels: 56 us -> 34.3 us
  starting transfers between devices: 58.8 us -> 69.8 us
  other arithmetic: 5.21 us -> 1.25 us
  waiting for transfers between devices: 54.8 us -> 52.3 us
  local copies, waits for them, and re-layouts: 5.79 us -> 8.08 us
    pallas_call x13 -> x14, Pallas kernels: 56 us -> 34.3 us  [run(): pl.pallas_call(body, out_shape=out_shape, in_specs=specs, out_specs=outs,...]
    ppermute x24, starting transfers between devices: 42.6 us -> 54 us  [shift(): lax.ppermute(values, axis, [(i, (i + step) % count) for i in range(count)])]
    ppermute x6, waiting for transfers between devices: 5.07 us -> 1.89 us  [in_plane_stats(): lax.ppermute(values, 'spatial', [(i, i ^ size) for i in range(planes)])]
    unnamed x70 -> x26, local copies, waits for them, and re-layouts: 4.37 us -> 7.26 us
  transfers between devices with their start and end apart: 42 -> 42, of which waited for: 15 -> 14; matrix products, arithmetic and copies ran while one was open for 3% -> 1% of each run, Pallas kernels for 16% -> 7%
where the time goes in v3:
time: 167 us
  starting transfers between devices  69.8 us (42%)
  waiting for transfers between devices  52.3 us (31%)
  Pallas kernels  34.3 us (21%)
  local copies, waits for them, and re-layouts  8.08 us (5%)
    ppermute x24, starting transfers between devices, shift(): lax.ppermute(values, axis, [(i, (i + step) % count) for i in range(count)])  54 us
    ppermute x24, waiting for transfers between devices, shift(): lax.ppermute(values, axis, [(i, (i + step) % count) for i in range(count)])  50.3 us
    pallas_call x14, Pallas kernels, run(): pl.pallas_call(body, out_shape=out_shape, in_specs=specs, out_specs=outs,...  34.3 us
    ppermute x4, starting transfers between devices, shift_rows(): return lax.ppermute(values, 'spatial', pairs)  7.32 us
    unnamed x26, local copies, waits for them, and re-layouts  7.26 us
    ppermute x6, starting transfers between devices, in_plane_stats(): lax.ppermute(values, 'spatial', [(i, i ^ size) for i in range(planes)])  6.85 us
  transfers between devices with their start and end apart: 42, of which 14 were waited for; matrix products, arithmetic and copies ran while one was open for 1% of the time, Pallas kernels for 7%

profile of v3, /device:TPU:0, one launch (start us, length us, event | category | flops | bytes accessed | tf_op | source)
XLA Modules:
  0.0 166.6 jit_solution(15100360571453728354)
XLA Ops:
  0.0 1.1 copy-done.3
  1.1 0.9 copy-done.5
  2.0 0.7 shard_map.163
  2.7 0.6 collective-permute-start.3
  3.3 0.8 collective-permute-done.3
  4.2 2.9 %collective-permute-start.4 = (f32[2,640]{1,0:T(2,128)S(1)}, f32[2,640]{1,0:T(2,128)S(1)}, u32[]{:S(2)}, u32[]{:S(2)}) collective-permute-start(f32[2,640]{1,0:T(2,128)S(1)} %pad_maximum_fusion.3), channel_id=1, source_target_pairs={{0,8},{4,12},{8,0},{12,4},{16,24},{20,28},{24,16},{28,20},{1,9},{5... | collective-permute-start | bytes 15368 | tf_op jit(solution)/shard_map/ppermute | solution.py:673
  7.0 1.6 collective-permute-start
  8.6 2.6 %collective-permute-start.1 = (bf16[1,128,640]{2,1,0:T(8,128)(2,1)S(1)}, bf16[1,128,640]{2,1,0:T(8,128)(2,1)S(1)}, u32[]{:S(2)}, u32[]{:S(2)}) collective-permute-start(bf16[1,128,640]{2,1,0:T(8,128)(2,1)S(1)} %get-tuple-element.21.refs_0_.refs_1_), channel_id=1, source_target_pairs={{0,2},{1,3},{2,0},{3,1},{4,6},{5,7},{6,4},{7,5},{8,10},{9,11},{10,... | collective-permute-start | bytes 491528 | tf_op jit(solution)/shard_map/ppermute | solution.py:51
  11.2 1.3 collective-permute-start.2
  12.6 1.6 collective-permute-start.5
  14.2 0.8 fusion.11
  15.0 1.0 collective-permute-done.refs_1_.refs_2_
  16.0 6.0 %collective-permute-done.1.refs_2_.refs_3_ = bf16[1,128,640]{2,1,0:T(8,128)(2,1)S(1)} collective-permute-done((bf16[1,128,640]{2,1,0:T(8,128)(2,1)S(1)}, bf16[1,128,640]{2,1,0:T(8,128)(2,1)S(1)}, u32[]{:S(2)}, u32[]{:S(2)}) %collective-permute-start.1) | collective-permute-done | bytes 163872 | tf_op jit(solution)/shard_map/ppermute | solution.py:51
  22.0 0.8 shard_map.165
  22.8 1.3 collective-permute-start.10
  24.1 3.0 %collective-permute-start.9 = (bf16[4,64,640]{2,1,0:T(8,128)(2,1)S(1)}, bf16[4,64,640]{2,1,0:T(8,128)(2,1)S(1)}, u32[]{:S(2)}, u32[]{:S(2)}) collective-permute-start(bf16[4,64,640]{2,1,0:T(8,128)(2,1)S(1)} %get-tuple-element.23), channel_id=1, source_target_pairs={{0,4},{4,8},{8,12},{12,16},{16,20},{20,24},{24,28},{1,5},{5,9},{9,... | collective-permute-start | bytes 983048 | tf_op jit(solution)/shard_map/ppermute | solution.py:788
  27.2 1.0 copy-done.4
  28.2 4.0 %collective-permute-start.6 = (bf16[1,144,640]{2,1,0:T(8,128)(2,1)S(1)}, bf16[1,144,640]{2,1,0:T(8,128)(2,1)}, u32[]{:S(2)}, u32[]{:S(2)}) collective-permute-start(bf16[1,144,640]{2,1,0:T(8,128)(2,1)S(1)} %shard_map.164.refs_5_), channel_id=1, source_target_pairs={{0,1},{1,2},{2,3},{3,0},{4,5},{5,6},{6,7},{7,4},{8,9},{9,10},{10,1... | collective-permute-start | bytes 552968 | tf_op jit(solution)/shard_map/ppermute | solution.py:51
  32.2 1.6 collective-permute-start.7
  33.9 0.8 collective-permute-start.8
  35.4 1.9 %copy-done.1 = f32[1280,640]{1,0:T(8,128)S(1)} copy-done((f32[1280,640]{1,0:T(8,128)S(1)}, f32[1280,640]{1,0:T(8,128)}, u32[]{:S(2)}) %copy-start.1) | copy-done | bytes 3276824
  37.3 0.7 copy-done.8
  38.0 1.8 %shard_map.166.refs_12_ = f32[160,128]{1,0:T(8,128)S(1)} custom-call(s32[3]{0:T(128)S(1)} %pad_add_fusion.n_ref.refs_0_, s32[1]{0:T(128)S(6)} %copy.18.i_ref, f32[1,50]{1,0:T(1,128)S(1)} %bitcast.13, f32[320,1280]{1,0:T(8,128)S(1)} %copy-done.2, f32[1280,640]{1,0:T(8,128)S(1)} %copy-done.1), custom_call_target="tpu_custom_call" | custom-call | tf_op jit(solution)/shard_map/pallas_call | solution.py:34
  39.8 6.6 %collective-permute-done.7.refs_7_ = bf16[1,144,640]{2,1,0:T(8,128)(2,1)} collective-permute-done((bf16[1,144,640]{2,1,0:T(8,128)(2,1)S(1)}, bf16[1,144,640]{2,1,0:T(8,128)(2,1)}, u32[]{:S(2)}, u32[]{:S(2)}) %collective-permute-start.7) | collective-permute-done | bytes 184352 | tf_op jit(solution)/shard_map/ppermute | solution.py:51
  46.5 6.0 %shard_map.167 = (bf16[160,512]{1,0:T(8,128)(2,1)S(1)}, bf16[160,512]{1,0:T(8,128)(2,1)S(1)}, f32[8,160]{1,0:T(8,128)S(1)}, bf16[160,512]{1,0:T(8,128)(2,1)S(1)}...) custom-call(s32[3]{0:T(128)S(1)} %pad_add_fusion.n_ref.refs_0_, ...), custom_call_target="tpu_custom_call" | custom-call | flops 1887436800 | tf_op jit(solution)/shard_map/pallas_call | solution.py:34
  52.6 1.1 collective-permute-done.14
  53.7 1.0 collective-permute-start.15
  54.7 0.9 fusion.1.refs_0_
  55.6 4.6 %collective-permute-start.32 = (bf16[1,80,640]{2,1,0:T(8,128)(2,1)S(1)}, bf16[1,80,640]{2,1,0:T(8,128)(2,1)S(1)}, u32[]{:S(2)}, u32[]{:S(2)}) collective-permute-start(bf16[1,80,640]{2,1,0:T(8,128)(2,1)S(1)} %fusion.1.refs_0_), channel_id=1, source_target_pairs={{0,1},{1,2},{2,3},{3,0},{4,5},{5,6},{6,7},{7,4},{8,9},{9,10},{10,1... | collective-permute-start | bytes 307208 | tf_op jit(solution)/shard_map/ppermute | solution.py:51
  60.2 1.4 collective-permute-start.33
  61.6 1.0 collective-permute-start.34
  62.6 0.7 collective-permute-start.16
  63.4 1.5 collective-permute-done.32.refs_1_
  64.9 3.8 %collective-permute-done.33.refs_2_ = bf16[1,80,640]{2,1,0:T(8,128)(2,1)S(1)} collective-permute-done((bf16[1,80,640]{2,1,0:T(8,128)(2,1)S(1)}, bf16[1,80,640]{2,1,0:T(8,128)(2,1)S(1)}, u32[]{:S(2)}, u32[]{:S(2)}) %collective-permute-start.33) | collective-permute-done | bytes 102432 | tf_op jit(solution)/shard_map/ppermute | solution.py:51
  68.6 0.6 shard_map.173.refs_0_
  69.2 1.0 collective-permute-start.35
  70.2 2.7 %collective-permute-start.11 = (bf16[160,512]{1,0:T(8,128)(2,1)S(1)}, bf16[160,512]{1,0:T(8,128)(2,1)S(1)}, u32[]{:S(2)}, u32[]{:S(2)}) collective-permute-start(bf16[160,512]{1,0:T(8,128)(2,1)S(1)} %get-tuple-element.25.refs_0_.refs_1_), channel_id=1, source_target_pairs={{0,1},{1,2},{2,3},{3,0},{4,5},{5,6},{6,7},{7,4},{8,9},{9,10},{10,1... | collective-permute-start | bytes 491528 | tf_op jit(solution)/shard_map/ppermute | solution.py:51
  72.8 1.5 collective-permute-start.12
  74.4 0.8 collective-permute-start.13
  75.4 1.3 collective-permute-start.17
  76.6 2.5 %collective-permute-done.11.refs_1_.refs_2_ = bf16[160,512]{1,0:T(8,128)(2,1)S(1)} collective-permute-done((bf16[160,512]{1,0:T(8,128)(2,1)S(1)}, bf16[160,512]{1,0:T(8,128)(2,1)S(1)}, u32[]{:S(2)}, u32[]{:S(2)}) %collective-permute-start.11) | collective-permute-done | bytes 163872 | tf_op jit(solution)/shard_map/ppermute | solution.py:51
  79.1 7.0 %collective-permute-done.12.refs_2_.refs_3_ = bf16[160,512]{1,0:T(8,128)(2,1)S(1)} collective-permute-done((bf16[160,512]{1,0:T(8,128)(2,1)S(1)}, bf16[160,512]{1,0:T(8,128)(2,1)S(1)}, u32[]{:S(2)}, u32[]{:S(2)}) %collective-permute-start.12) | collective-permute-done | bytes 163872 | tf_op jit(solution)/shard_map/ppermute | solution.py:51
  86.4 1.7 %collective-permute-start.20 = (bf16[640,256]{1,0:T(8,128)(2,1)S(1)}, bf16[640,256]{1,0:T(8,128)(2,1)S(1)}, u32[]{:S(2)}, u32[]{:S(2)}) collective-permute-start(bf16[640,256]{1,0:T(8,128)(2,1)S(1)} %get-tuple-element.29), channel_id=1, source_target_pairs={{0,4},{4,8},{8,12},{12,16},{16,20},{20,24},{24,28},{1,5},{5,9},{9,... | collective-permute-start | bytes 983048 | tf_op jit(solution)/shard_map/ppermute | solution.py:788
  88.2 1.3 collective-permute-start.21
  89.5 5.1 %collective-permute-start.36 = (bf16[4,80,640]{2,1,0:T(8,128)(2,1)S(1)}, bf16[4,80,640]{2,1,0:T(8,128)(2,1)S(1)}, u32[]{:S(2)}, u32[]{:S(2)}) collective-permute-start(bf16[4,80,640]{2,1,0:T(8,128)(2,1)S(1)} %shard_map.173.refs_0_), channel_id=1, source_target_pairs={{0,16},{4,20},{8,24},{12,28},{16,0},{20,4},{24,8},{28,12},{1,17},{... | collective-permute-start | bytes 1228808 | tf_op jit(solution)/shard_map/ppermute | solution.py:51
  94.5 6.0 %collective-permute-start.18 = (bf16[160,640]{1,0:T(8,128)(2,1)S(1)}, bf16[160,640]{1,0:T(8,128)(2,1)S(1)}, u32[]{:S(2)}, u32[]{:S(2)}) collective-permute-start(bf16[160,640]{1,0:T(8,128)(2,1)S(1)} %shard_map.168.refs_5_), channel_id=1, source_target_pairs={{0,2},{1,3},{2,0},{3,1},{4,6},{5,7},{6,4},{7,5},{8,10},{9,11},{10,... | collective-permute-start | bytes 614408 | tf_op jit(solution)/shard_map/ppermute | solution.py:51
  100.5 3.4 %collective-permute-start.19 = (bf16[160,640]{1,0:T(8,128)(2,1)S(1)}, bf16[160,640]{1,0:T(8,128)(2,1)S(1)}, u32[]{:S(2)}, u32[]{:S(2)}) collective-permute-start(bf16[160,640]{1,0:T(8,128)(2,1)S(1)} %shard_map.168.refs_5_), channel_id=1, source_target_pairs={{0,3},{1,0},{2,1},{3,2},{4,7},{5,4},{6,5},{7,6},{8,11},{9,8},{10,9... | collective-permute-start | bytes 614408 | tf_op jit(solution)/shard_map/ppermute | solution.py:51
  103.9 6.8 %collective-permute-done.18.refs_7_ = bf16[160,640]{1,0:T(8,128)(2,1)S(1)} collective-permute-done((bf16[160,640]{1,0:T(8,128)(2,1)S(1)}, bf16[160,640]{1,0:T(8,128)(2,1)S(1)}, u32[]{:S(2)}, u32[]{:S(2)}) %collective-permute-start.18) | collective-permute-done | bytes 204832 | tf_op jit(solution)/shard_map/ppermute | solution.py:51
  111.7 3.0 %shard_map.171 = (bf16[1,160,256]{2,1,0:T(8,128)(2,1)S(1)}, bf16[1,160,256]{2,1,0:T(8,128)(2,1)S(1)}) custom-call(s32[3]{0:T(128)S(1)} %pad_add_fusion.n_ref.refs_0_, bf16[160,512]{1,0:T(8,128)(2,1)S(1)} %get-tuple-element.25.refs_0_.refs_1_, bf16[160,512]{1,0:T(8,128)(2,1)S(1)} %collective-permute-done.11.refs_1_.refs_2_, ...), custom_call_target="tpu_custom_call" | custom-call | flops 1887436800 | tf_op jit(solution)/shard_map/pallas_call | solution.py:34
  114.7 1.4 collective-permute-start.23
  116.1 6.2 %collective-permute-start.24 = (bf16[1,160,256]{2,1,0:T(8,128)(2,1)S(1)}, bf16[1,160,256]{2,1,0:T(8,128)(2,1)S(1)}, u32[]{:S(2)}, u32[]{:S(2)}) collective-permute-start(bf16[1,160,256]{2,1,0:T(8,128)(2,1)S(1)} %get-tuple-element.36), channel_id=1, source_target_pairs={{0,1},{1,2},{2,3},{3,0},{4,5},{5,6},{6,7},{7,4},{8,9},{9,10},{10,1... | collective-permute-start | bytes 245768 | tf_op jit(solution)/shard_map/ppermute | solution.py:51
  122.3 3.1 %shard_map.170 = (bf16[1,160,256]{2,1,0:T(8,128)(2,1)S(1)}, bf16[1,160,256]{2,1,0:T(8,128)(2,1)S(1)}) custom-call(s32[3]{0:T(128)S(1)} %pad_add_fusion.n_ref.refs_0_, bf16[160,512]{1,0:T(8,128)(2,1)S(1)} %get-tuple-element.25.refs_0_.refs_1_, bf16[160,512]{1,0:T(8,128)(2,1)S(1)} %collective-permute-done.11.refs_1_.refs_2_, ...), custom_call_target="tpu_custom_call" | custom-call | flops 1887436800 | tf_op jit(solution)/shard_map/pallas_call | solution.py:34
  125.4 0.7 collective-permute-done.24.refs_3_
  126.1 2.0 %collective-permute-start.22 = (bf16[1,160,256]{2,1,0:T(8,128)(2,1)S(1)}, bf16[1,160,256]{2,1,0:T(8,128)(2,1)S(1)}, u32[]{:S(2)}, u32[]{:S(2)}) collective-permute-start(bf16[1,160,256]{2,1,0:T(8,128)(2,1)S(1)} %get-tuple-element.34), channel_id=1, source_target_pairs={{0,3},{1,0},{2,1},{3,2},{4,7},{5,4},{6,5},{7,6},{8,11},{9,8},{10,9... | collective-permute-start | bytes 245768 | tf_op jit(solution)/shard_map/ppermute | solution.py:51
  128.1 2.4 %collective-permute-done.22.refs_1_ = bf16[1,160,256]{2,1,0:T(8,128)(2,1)S(1)} collective-permute-done((bf16[1,160,256]{2,1,0:T(8,128)(2,1)S(1)}, bf16[1,160,256]{2,1,0:T(8,128)(2,1)S(1)}, u32[]{:S(2)}, u32[]{:S(2)}) %collective-permute-start.22) | collective-permute-done | bytes 81952 | tf_op jit(solution)/shard_map/ppermute | solution.py:51
  130.6 0.6 shard_map.172.refs_0_
  131.4 0.7 collective-permute-start.26
  132.1 2.4 %collective-permute-start.27 = (bf16[1,640,256]{2,1,0:T(8,128)(2,1)S(1)}, bf16[1,640,256]{2,1,0:T(8,128)(2,1)S(1)}, u32[]{:S(2)}, u32[]{:S(2)}) collective-permute-start(bf16[1,640,256]{2,1,0:T(8,128)(2,1)S(1)} %shard_map.172.refs_0_), channel_id=1, source_target_pairs={{0,24},{4,28},{8,0},{12,4},{16,8},{20,12},{24,16},{28,20},{1,25},{... | collective-permute-start | bytes 983048 | tf_op jit(solution)/shard_map/ppermute | solution.py:51
  135.0 7.7 %collective-permute-done.25.refs_1_ = bf16[1,640,256]{2,1,0:T(8,128)(2,1)S(1)} collective-permute-done((bf16[1,640,256]{2,1,0:T(8,128)(2,1)S(1)}, bf16[1,640,256]{2,1,0:T(8,128)(2,1)S(1)}, u32[]{:S(2)}, u32[]{:S(2)}) %collective-permute-start.25) | collective-permute-done | bytes 327712 | tf_op jit(solution)/shard_map/ppermute | solution.py:51
  142.7 4.3 %collective-permute-done.26.refs_2_ = bf16[1,640,256]{2,1,0:T(8,128)(2,1)S(1)} collective-permute-done((bf16[1,640,256]{2,1,0:T(8,128)(2,1)S(1)}, bf16[1,640,256]{2,1,0:T(8,128)(2,1)S(1)}, u32[]{:S(2)}, u32[]{:S(2)}) %collective-permute-start.26) | collective-permute-done | bytes 327712 | tf_op jit(solution)/shard_map/ppermute | solution.py:51
  147.0 0.5 collective-permute-start.31
  147.7 0.8 shard_map.174.refs_8_
  148.6 1.7 %copy-done = bf16[2560,640]{1,0:T(8,128)(2,1)} copy-done((bf16[2560,640]{1,0:T(8,128)(2,1)}, bf16[2560,640]{1,0:T(8,128)(2,1)S(1)}, u32[]{:S(2)}) %copy-start) | copy-done | bytes 3276824
  150.3 16.4 %shard_map.176 = bf16[1,4,64,640]{3,2,1,0:T(8,128)(2,1)} custom-call(bf16[1,640,256]{2,1,0:T(8,128)(2,1)S(1)} %shard_map.172.refs_0_, bf16[1,640,256]{2,1,0:T(8,128)(2,1)S(1)} %collective-permute-done.25.refs_1_, bf16[1,640,256]{2,1,0:T(8,128)(2,1)S(1)} %collective-permute-done.26.refs_2_, bf16[1,640,256]{2,1,0:T(8,128)(2,1)S(1)} %collective-permute-done.27.refs_3_, ...), custom_call_target="tpu_custom_call" | custom-call | tf_op jit(solution)/shard_map/pallas_call | solution.py:34
  (79 shorter events, 3.0 us)
Async XLA Ops:
  0.0 35.4 %copy-start.2 = (f32[320,1280]{1,0:T(8,128)S(1)}, f32[320,1280]{1,0:T(8,128)}, u32[]{:S(2)}) copy-start(f32[320,1280]{1,0:T(8,128)} %w_ref.1) | copy-start | bytes 4915204
  0.0 1.1 copy-start.3
  1.1 0.9 copy-start.5
  2.7 1.4 collective-permute-start.3
  4.2 8.4 %collective-permute-start.4 = (f32[2,640]{1,0:T(2,128)S(1)}, f32[2,640]{1,0:T(2,128)S(1)}, u32[]{:S(2)}, u32[]{:S(2)}) collective-permute-start(f32[2,640]{1,0:T(2,128)S(1)} %pad_maximum_fusion.3), channel_id=1, source_target_pairs={{0,8},{4,12},{8,0},{12,4},{16,24},{20,28},{24,16},{28,20},{1,9},{5... | collective-permute-start | bytes 15368 | tf_op jit(solution)/shard_map/ppermute | solution.py:673
  7.0 9.0 %collective-permute-start = (bf16[1,128,640]{2,1,0:T(8,128)(2,1)S(1)}, bf16[1,128,640]{2,1,0:T(8,128)(2,1)S(1)}, u32[]{:S(2)}, u32[]{:S(2)}) collective-permute-start(bf16[1,128,640]{2,1,0:T(8,128)(2,1)S(1)} %get-tuple-element.21.refs_0_.refs_1_), channel_id=1, source_target_pairs={{0,1},{1,2},{2,3},{3,0},{4,5},{5,6},{6,7},{7,4},{8,9},{9,10},{10,1... | collective-permute-start | bytes 491528 | tf_op jit(solution)/shard_map/ppermute | solution.py:51
  8.6 13.4 %collective-permute-start.1 = (bf16[1,128,640]{2,1,0:T(8,128)(2,1)S(1)}, bf16[1,128,640]{2,1,0:T(8,128)(2,1)S(1)}, u32[]{:S(2)}, u32[]{:S(2)}) collective-permute-start(bf16[1,128,640]{2,1,0:T(8,128)(2,1)S(1)} %get-tuple-element.21.refs_0_.refs_1_), channel_id=1, source_target_pairs={{0,2},{1,3},{2,0},{3,1},{4,6},{5,7},{6,4},{7,5},{8,10},{9,11},{10,... | collective-permute-start | bytes 491528 | tf_op jit(solution)/shard_map/ppermute | solution.py:51
  11.2 10.8 %collective-permute-start.2 = (bf16[1,128,640]{2,1,0:T(8,128)(2,1)S(1)}, bf16[1,128,640]{2,1,0:T(8,128)(2,1)S(1)}, u32[]{:S(2)}, u32[]{:S(2)}) collective-permute-start(bf16[1,128,640]{2,1,0:T(8,128)(2,1)S(1)} %get-tuple-element.21.refs_0_.refs_1_), channel_id=1, source_target_pairs={{0,3},{1,0},{2,1},{3,2},{4,7},{5,4},{6,5},{7,6},{8,11},{9,8},{10,9... | collective-permute-start | bytes 491528 | tf_op jit(solution)/shard_map/ppermute | solution.py:51
  12.6 14.5 %collective-permute-start.5 = (f32[2,640]{1,0:T(2,128)S(1)}, f32[2,640]{1,0:T(2,128)S(1)}, u32[]{:S(2)}, u32[]{:S(2)}) collective-permute-start(f32[2,640]{1,0:T(2,128)S(1)} %pad_maximum_fusion.4), channel_id=1, source_target_pairs={{0,16},{4,20},{8,24},{12,28},{16,0},{20,4},{24,8},{28,12},{1,17},{... | collective-permute-start | bytes 15368 | tf_op jit(solution)/shard_map/ppermute | solution.py:673
  22.8 23.6 %collective-permute-start.10 = (bf16[4,64,640]{2,1,0:T(8,128)(2,1)}, bf16[4,64,640]{2,1,0:T(8,128)(2,1)S(1)}, u32[]{:S(2)}, u32[]{:S(2)}) collective-permute-start(bf16[4,64,640]{2,1,0:T(8,128)(2,1)} %get-tuple-element.24), channel_id=1, source_target_pairs={{4,0},{8,4},{12,8},{16,12},{20,16},{24,20},{28,24},{5,1},{9,5},{13... | collective-permute-start | bytes 983048 | tf_op jit(solution)/shard_map/ppermute | solution.py:788
  24.1 22.3 %collective-permute-start.9 = (bf16[4,64,640]{2,1,0:T(8,128)(2,1)S(1)}, bf16[4,64,640]{2,1,0:T(8,128)(2,1)S(1)}, u32[]{:S(2)}, u32[]{:S(2)}) collective-permute-start(bf16[4,64,640]{2,1,0:T(8,128)(2,1)S(1)} %get-tuple-element.23), channel_id=1, source_target_pairs={{0,4},{4,8},{8,12},{12,16},{16,20},{20,24},{24,28},{1,5},{5,9},{9,... | collective-permute-start | bytes 983048 | tf_op jit(solution)/shard_map/ppermute | solution.py:788
  27.2 1.0 copy-start.4
  28.2 11.6 %collective-permute-start.6 = (bf16[1,144,640]{2,1,0:T(8,128)(2,1)S(1)}, bf16[1,144,640]{2,1,0:T(8,128)(2,1)}, u32[]{:S(2)}, u32[]{:S(2)}) collective-permute-start(bf16[1,144,640]{2,1,0:T(8,128)(2,1)S(1)} %shard_map.164.refs_5_), channel_id=1, source_target_pairs={{0,1},{1,2},{2,3},{3,0},{4,5},{5,6},{6,7},{7,4},{8,9},{9,10},{10,1... | collective-permute-start | bytes 552968 | tf_op jit(solution)/shard_map/ppermute | solution.py:51
  32.2 14.2 %collective-permute-start.7 = (bf16[1,144,640]{2,1,0:T(8,128)(2,1)S(1)}, bf16[1,144,640]{2,1,0:T(8,128)(2,1)}, u32[]{:S(2)}, u32[]{:S(2)}) collective-permute-start(bf16[1,144,640]{2,1,0:T(8,128)(2,1)S(1)} %shard_map.164.refs_5_), channel_id=1, source_target_pairs={{0,2},{1,3},{2,0},{3,1},{4,6},{5,7},{6,4},{7,5},{8,10},{9,11},{10,... | collective-permute-start | bytes 552968 | tf_op jit(solution)/shard_map/ppermute | solution.py:51
  33.9 12.5 %collective-permute-start.8 = (bf16[1,144,640]{2,1,0:T(8,128)(2,1)S(1)}, bf16[1,144,640]{2,1,0:T(8,128)(2,1)}, u32[]{:S(2)}, u32[]{:S(2)}) collective-permute-start(bf16[1,144,640]{2,1,0:T(8,128)(2,1)S(1)} %shard_map.164.refs_5_), channel_id=1, source_target_pairs={{0,3},{1,0},{2,1},{3,2},{4,7},{5,4},{6,5},{7,6},{8,11},{9,8},{10,9... | collective-permute-start | bytes 552968 | tf_op jit(solution)/shard_map/ppermute | solution.py:51
  35.4 1.9 %copy-start.1 = (f32[1280,640]{1,0:T(8,128)S(1)}, f32[1280,640]{1,0:T(8,128)}, u32[]{:S(2)}) copy-start(f32[1280,640]{1,0:T(8,128)} %t_ref.1) | copy-start | bytes 9830404
  37.3 0.7 copy-start.8
  38.0 8.4 %copy-start.9 = (bf16[5760,160]{0,1:T(8,128)(2,1)S(1)}, bf16[5760,160]{0,1:T(8,128)(2,1)}, u32[]{:S(2)}) copy-start(bf16[5760,160]{0,1:T(8,128)(2,1)} %param.23) | copy-start | bytes 5529604
  38.0 8.4 %copy-start.11 = (f32[160,160]{1,0:T(8,128)S(1)}, f32[160,160]{1,0:T(8,128)}, u32[]{:S(2)}) copy-start(f32[160,160]{1,0:T(8,128)} %constant.73.clone.refs_13_) | copy-start | bytes 307204
  38.0 8.4 %copy-start.12 = (f32[8,128]{1,0:T(8,128)S(1)}, f32[8,128]{1,0:T(8,128)}, u32[]{:S(2)}) copy-start(f32[8,128]{1,0:T(8,128)} %constant.74.clone.refs_15_) | copy-start | bytes 12292
  52.5 59.2 %copy-start.10 = (bf16[5760,160]{0,1:T(8,128)(2,1)S(1)}, bf16[5760,160]{0,1:T(8,128)(2,1)}, u32[]{:S(2)}) copy-start(bf16[5760,160]{0,1:T(8,128)(2,1)} %param.24) | copy-start | bytes 5529604
  52.5 1.2 collective-permute-start.14
  53.7 8.9 %collective-permute-start.15 = (f32[8,160]{1,0:T(8,128)S(1)}, f32[8,160]{1,0:T(8,128)S(1)}, u32[]{:S(2)}, u32[]{:S(2)}) collective-permute-start(f32[8,160]{1,0:T(8,128)S(1)} %pad_maximum_fusion), channel_id=1, source_target_pairs={{0,8},{4,12},{8,0},{12,4},{16,24},{20,28},{24,16},{28,20},{1,9},{5... | collective-permute-start | bytes 15368 | tf_op jit(solution)/shard_map/ppermute | solution.py:673
  55.6 9.2 %collective-permute-start.32 = (bf16[1,80,640]{2,1,0:T(8,128)(2,1)S(1)}, bf16[1,80,640]{2,1,0:T(8,128)(2,1)S(1)}, u32[]{:S(2)}, u32[]{:S(2)}) collective-permute-start(bf16[1,80,640]{2,1,0:T(8,128)(2,1)S(1)} %fusion.1.refs_0_), channel_id=1, source_target_pairs={{0,1},{1,2},{2,3},{3,0},{4,5},{5,6},{6,7},{7,4},{8,9},{9,10},{10,1... | collective-permute-start | bytes 307208 | tf_op jit(solution)/shard_map/ppermute | solution.py:51
  60.2 8.5 %collective-permute-start.33 = (bf16[1,80,640]{2,1,0:T(8,128)(2,1)S(1)}, bf16[1,80,640]{2,1,0:T(8,128)(2,1)S(1)}, u32[]{:S(2)}, u32[]{:S(2)}) collective-permute-start(bf16[1,80,640]{2,1,0:T(8,128)(2,1)S(1)} %fusion.1.refs_0_), channel_id=1, source_target_pairs={{0,2},{1,3},{2,0},{3,1},{4,6},{5,7},{6,4},{7,5},{8,10},{9,11},{10,... | collective-permute-start | bytes 307208 | tf_op jit(solution)/shard_map/ppermute | solution.py:51
  61.6 7.0 %collective-permute-start.34 = (bf16[1,80,640]{2,1,0:T(8,128)(2,1)S(1)}, bf16[1,80,640]{2,1,0:T(8,128)(2,1)S(1)}, u32[]{:S(2)}, u32[]{:S(2)}) collective-permute-start(bf16[1,80,640]{2,1,0:T(8,128)(2,1)S(1)} %fusion.1.refs_0_), channel_id=1, source_target_pairs={{0,3},{1,0},{2,1},{3,2},{4,7},{5,4},{6,5},{7,6},{8,11},{9,8},{10,9... | collective-permute-start | bytes 307208 | tf_op jit(solution)/shard_map/ppermute | solution.py:51
  62.6 12.6 %collective-permute-start.16 = (f32[8,160]{1,0:T(8,128)S(1)}, f32[8,160]{1,0:T(8,128)S(1)}, u32[]{:S(2)}, u32[]{:S(2)}) collective-permute-start(f32[8,160]{1,0:T(8,128)S(1)} %pad_maximum_fusion.1), channel_id=1, source_target_pairs={{0,16},{4,20},{8,24},{12,28},{16,0},{20,4},{24,8},{28,12},{1,17},{... | collective-permute-start | bytes 15368 | tf_op jit(solution)/shard_map/ppermute | solution.py:673
  69.2 25.3 %collective-permute-start.35 = (bf16[4,80,640]{2,1,0:T(8,128)(2,1)S(1)}, bf16[4,80,640]{2,1,0:T(8,128)(2,1)S(1)}, u32[]{:S(2)}, u32[]{:S(2)}) collective-permute-start(bf16[4,80,640]{2,1,0:T(8,128)(2,1)S(1)} %shard_map.173.refs_0_), channel_id=1, source_target_pairs={{0,8},{4,12},{8,16},{12,20},{16,24},{20,28},{24,0},{28,4},{1,9},{5... | collective-permute-start | bytes 1228808 | tf_op jit(solution)/shard_map/ppermute | solution.py:51
  70.2 9.0 %collective-permute-start.11 = (bf16[160,512]{1,0:T(8,128)(2,1)S(1)}, bf16[160,512]{1,0:T(8,128)(2,1)S(1)}, u32[]{:S(2)}, u32[]{:S(2)}) collective-permute-start(bf16[160,512]{1,0:T(8,128)(2,1)S(1)} %get-tuple-element.25.refs_0_.refs_1_), channel_id=1, source_target_pairs={{0,1},{1,2},{2,3},{3,0},{4,5},{5,6},{6,7},{7,4},{8,9},{9,10},{10,1... | collective-permute-start | bytes 491528 | tf_op jit(solution)/shard_map/ppermute | solution.py:51
  72.8 13.3 %collective-permute-start.12 = (bf16[160,512]{1,0:T(8,128)(2,1)S(1)}, bf16[160,512]{1,0:T(8,128)(2,1)S(1)}, u32[]{:S(2)}, u32[]{:S(2)}) collective-permute-start(bf16[160,512]{1,0:T(8,128)(2,1)S(1)} %get-tuple-element.25.refs_0_.refs_1_), channel_id=1, source_target_pairs={{0,2},{1,3},{2,0},{3,1},{4,6},{5,7},{6,4},{7,5},{8,10},{9,11},{10,... | collective-permute-start | bytes 491528 | tf_op jit(solution)/shard_map/ppermute | solution.py:51
  74.4 11.8 %collective-permute-start.13 = (bf16[160,512]{1,0:T(8,128)(2,1)S(1)}, bf16[160,512]{1,0:T(8,128)(2,1)S(1)}, u32[]{:S(2)}, u32[]{:S(2)}) collective-permute-start(bf16[160,512]{1,0:T(8,128)(2,1)S(1)} %get-tuple-element.25.refs_0_.refs_1_), channel_id=1, source_target_pairs={{0,3},{1,0},{2,1},{3,2},{4,7},{5,4},{6,5},{7,6},{8,11},{9,8},{10,9... | collective-permute-start | bytes 491528 | tf_op jit(solution)/shard_map/ppermute | solution.py:51
  75.4 25.1 %collective-permute-start.17 = (bf16[160,640]{1,0:T(8,128)(2,1)S(1)}, bf16[160,640]{1,0:T(8,128)(2,1)S(1)}, u32[]{:S(2)}, u32[]{:S(2)}) collective-permute-start(bf16[160,640]{1,0:T(8,128)(2,1)S(1)} %shard_map.168.refs_5_), channel_id=1, source_target_pairs={{0,1},{1,2},{2,3},{3,0},{4,5},{5,6},{6,7},{7,4},{8,9},{9,10},{10,1... | collective-permute-start | bytes 614408 | tf_op jit(solution)/shard_map/ppermute | solution.py:51
  86.4 24.7 %collective-permute-start.20 = (bf16[640,256]{1,0:T(8,128)(2,1)S(1)}, bf16[640,256]{1,0:T(8,128)(2,1)S(1)}, u32[]{:S(2)}, u32[]{:S(2)}) collective-permute-start(bf16[640,256]{1,0:T(8,128)(2,1)S(1)} %get-tuple-element.29), channel_id=1, source_target_pairs={{0,4},{4,8},{8,12},{12,16},{16,20},{20,24},{24,28},{1,5},{5,9},{9,... | collective-permute-start | bytes 983048 | tf_op jit(solution)/shard_map/ppermute | solution.py:788
  88.2 23.5 %collective-permute-start.21 = (bf16[640,256]{1,0:T(8,128)(2,1)S(1)}, bf16[640,256]{1,0:T(8,128)(2,1)S(1)}, u32[]{:S(2)}, u32[]{:S(2)}) collective-permute-start(bf16[640,256]{1,0:T(8,128)(2,1)S(1)} %get-tuple-element.30), channel_id=1, source_target_pairs={{4,0},{8,4},{12,8},{16,12},{20,16},{24,20},{28,24},{5,1},{9,5},{13... | collective-permute-start | bytes 983048 | tf_op jit(solution)/shard_map/ppermute | solution.py:788
  89.5 26.6 %collective-permute-start.36 = (bf16[4,80,640]{2,1,0:T(8,128)(2,1)S(1)}, bf16[4,80,640]{2,1,0:T(8,128)(2,1)S(1)}, u32[]{:S(2)}, u32[]{:S(2)}) collective-permute-start(bf16[4,80,640]{2,1,0:T(8,128)(2,1)S(1)} %shard_map.173.refs_0_), channel_id=1, source_target_pairs={{0,16},{4,20},{8,24},{12,28},{16,0},{20,4},{24,8},{28,12},{1,17},{... | collective-permute-start | bytes 1228808 | tf_op jit(solution)/shard_map/ppermute | solution.py:51
  94.5 16.2 %collective-permute-start.18 = (bf16[160,640]{1,0:T(8,128)(2,1)S(1)}, bf16[160,640]{1,0:T(8,128)(2,1)S(1)}, u32[]{:S(2)}, u32[]{:S(2)}) collective-permute-start(bf16[160,640]{1,0:T(8,128)(2,1)S(1)} %shard_map.168.refs_5_), channel_id=1, source_target_pairs={{0,2},{1,3},{2,0},{3,1},{4,6},{5,7},{6,4},{7,5},{8,10},{9,11},{10,... | collective-permute-start | bytes 614408 | tf_op jit(solution)/shard_map/ppermute | solution.py:51
  100.5 10.6 %collective-permute-start.19 = (bf16[160,640]{1,0:T(8,128)(2,1)S(1)}, bf16[160,640]{1,0:T(8,128)(2,1)S(1)}, u32[]{:S(2)}, u32[]{:S(2)}) collective-permute-start(bf16[160,640]{1,0:T(8,128)(2,1)S(1)} %shard_map.168.refs_5_), channel_id=1, source_target_pairs={{0,3},{1,0},{2,1},{3,2},{4,7},{5,4},{6,5},{7,6},{8,11},{9,8},{10,9... | collective-permute-start | bytes 614408 | tf_op jit(solution)/shard_map/ppermute | solution.py:51
  110.7 20.7 %collective-permute-start.37 = (bf16[4,80,640]{2,1,0:T(8,128)(2,1)S(1)}, bf16[4,80,640]{2,1,0:T(8,128)(2,1)S(1)}, u32[]{:S(2)}, u32[]{:S(2)}) collective-permute-start(bf16[4,80,640]{2,1,0:T(8,128)(2,1)S(1)} %shard_map.173.refs_0_), channel_id=1, source_target_pairs={{0,24},{4,28},{8,0},{12,4},{16,8},{20,12},{24,16},{28,20},{1,25},{... | collective-permute-start | bytes 1228808 | tf_op jit(solution)/shard_map/ppermute | solution.py:51
  111.1 20.9 %collective-permute-start.38 = (bf16[4,80,640]{2,1,0:T(8,128)(2,1)S(1)}, bf16[4,80,640]{2,1,0:T(8,128)(2,1)S(1)}, u32[]{:S(2)}, u32[]{:S(2)}) collective-permute-start(bf16[4,80,640]{2,1,0:T(8,128)(2,1)S(1)} %shard_map.173.refs_0_), channel_id=1, source_target_pairs={{0,4},{4,0},{8,12},{12,8},{16,20},{20,16},{24,28},{28,24},{1,5},{5... | collective-permute-start | bytes 1228808 | tf_op jit(solution)/shard_map/ppermute | solution.py:683
  111.1 23.4 %collective-permute-start.39 = (bf16[4,80,640]{2,1,0:T(8,128)(2,1)S(1)}, bf16[4,80,640]{2,1,0:T(8,128)(2,1)S(1)}, u32[]{:S(2)}, u32[]{:S(2)}) collective-permute-start(bf16[4,80,640]{2,1,0:T(8,128)(2,1)S(1)} %collective-permute-done.35.refs_1_), channel_id=1, source_target_pairs={{0,4},{4,0},{8,12},{12,8},{16,20},{20,16},{24,28},{28,24},{1,5},{5... | collective-permute-start | bytes 1228808 | tf_op jit(solution)/shard_map/ppermute | solution.py:683
  114.7 10.6 %collective-permute-start.23 = (bf16[1,160,256]{2,1,0:T(8,128)(2,1)S(1)}, bf16[1,160,256]{2,1,0:T(8,128)(2,1)S(1)}, u32[]{:S(2)}, u32[]{:S(2)}) collective-permute-start(bf16[1,160,256]{2,1,0:T(8,128)(2,1)S(1)} %get-tuple-element.35), channel_id=1, source_target_pairs={{0,2},{1,3},{2,0},{3,1},{4,6},{5,7},{6,4},{7,5},{8,10},{9,11},{10,... | collective-permute-start | bytes 245768 | tf_op jit(solution)/shard_map/ppermute | solution.py:51
  116.1 10.1 %collective-permute-start.24 = (bf16[1,160,256]{2,1,0:T(8,128)(2,1)S(1)}, bf16[1,160,256]{2,1,0:T(8,128)(2,1)S(1)}, u32[]{:S(2)}, u32[]{:S(2)}) collective-permute-start(bf16[1,160,256]{2,1,0:T(8,128)(2,1)S(1)} %get-tuple-element.36), channel_id=1, source_target_pairs={{0,1},{1,2},{2,3},{3,0},{4,5},{5,6},{6,7},{7,4},{8,9},{9,10},{10,1... | collective-permute-start | bytes 245768 | tf_op jit(solution)/shard_map/ppermute | solution.py:51
  125.3 9.2 %collective-permute-start.40 = (bf16[4,80,640]{2,1,0:T(8,128)(2,1)S(1)}, bf16[4,80,640]{2,1,0:T(8,128)(2,1)S(1)}, u32[]{:S(2)}, u32[]{:S(2)}) collective-permute-start(bf16[4,80,640]{2,1,0:T(8,128)(2,1)S(1)} %collective-permute-done.36.refs_2_), channel_id=1, source_target_pairs={{0,4},{4,0},{8,12},{12,8},{16,20},{20,16},{24,28},{28,24},{1,5},{5... | collective-permute-start | bytes 1228808 | tf_op jit(solution)/shard_map/ppermute | solution.py:683
  126.1 4.4 %collective-permute-start.22 = (bf16[1,160,256]{2,1,0:T(8,128)(2,1)S(1)}, bf16[1,160,256]{2,1,0:T(8,128)(2,1)S(1)}, u32[]{:S(2)}, u32[]{:S(2)}) collective-permute-start(bf16[1,160,256]{2,1,0:T(8,128)(2,1)S(1)} %get-tuple-element.34), channel_id=1, source_target_pairs={{0,3},{1,0},{2,1},{3,2},{4,7},{5,4},{6,5},{7,6},{8,11},{9,8},{10,9... | collective-permute-start | bytes 245768 | tf_op jit(solution)/shard_map/ppermute | solution.py:51
  131.2 11.5 %collective-permute-start.25 = (bf16[1,640,256]{2,1,0:T(8,128)(2,1)S(1)}, bf16[1,640,256]{2,1,0:T(8,128)(2,1)S(1)}, u32[]{:S(2)}, u32[]{:S(2)}) collective-permute-start(bf16[1,640,256]{2,1,0:T(8,128)(2,1)S(1)} %shard_map.172.refs_0_), channel_id=1, source_target_pairs={{0,8},{4,12},{8,16},{12,20},{16,24},{20,28},{24,0},{28,4},{1,9},{5... | collective-permute-start | bytes 983048 | tf_op jit(solution)/shard_map/ppermute | solution.py:51
  131.4 15.6 %collective-permute-start.26 = (bf16[1,640,256]{2,1,0:T(8,128)(2,1)S(1)}, bf16[1,640,256]{2,1,0:T(8,128)(2,1)S(1)}, u32[]{:S(2)}, u32[]{:S(2)}) collective-permute-start(bf16[1,640,256]{2,1,0:T(8,128)(2,1)S(1)} %shard_map.172.refs_0_), channel_id=1, source_target_pairs={{0,16},{4,20},{8,24},{12,28},{16,0},{20,4},{24,8},{28,12},{1,17},{... | collective-permute-start | bytes 983048 | tf_op jit(solution)/shard_map/ppermute | solution.py:51
  132.1 14.9 %collective-permute-start.27 = (bf16[1,640,256]{2,1,0:T(8,128)(2,1)S(1)}, bf16[1,640,256]{2,1,0:T(8,128)(2,1)S(1)}, u32[]{:S(2)}, u32[]{:S(2)}) collective-permute-start(bf16[1,640,256]{2,1,0:T(8,128)(2,1)S(1)} %shard_map.172.refs_0_), channel_id=1, source_target_pairs={{0,24},{4,28},{8,0},{12,4},{16,8},{20,12},{24,16},{28,20},{1,25},{... | collective-permute-start | bytes 983048 | tf_op jit(solution)/shard_map/ppermute | solution.py:51
  134.5 13.2 %collective-permute-start.41 = (bf16[4,80,640]{2,1,0:T(8,128)(2,1)S(1)}, bf16[4,80,640]{2,1,0:T(8,128)(2,1)S(1)}, u32[]{:S(2)}, u32[]{:S(2)}) collective-permute-start(bf16[4,80,640]{2,1,0:T(8,128)(2,1)S(1)} %collective-permute-done.37.refs_3_), channel_id=1, source_target_pairs={{0,4},{4,0},{8,12},{12,8},{16,20},{20,16},{24,28},{28,24},{1,5},{5... | collective-permute-start | bytes 1228808 | tf_op jit(solution)/shard_map/ppermute | solution.py:683
  134.5 15.7 %collective-permute-start.28 = (bf16[1,640,256]{2,1,0:T(8,128)(2,1)S(1)}, bf16[1,640,256]{2,1,0:T(8,128)(2,1)S(1)}, u32[]{:S(2)}, u32[]{:S(2)}) collective-permute-start(bf16[1,640,256]{2,1,0:T(8,128)(2,1)S(1)} %shard_map.172.refs_0_), channel_id=1, source_target_pairs={{0,4},{4,0},{8,12},{12,8},{16,20},{20,16},{24,28},{28,24},{1,5},{5... | collective-permute-start | bytes 983048 | tf_op jit(solution)/shard_map/ppermute | solution.py:683
  142.7 7.6 %collective-permute-start.29 = (bf16[1,640,256]{2,1,0:T(8,128)(2,1)S(1)}, bf16[1,640,256]{2,1,0:T(8,128)(2,1)S(1)}, u32[]{:S(2)}, u32[]{:S(2)}) collective-permute-start(bf16[1,640,256]{2,1,0:T(8,128)(2,1)S(1)} %collective-permute-done.25.refs_1_), channel_id=1, source_target_pairs={{0,4},{4,0},{8,12},{12,8},{16,20},{20,16},{24,28},{28,24},{1,5},{5... | collective-permute-start | bytes 983048 | tf_op jit(solution)/shard_map/ppermute | solution.py:683
  147.0 3.3 %collective-permute-start.30 = (bf16[1,640,256]{2,1,0:T(8,128)(2,1)S(1)}, bf16[1,640,256]{2,1,0:T(8,128)(2,1)S(1)}, u32[]{:S(2)}, u32[]{:S(2)}) collective-permute-start(bf16[1,640,256]{2,1,0:T(8,128)(2,1)S(1)} %collective-permute-done.26.refs_2_), channel_id=1, source_target_pairs={{0,4},{4,0},{8,12},{12,8},{16,20},{20,16},{24,28},{28,24},{1,5},{5... | collective-permute-start | bytes 983048 | tf_op jit(solution)/shard_map/ppermute | solution.py:683
  147.0 3.3 %collective-permute-start.31 = (bf16[1,640,256]{2,1,0:T(8,128)(2,1)S(1)}, bf16[1,640,256]{2,1,0:T(8,128)(2,1)S(1)}, u32[]{:S(2)}, u32[]{:S(2)}) collective-permute-start(bf16[1,640,256]{2,1,0:T(8,128)(2,1)S(1)} %collective-permute-done.27.refs_3_), channel_id=1, source_target_pairs={{0,4},{4,0},{8,12},{12,8},{16,20},{20,16},{24,28},{28,24},{1,5},{5... | collective-permute-start | bytes 983048 | tf_op jit(solution)/shard_map/ppermute | solution.py:683
  147.7 2.5 %copy-start.6 = (bf16[640,128]{1,0:T(8,128)(2,1)S(1)}, bf16[640,128]{1,0:T(8,128)(2,1)}, u32[]{:S(2)}) copy-start(bf16[640,128]{1,0:T(8,128)(2,1)} %constant.71.clone.g_ref.refs_11_) | copy-start | bytes 491524
  147.7 2.5 %copy-start.7 = (bf16[128,640]{1,0:T(8,128)(2,1)S(1)}, bf16[128,640]{1,0:T(8,128)(2,1)}, u32[]{:S(2)}) copy-start(bf16[128,640]{1,0:T(8,128)(2,1)} %constant.76.refs_10_) | copy-start | bytes 491524
  148.6 1.7 %copy-start = (bf16[2560,640]{1,0:T(8,128)(2,1)}, bf16[2560,640]{1,0:T(8,128)(2,1)S(1)}, u32[]{:S(2)}) copy-start(bf16[2560,640]{1,0:T(8,128)(2,1)S(1)} %shard_map.174.refs_8_) | copy-start | bytes 9830404

commit v4 on v3

--- a/solution.py
+++ b/solution.py
@@ -19,13 +19,15 @@
 NT = (((1,), (1,)), ((), ()))
 
 
-def call(body, out_shape, scratch=(), scalars=0, flops=0, near=(), limit=16):
+def call(body, out_shape, scratch=(), scalars=0, flops=0, near=(), far=(), limit=16):
     def run(*operands):
         near_ones = set(range(len(operands))) if near is True else set(near)
         placed = [
             pltpu.with_memory_space_constraint(x, pltpu.VMEM) if i in near_ones and i >= scalars else x
             for i, x in enumerate(operands)
         ]
+        for i in far:
+            placed[i] = pltpu.with_memory_space_constraint(placed[i], pltpu.HBM)
         specs = [
             pl.BlockSpec(memory_space=pltpu.SMEM if i < scalars else pltpu.VMEM)
             for i in range(len(operands))
@@ -107,7 +109,8 @@
         )
         o_ref[...] = jnp.broadcast_to(jnp.sum(parts, axis=1, keepdims=True), (rows, LANES))
 
-    return call(body, jax.ShapeDtypeStruct((rows, LANES), jnp.float32), scalars=2)(
+    shape = jax.ShapeDtypeStruct((rows, LANES), jnp.float32)
+    return call(body, shape, scalars=2, far=(3, 4))(
         ends, step_index, roster[None, :], time_weight, temb_weight
     )
 
@@ -144,13 +147,11 @@
     return row
 
 
-def local_stats(features, member, width, columns):
+def local_stats(features, member, width):
     samples, length, channels = features.shape
 
-    def body(x_ref, g_ref, o_ref, e_ref):
+    def body(x_ref, g_ref, o_ref):
         for i in range(samples):
-            e_ref[i, :columns] = x_ref[i, :columns]
-            e_ref[i, columns:] = x_ref[i, length - columns :]
             v = x_ref[i].astype(jnp.float32)
             mean = group_sums(jnp.sum(v, axis=0, keepdims=True), g_ref[...]) / (length * width)
             c = v - mean
@@ -159,11 +160,7 @@
                 jnp.sum(c * c, axis=0, keepdims=True), g_ref[...]
             )
 
-    shapes = (
-        jax.ShapeDtypeStruct((2 * samples, channels), jnp.float32),
-        jax.ShapeDtypeStruct((samples, 2 * columns, channels), jnp.bfloat16),
-    )
-    return call(body, shapes)(features, member)
+    return call(body, jax.ShapeDtypeStruct((2 * samples, channels), jnp.float32))(features, member)
 
 
 def place_weights(where, pieces, wide, channels):
@@ -685,8 +682,8 @@
         return near + far, jnp.concatenate([back, back ^ 1]).astype(jnp.int32)
 
     flat = features.reshape(samples, length, channels)
-    own_stats, edges = local_stats(flat, members(channels, channels, channels, group), group, width)
-    edges = ring(edges)
+    edges = ring(jnp.concatenate([flat[:, :width], flat[:, length - width :]], axis=1))
+    own_stats = local_stats(flat, members(channels, channels, channels, group), group)
     last, first = halo_rows(edges, width)
     above = shift_rows(last, 1)
     below = shift_rows(first, -1)

time: 167 us -> 165 us (0.988)
  local copies, waits for them, and re-layouts: 8.08 us -> 4.45 us
    unnamed x26 -> x24, local copies, waits for them, and re-layouts: 7.26 us -> 3.61 us
  transfers between devices with their start and end apart: 42 -> 42, of which waited for: 14 -> 14; matrix products, arithmetic and copies ran while one was open for 1% -> 1% of each run, Pallas kernels for 7% -> 8%
where the time goes in v4:
time: 165 us; the launch traced here: 164 us
  starting transfers between devices  69.4 us (42%)
  waiting for transfers between devices  53 us (32%)
  Pallas kernels  35.1 us (21%)
  local copies, waits for them, and re-layouts  4.45 us (3%)
    ppermute x24, starting transfers between devices, shift(): lax.ppermute(values, axis, [(i, (i + step) % count) for i in range(count)])  53.6 us
    ppermute x24, waiting for transfers between devices, shift(): lax.ppermute(values, axis, [(i, (i + step) % count) for i in range(count)])  51.1 us
    pallas_call x14, Pallas kernels, run(): pl.pallas_call(body, out_shape=out_shape, in_specs=specs, out_specs=outs,...  35.1 us
    ppermute x4, starting transfers between devices, shift_rows(): return lax.ppermute(values, 'spatial', pairs)  7.33 us
    ppermute x6, starting transfers between devices, in_plane_stats(): lax.ppermute(values, 'spatial', [(i, i ^ size) for i in range(planes)])  6.86 us
    unnamed x24, local copies, waits for them, and re-layouts  3.61 us
  transfers between devices with their start and end apart: 42, of which 14 were waited for; matrix products, arithmetic and copies ran while one was open for 1% of the time, Pallas kernels for 8%

profile of v4, /device:TPU:0, one launch (start us, length us, event | category | flops | bytes accessed | tf_op | source)
XLA Modules:
  0.0 164.2 jit_solution(8576414905987634585)
XLA Ops:
  0.0 1.0 copy-done.1
  1.0 0.9 copy-done.3
  1.9 0.7 shard_map.163
  2.6 0.6 collective-permute-start.3
  3.2 0.8 collective-permute-done.3
  4.1 2.9 %collective-permute-start.4 = (f32[2,640]{1,0:T(2,128)S(1)}, f32[2,640]{1,0:T(2,128)S(1)}, u32[]{:S(2)}, u32[]{:S(2)}) collective-permute-start(f32[2,640]{1,0:T(2,128)S(1)} %pad_maximum_fusion.4), channel_id=1, source_target_pairs={{0,8},{4,12},{8,0},{12,4},{16,24},{20,28},{24,16},{28,20},{1,9},{5... | collective-permute-start | bytes 15368 | tf_op jit(solution)/shard_map/ppermute | solution.py:670
  7.0 1.6 collective-permute-start
  8.6 2.6 %collective-permute-start.1 = (bf16[1,128,640]{2,1,0:T(8,128)(2,1)S(1)}, bf16[1,128,640]{2,1,0:T(8,128)(2,1)S(1)}, u32[]{:S(2)}, u32[]{:S(2)}) collective-permute-start(bf16[1,128,640]{2,1,0:T(8,128)(2,1)S(1)} %pad_maximum_fusion.refs_0_.refs_1_), channel_id=1, source_target_pairs={{0,2},{1,3},{2,0},{3,1},{4,6},{5,7},{6,4},{7,5},{8,10},{9,11},{10,... | collective-permute-start | bytes 491528 | tf_op jit(solution)/shard_map/ppermute | solution.py:53
  11.2 1.3 collective-permute-start.2
  12.6 1.6 collective-permute-start.5
  14.1 0.8 fusion.12
  15.0 1.0 collective-permute-done.refs_1_.refs_2_
  16.0 6.0 %collective-permute-done.1.refs_2_.refs_3_ = bf16[1,128,640]{2,1,0:T(8,128)(2,1)S(1)} collective-permute-done((bf16[1,128,640]{2,1,0:T(8,128)(2,1)S(1)}, bf16[1,128,640]{2,1,0:T(8,128)(2,1)S(1)}, u32[]{:S(2)}, u32[]{:S(2)}) %collective-permute-start.1) | collective-permute-done | bytes 163872 | tf_op jit(solution)/shard_map/ppermute | solution.py:53
  22.0 1.3 collective-permute-start.10
  23.3 3.1 %collective-permute-start.9 = (bf16[4,64,640]{2,1,0:T(8,128)(2,1)S(1)}, bf16[4,64,640]{2,1,0:T(8,128)(2,1)S(1)}, u32[]{:S(2)}, u32[]{:S(2)}) collective-permute-start(bf16[4,64,640]{2,1,0:T(8,128)(2,1)S(1)} %get-tuple-element.19), channel_id=1, source_target_pairs={{0,4},{4,8},{8,12},{12,16},{16,20},{20,24},{24,28},{1,5},{5,9},{9,... | collective-permute-start | bytes 983048 | tf_op jit(solution)/shard_map/ppermute | solution.py:785
  26.5 4.0 %collective-permute-start.6 = (bf16[1,144,640]{2,1,0:T(8,128)(2,1)S(1)}, bf16[1,144,640]{2,1,0:T(8,128)(2,1)S(1)}, u32[]{:S(2)}, u32[]{:S(2)}) collective-permute-start(bf16[1,144,640]{2,1,0:T(8,128)(2,1)S(1)} %shard_map.164.refs_5_), channel_id=1, source_target_pairs={{0,1},{1,2},{2,3},{3,0},{4,5},{5,6},{6,7},{7,4},{8,9},{9,10},{10,1... | collective-permute-start | bytes 552968 | tf_op jit(solution)/shard_map/ppermute | solution.py:53
  30.5 1.6 collective-permute-start.7
  32.2 0.8 collective-permute-start.8
  33.7 3.8 %shard_map.166.refs_12_ = f32[160,128]{1,0:T(8,128)S(1)} custom-call(s32[3]{0:T(128)S(1)} %pad_add_fusion.n_ref.refs_0_, s32[1]{0:T(128)S(6)} %copy.18.i_ref, f32[1,50]{1,0:T(1,128)S(1)} %bitcast.14, f32[320,1280]{1,0:T(8,128)} %w_ref.1, f32[1280,640]{1,0:T(8,128)} %t_ref.1), custom_call_target="tpu_custom_call" | custom-call | tf_op jit(solution)/shard_map/pallas_call | solution.py:36
  37.5 7.1 %collective-permute-done.7.refs_7_ = bf16[1,144,640]{2,1,0:T(8,128)(2,1)S(1)} collective-permute-done((bf16[1,144,640]{2,1,0:T(8,128)(2,1)S(1)}, bf16[1,144,640]{2,1,0:T(8,128)(2,1)S(1)}, u32[]{:S(2)}, u32[]{:S(2)}) %collective-permute-start.7) | collective-permute-done | bytes 184352 | tf_op jit(solution)/shard_map/ppermute | solution.py:53
  44.6 5.5 %shard_map.167 = (bf16[160,512]{1,0:T(8,128)(2,1)S(1)}, bf16[160,512]{1,0:T(8,128)(2,1)S(1)}, f32[8,160]{1,0:T(8,128)S(1)}, bf16[160,512]{1,0:T(8,128)(2,1)S(1)}...) custom-call(s32[3]{0:T(128)S(1)} %pad_add_fusion.n_ref.refs_0_, ...), custom_call_target="tpu_custom_call" | custom-call | flops 1887436800 | tf_op jit(solution)/shard_map/pallas_call | solution.py:36
  50.3 1.1 collective-permute-done.14
  51.3 1.0 collective-permute-start.15
  52.3 0.9 fusion.1.refs_0_
  53.3 4.6 %collective-permute-start.32 = (bf16[1,80,640]{2,1,0:T(8,128)(2,1)S(1)}, bf16[1,80,640]{2,1,0:T(8,128)(2,1)S(1)}, u32[]{:S(2)}, u32[]{:S(2)}) collective-permute-start(bf16[1,80,640]{2,1,0:T(8,128)(2,1)S(1)} %fusion.1.refs_0_), channel_id=1, source_target_pairs={{0,1},{1,2},{2,3},{3,0},{4,5},{5,6},{6,7},{7,4},{8,9},{9,10},{10,1... | collective-permute-start | bytes 307208 | tf_op jit(solution)/shard_map/ppermute | solution.py:53
  57.8 1.4 collective-permute-start.33
  59.2 1.0 collective-permute-start.34
  60.3 0.7 collective-permute-start.16
  61.0 1.5 collective-permute-done.32.refs_1_
  62.5 3.8 %collective-permute-done.33.refs_2_ = bf16[1,80,640]{2,1,0:T(8,128)(2,1)S(1)} collective-permute-done((bf16[1,80,640]{2,1,0:T(8,128)(2,1)S(1)}, bf16[1,80,640]{2,1,0:T(8,128)(2,1)S(1)}, u32[]{:S(2)}, u32[]{:S(2)}) %collective-permute-start.33) | collective-permute-done | bytes 102432 | tf_op jit(solution)/shard_map/ppermute | solution.py:53
  66.3 0.6 shard_map.173.refs_0_
  66.9 1.0 collective-permute-start.35
  67.8 2.7 %collective-permute-start.11 = (bf16[160,512]{1,0:T(8,128)(2,1)S(1)}, bf16[160,512]{1,0:T(8,128)(2,1)S(1)}, u32[]{:S(2)}, u32[]{:S(2)}) collective-permute-start(bf16[160,512]{1,0:T(8,128)(2,1)S(1)} %get-tuple-element.21.refs_0_.refs_1_), channel_id=1, source_target_pairs={{0,1},{1,2},{2,3},{3,0},{4,5},{5,6},{6,7},{7,4},{8,9},{9,10},{10,1... | collective-permute-start | bytes 491528 | tf_op jit(solution)/shard_map/ppermute | solution.py:53
  70.5 1.5 collective-permute-start.12
  72.0 0.8 collective-permute-start.13
  73.0 1.3 collective-permute-start.17
  74.3 2.5 %collective-permute-done.11.refs_1_.refs_2_ = bf16[160,512]{1,0:T(8,128)(2,1)S(1)} collective-permute-done((bf16[160,512]{1,0:T(8,128)(2,1)S(1)}, bf16[160,512]{1,0:T(8,128)(2,1)S(1)}, u32[]{:S(2)}, u32[]{:S(2)}) %collective-permute-start.11) | collective-permute-done | bytes 163872 | tf_op jit(solution)/shard_map/ppermute | solution.py:53
  76.8 7.0 %collective-permute-done.12.refs_2_.refs_3_ = bf16[160,512]{1,0:T(8,128)(2,1)S(1)} collective-permute-done((bf16[160,512]{1,0:T(8,128)(2,1)S(1)}, bf16[160,512]{1,0:T(8,128)(2,1)S(1)}, u32[]{:S(2)}, u32[]{:S(2)}) %collective-permute-start.12) | collective-permute-done | bytes 163872 | tf_op jit(solution)/shard_map/ppermute | solution.py:53
  84.1 1.7 %collective-permute-start.20 = (bf16[640,256]{1,0:T(8,128)(2,1)S(1)}, bf16[640,256]{1,0:T(8,128)(2,1)S(1)}, u32[]{:S(2)}, u32[]{:S(2)}) collective-permute-start(bf16[640,256]{1,0:T(8,128)(2,1)S(1)} %get-tuple-element.25), channel_id=1, source_target_pairs={{0,4},{4,8},{8,12},{12,16},{16,20},{20,24},{24,28},{1,5},{5,9},{9,... | collective-permute-start | bytes 983048 | tf_op jit(solution)/shard_map/ppermute | solution.py:785
  85.8 1.3 collective-permute-start.21
  87.1 4.2 %collective-permute-start.36 = (bf16[4,80,640]{2,1,0:T(8,128)(2,1)S(1)}, bf16[4,80,640]{2,1,0:T(8,128)(2,1)S(1)}, u32[]{:S(2)}, u32[]{:S(2)}) collective-permute-start(bf16[4,80,640]{2,1,0:T(8,128)(2,1)S(1)} %shard_map.173.refs_0_), channel_id=1, source_target_pairs={{0,16},{4,20},{8,24},{12,28},{16,0},{20,4},{24,8},{28,12},{1,17},{... | collective-permute-start | bytes 1228808 | tf_op jit(solution)/shard_map/ppermute | solution.py:53
  91.3 6.0 %collective-permute-start.18 = (bf16[160,640]{1,0:T(8,128)(2,1)S(1)}, bf16[160,640]{1,0:T(8,128)(2,1)S(1)}, u32[]{:S(2)}, u32[]{:S(2)}) collective-permute-start(bf16[160,640]{1,0:T(8,128)(2,1)S(1)} %shard_map.168.refs_5_), channel_id=1, source_target_pairs={{0,2},{1,3},{2,0},{3,1},{4,6},{5,7},{6,4},{7,5},{8,10},{9,11},{10,... | collective-permute-start | bytes 614408 | tf_op jit(solution)/shard_map/ppermute | solution.py:53
  97.3 3.4 %collective-permute-start.19 = (bf16[160,640]{1,0:T(8,128)(2,1)S(1)}, bf16[160,640]{1,0:T(8,128)(2,1)S(1)}, u32[]{:S(2)}, u32[]{:S(2)}) collective-permute-start(bf16[160,640]{1,0:T(8,128)(2,1)S(1)} %shard_map.168.refs_5_), channel_id=1, source_target_pairs={{0,3},{1,0},{2,1},{3,2},{4,7},{5,4},{6,5},{7,6},{8,11},{9,8},{10,9... | collective-permute-start | bytes 614408 | tf_op jit(solution)/shard_map/ppermute | solution.py:53
  100.7 6.9 %collective-permute-done.18.refs_7_ = bf16[160,640]{1,0:T(8,128)(2,1)S(1)} collective-permute-done((bf16[160,640]{1,0:T(8,128)(2,1)S(1)}, bf16[160,640]{1,0:T(8,128)(2,1)S(1)}, u32[]{:S(2)}, u32[]{:S(2)}) %collective-permute-start.18) | collective-permute-done | bytes 204832 | tf_op jit(solution)/shard_map/ppermute | solution.py:53
  107.6 1.2 collective-permute-start.37
  108.8 0.5 collective-permute-start.39
  109.3 3.1 %shard_map.171 = (bf16[1,160,256]{2,1,0:T(8,128)(2,1)S(1)}, bf16[1,160,256]{2,1,0:T(8,128)(2,1)S(1)}) custom-call(s32[3]{0:T(128)S(1)} %pad_add_fusion.n_ref.refs_0_, bf16[160,512]{1,0:T(8,128)(2,1)S(1)} %get-tuple-element.21.refs_0_.refs_1_, bf16[160,512]{1,0:T(8,128)(2,1)S(1)} %collective-permute-done.11.refs_1_.refs_2_, ...), custom_call_target="tpu_custom_call" | custom-call | flops 1887436800 | tf_op jit(solution)/shard_map/pallas_call | solution.py:36
  112.4 1.3 collective-permute-start.23
  113.7 5.4 %collective-permute-start.24 = (bf16[1,160,256]{2,1,0:T(8,128)(2,1)S(1)}, bf16[1,160,256]{2,1,0:T(8,128)(2,1)S(1)}, u32[]{:S(2)}, u32[]{:S(2)}) collective-permute-start(bf16[1,160,256]{2,1,0:T(8,128)(2,1)S(1)} %get-tuple-element.32), channel_id=1, source_target_pairs={{0,1},{1,2},{2,3},{3,0},{4,5},{5,6},{6,7},{7,4},{8,9},{9,10},{10,1... | collective-permute-start | bytes 245768 | tf_op jit(solution)/shard_map/ppermute | solution.py:53
  119.0 3.1 %shard_map.170 = (bf16[1,160,256]{2,1,0:T(8,128)(2,1)S(1)}, bf16[1,160,256]{2,1,0:T(8,128)(2,1)S(1)}) custom-call(s32[3]{0:T(128)S(1)} %pad_add_fusion.n_ref.refs_0_, bf16[160,512]{1,0:T(8,128)(2,1)S(1)} %get-tuple-element.21.refs_0_.refs_1_, bf16[160,512]{1,0:T(8,128)(2,1)S(1)} %collective-permute-done.11.refs_1_.refs_2_, ...), custom_call_target="tpu_custom_call" | custom-call | flops 1887436800 | tf_op jit(solution)/shard_map/pallas_call | solution.py:36
  122.2 0.7 collective-permute-done.24.refs_3_
  122.9 2.0 %collective-permute-start.22 = (bf16[1,160,256]{2,1,0:T(8,128)(2,1)S(1)}, bf16[1,160,256]{2,1,0:T(8,128)(2,1)S(1)}, u32[]{:S(2)}, u32[]{:S(2)}) collective-permute-start(bf16[1,160,256]{2,1,0:T(8,128)(2,1)S(1)} %get-tuple-element.30), channel_id=1, source_target_pairs={{0,3},{1,0},{2,1},{3,2},{4,7},{5,4},{6,5},{7,6},{8,11},{9,8},{10,9... | collective-permute-start | bytes 245768 | tf_op jit(solution)/shard_map/ppermute | solution.py:53
  124.9 2.4 %collective-permute-done.22.refs_1_ = bf16[1,160,256]{2,1,0:T(8,128)(2,1)S(1)} collective-permute-done((bf16[1,160,256]{2,1,0:T(8,128)(2,1)S(1)}, bf16[1,160,256]{2,1,0:T(8,128)(2,1)S(1)}, u32[]{:S(2)}, u32[]{:S(2)}) %collective-permute-start.22) | collective-permute-done | bytes 81952 | tf_op jit(solution)/shard_map/ppermute | solution.py:53
  127.3 0.6 shard_map.172.refs_0_
  127.9 1.1 collective-permute-start.25
  129.0 0.7 collective-permute-start.26
  129.7 2.1 %collective-permute-start.27 = (bf16[1,640,256]{2,1,0:T(8,128)(2,1)S(1)}, bf16[1,640,256]{2,1,0:T(8,128)(2,1)S(1)}, u32[]{:S(2)}, u32[]{:S(2)}) collective-permute-start(bf16[1,640,256]{2,1,0:T(8,128)(2,1)S(1)} %shard_map.172.refs_0_), channel_id=1, source_target_pairs={{0,24},{4,28},{8,0},{12,4},{16,8},{20,12},{24,16},{28,20},{1,25},{... | collective-permute-start | bytes 983048 | tf_op jit(solution)/shard_map/ppermute | solution.py:53
  131.8 0.5 collective-permute-start.28
  132.3 7.1 %collective-permute-done.25.refs_1_ = bf16[1,640,256]{2,1,0:T(8,128)(2,1)S(1)} collective-permute-done((bf16[1,640,256]{2,1,0:T(8,128)(2,1)S(1)}, bf16[1,640,256]{2,1,0:T(8,128)(2,1)S(1)}, u32[]{:S(2)}, u32[]{:S(2)}) %collective-permute-start.25) | collective-permute-done | bytes 327712 | tf_op jit(solution)/shard_map/ppermute | solution.py:53
  139.4 5.0 %collective-permute-done.26.refs_2_ = bf16[1,640,256]{2,1,0:T(8,128)(2,1)S(1)} collective-permute-done((bf16[1,640,256]{2,1,0:T(8,128)(2,1)S(1)}, bf16[1,640,256]{2,1,0:T(8,128)(2,1)S(1)}, u32[]{:S(2)}, u32[]{:S(2)}) %collective-permute-start.26) | collective-permute-done | bytes 327712 | tf_op jit(solution)/shard_map/ppermute | solution.py:53
  144.4 0.5 collective-permute-start.31
  145.2 0.8 shard_map.174.refs_8_
  146.0 1.7 %copy-done = bf16[2560,640]{1,0:T(8,128)(2,1)} copy-done((bf16[2560,640]{1,0:T(8,128)(2,1)}, bf16[2560,640]{1,0:T(8,128)(2,1)S(1)}, u32[]{:S(2)}) %copy-start) | copy-done | bytes 3276824
  147.8 16.5 %shard_map.176 = bf16[1,4,64,640]{3,2,1,0:T(8,128)(2,1)} custom-call(bf16[1,640,256]{2,1,0:T(8,128)(2,1)S(1)} %shard_map.172.refs_0_, bf16[1,640,256]{2,1,0:T(8,128)(2,1)S(1)} %collective-permute-done.25.refs_1_, bf16[1,640,256]{2,1,0:T(8,128)(2,1)S(1)} %collective-permute-done.26.refs_2_, bf16[1,640,256]{2,1,0:T(8,128)(2,1)S(1)} %collective-permute-done.27.refs_3_, ...), custom_call_target="tpu_custom_call" | custom-call | tf_op jit(solution)/shard_map/pallas_call | solution.py:36
  (79 shorter events, 1.4 us)
Async XLA Ops:
  0.0 33.7 %copy-start.6 = (f32[50]{0:T(128)S(1)}, f32[50]{0:T(128)}, u32[]{:S(2)}) copy-start(f32[50]{0:T(128)} %param.19) | copy-start | bytes 604
  0.0 1.0 copy-start.1
  1.0 0.9 copy-start.3
  1.9 24.5 %copy-start.2 = (bf16[1,4,64,640]{3,2,1,0:T(8,128)(2,1)S(1)}, bf16[1,4,64,640]{3,2,1,0:T(8,128)(2,1)}, u32[]{:S(2)}) copy-start(bf16[1,4,64,640]{3,2,1,0:T(8,128)(2,1)} %param.17) | copy-start | bytes 983044
  2.6 1.4 collective-permute-start.3
  4.1 8.5 %collective-permute-start.4 = (f32[2,640]{1,0:T(2,128)S(1)}, f32[2,640]{1,0:T(2,128)S(1)}, u32[]{:S(2)}, u32[]{:S(2)}) collective-permute-start(f32[2,640]{1,0:T(2,128)S(1)} %pad_maximum_fusion.4), channel_id=1, source_target_pairs={{0,8},{4,12},{8,0},{12,4},{16,24},{20,28},{24,16},{28,20},{1,9},{5... | collective-permute-start | bytes 15368 | tf_op jit(solution)/shard_map/ppermute | solution.py:670
  7.0 9.0 %collective-permute-start = (bf16[1,128,640]{2,1,0:T(8,128)(2,1)S(1)}, bf16[1,128,640]{2,1,0:T(8,128)(2,1)S(1)}, u32[]{:S(2)}, u32[]{:S(2)}) collective-permute-start(bf16[1,128,640]{2,1,0:T(8,128)(2,1)S(1)} %pad_maximum_fusion.refs_0_.refs_1_), channel_id=1, source_target_pairs={{0,1},{1,2},{2,3},{3,0},{4,5},{5,6},{6,7},{7,4},{8,9},{9,10},{10,1... | collective-permute-start | bytes 491528 | tf_op jit(solution)/shard_map/ppermute | solution.py:53
  8.6 13.4 %collective-permute-start.1 = (bf16[1,128,640]{2,1,0:T(8,128)(2,1)S(1)}, bf16[1,128,640]{2,1,0:T(8,128)(2,1)S(1)}, u32[]{:S(2)}, u32[]{:S(2)}) collective-permute-start(bf16[1,128,640]{2,1,0:T(8,128)(2,1)S(1)} %pad_maximum_fusion.refs_0_.refs_1_), channel_id=1, source_target_pairs={{0,2},{1,3},{2,0},{3,1},{4,6},{5,7},{6,4},{7,5},{8,10},{9,11},{10,... | collective-permute-start | bytes 491528 | tf_op jit(solution)/shard_map/ppermute | solution.py:53
  11.2 10.8 %collective-permute-start.2 = (bf16[1,128,640]{2,1,0:T(8,128)(2,1)S(1)}, bf16[1,128,640]{2,1,0:T(8,128)(2,1)S(1)}, u32[]{:S(2)}, u32[]{:S(2)}) collective-permute-start(bf16[1,128,640]{2,1,0:T(8,128)(2,1)S(1)} %pad_maximum_fusion.refs_0_.refs_1_), channel_id=1, source_target_pairs={{0,3},{1,0},{2,1},{3,2},{4,7},{5,4},{6,5},{7,6},{8,11},{9,8},{10,9... | collective-permute-start | bytes 491528 | tf_op jit(solution)/shard_map/ppermute | solution.py:53
  12.6 13.8 %collective-permute-start.5 = (f32[2,640]{1,0:T(2,128)S(1)}, f32[2,640]{1,0:T(2,128)S(1)}, u32[]{:S(2)}, u32[]{:S(2)}) collective-permute-start(f32[2,640]{1,0:T(2,128)S(1)} %pad_maximum_fusion.5), channel_id=1, source_target_pairs={{0,16},{4,20},{8,24},{12,28},{16,0},{20,4},{24,8},{28,12},{1,17},{... | collective-permute-start | bytes 15368 | tf_op jit(solution)/shard_map/ppermute | solution.py:670
  22.0 22.6 %collective-permute-start.10 = (bf16[4,64,640]{2,1,0:T(8,128)(2,1)S(1)}, bf16[4,64,640]{2,1,0:T(8,128)(2,1)S(1)}, u32[]{:S(2)}, u32[]{:S(2)}) collective-permute-start(bf16[4,64,640]{2,1,0:T(8,128)(2,1)S(1)} %get-tuple-element.20), channel_id=1, source_target_pairs={{4,0},{8,4},{12,8},{16,12},{20,16},{24,20},{28,24},{5,1},{9,5},{13... | collective-permute-start | bytes 983048 | tf_op jit(solution)/shard_map/ppermute | solution.py:785
  23.3 21.3 %collective-permute-start.9 = (bf16[4,64,640]{2,1,0:T(8,128)(2,1)S(1)}, bf16[4,64,640]{2,1,0:T(8,128)(2,1)S(1)}, u32[]{:S(2)}, u32[]{:S(2)}) collective-permute-start(bf16[4,64,640]{2,1,0:T(8,128)(2,1)S(1)} %get-tuple-element.19), channel_id=1, source_target_pairs={{0,4},{4,8},{8,12},{12,16},{16,20},{20,24},{24,28},{1,5},{5,9},{9,... | collective-permute-start | bytes 983048 | tf_op jit(solution)/shard_map/ppermute | solution.py:785
  26.5 11.0 %collective-permute-start.6 = (bf16[1,144,640]{2,1,0:T(8,128)(2,1)S(1)}, bf16[1,144,640]{2,1,0:T(8,128)(2,1)S(1)}, u32[]{:S(2)}, u32[]{:S(2)}) collective-permute-start(bf16[1,144,640]{2,1,0:T(8,128)(2,1)S(1)} %shard_map.164.refs_5_), channel_id=1, source_target_pairs={{0,1},{1,2},{2,3},{3,0},{4,5},{5,6},{6,7},{7,4},{8,9},{9,10},{10,1... | collective-permute-start | bytes 552968 | tf_op jit(solution)/shard_map/ppermute | solution.py:53
  30.5 14.1 %collective-permute-start.7 = (bf16[1,144,640]{2,1,0:T(8,128)(2,1)S(1)}, bf16[1,144,640]{2,1,0:T(8,128)(2,1)S(1)}, u32[]{:S(2)}, u32[]{:S(2)}) collective-permute-start(bf16[1,144,640]{2,1,0:T(8,128)(2,1)S(1)} %shard_map.164.refs_5_), channel_id=1, source_target_pairs={{0,2},{1,3},{2,0},{3,1},{4,6},{5,7},{6,4},{7,5},{8,10},{9,11},{10,... | collective-permute-start | bytes 552968 | tf_op jit(solution)/shard_map/ppermute | solution.py:53
  32.2 12.4 %collective-permute-start.8 = (bf16[1,144,640]{2,1,0:T(8,128)(2,1)S(1)}, bf16[1,144,640]{2,1,0:T(8,128)(2,1)S(1)}, u32[]{:S(2)}, u32[]{:S(2)}) collective-permute-start(bf16[1,144,640]{2,1,0:T(8,128)(2,1)S(1)} %shard_map.164.refs_5_), channel_id=1, source_target_pairs={{0,3},{1,0},{2,1},{3,2},{4,7},{5,4},{6,5},{7,6},{8,11},{9,8},{10,9... | collective-permute-start | bytes 552968 | tf_op jit(solution)/shard_map/ppermute | solution.py:53
  33.7 10.9 %copy-start.7 = (bf16[5760,160]{0,1:T(8,128)(2,1)S(1)}, bf16[5760,160]{0,1:T(8,128)(2,1)}, u32[]{:S(2)}) copy-start(bf16[5760,160]{0,1:T(8,128)(2,1)} %param.23) | copy-start | bytes 5529604
  33.7 10.9 %copy-start.9 = (f32[160,160]{1,0:T(8,128)S(1)}, f32[160,160]{1,0:T(8,128)}, u32[]{:S(2)}) copy-start(f32[160,160]{1,0:T(8,128)} %constant.73.clone.refs_13_) | copy-start | bytes 307204
  33.7 10.9 %copy-start.10 = (f32[8,128]{1,0:T(8,128)S(1)}, f32[8,128]{1,0:T(8,128)}, u32[]{:S(2)}) copy-start(f32[8,128]{1,0:T(8,128)} %constant.74.clone.refs_15_) | copy-start | bytes 12292
  44.6 7.7 %copy-start.11 = (bf16[640,160]{0,1:T(8,128)(2,1)S(1)}, bf16[640,160]{0,1:T(8,128)(2,1)}, u32[]{:S(2)}) copy-start(bf16[640,160]{0,1:T(8,128)(2,1)} %param.26) | copy-start | bytes 614404
  50.1 59.2 %copy-start.8 = (bf16[5760,160]{0,1:T(8,128)(2,1)S(1)}, bf16[5760,160]{0,1:T(8,128)(2,1)}, u32[]{:S(2)}) copy-start(bf16[5760,160]{0,1:T(8,128)(2,1)} %param.24) | copy-start | bytes 5529604
  50.1 1.2 collective-permute-start.14
  51.3 8.9 %collective-permute-start.15 = (f32[8,160]{1,0:T(8,128)S(1)}, f32[8,160]{1,0:T(8,128)S(1)}, u32[]{:S(2)}, u32[]{:S(2)}) collective-permute-start(f32[8,160]{1,0:T(8,128)S(1)} %pad_maximum_fusion.1), channel_id=1, source_target_pairs={{0,8},{4,12},{8,0},{12,4},{16,24},{20,28},{24,16},{28,20},{1,9},{5... | collective-permute-start | bytes 15368 | tf_op jit(solution)/shard_map/ppermute | solution.py:670
  53.3 9.2 %collective-permute-start.32 = (bf16[1,80,640]{2,1,0:T(8,128)(2,1)S(1)}, bf16[1,80,640]{2,1,0:T(8,128)(2,1)S(1)}, u32[]{:S(2)}, u32[]{:S(2)}) collective-permute-start(bf16[1,80,640]{2,1,0:T(8,128)(2,1)S(1)} %fusion.1.refs_0_), channel_id=1, source_target_pairs={{0,1},{1,2},{2,3},{3,0},{4,5},{5,6},{6,7},{7,4},{8,9},{9,10},{10,1... | collective-permute-start | bytes 307208 | tf_op jit(solution)/shard_map/ppermute | solution.py:53
  57.8 8.5 %collective-permute-start.33 = (bf16[1,80,640]{2,1,0:T(8,128)(2,1)S(1)}, bf16[1,80,640]{2,1,0:T(8,128)(2,1)S(1)}, u32[]{:S(2)}, u32[]{:S(2)}) collective-permute-start(bf16[1,80,640]{2,1,0:T(8,128)(2,1)S(1)} %fusion.1.refs_0_), channel_id=1, source_target_pairs={{0,2},{1,3},{2,0},{3,1},{4,6},{5,7},{6,4},{7,5},{8,10},{9,11},{10,... | collective-permute-start | bytes 307208 | tf_op jit(solution)/shard_map/ppermute | solution.py:53
  59.2 7.0 %collective-permute-start.34 = (bf16[1,80,640]{2,1,0:T(8,128)(2,1)S(1)}, bf16[1,80,640]{2,1,0:T(8,128)(2,1)S(1)}, u32[]{:S(2)}, u32[]{:S(2)}) collective-permute-start(bf16[1,80,640]{2,1,0:T(8,128)(2,1)S(1)} %fusion.1.refs_0_), channel_id=1, source_target_pairs={{0,3},{1,0},{2,1},{3,2},{4,7},{5,4},{6,5},{7,6},{8,11},{9,8},{10,9... | collective-permute-start | bytes 307208 | tf_op jit(solution)/shard_map/ppermute | solution.py:53
  60.3 12.6 %collective-permute-start.16 = (f32[8,160]{1,0:T(8,128)S(1)}, f32[8,160]{1,0:T(8,128)S(1)}, u32[]{:S(2)}, u32[]{:S(2)}) collective-permute-start(f32[8,160]{1,0:T(8,128)S(1)} %pad_maximum_fusion.2), channel_id=1, source_target_pairs={{0,16},{4,20},{8,24},{12,28},{16,0},{20,4},{24,8},{28,12},{1,17},{... | collective-permute-start | bytes 15368 | tf_op jit(solution)/shard_map/ppermute | solution.py:670
  66.9 24.4 %collective-permute-start.35 = (bf16[4,80,640]{2,1,0:T(8,128)(2,1)S(1)}, bf16[4,80,640]{2,1,0:T(8,128)(2,1)S(1)}, u32[]{:S(2)}, u32[]{:S(2)}) collective-permute-start(bf16[4,80,640]{2,1,0:T(8,128)(2,1)S(1)} %shard_map.173.refs_0_), channel_id=1, source_target_pairs={{0,8},{4,12},{8,16},{12,20},{16,24},{20,28},{24,0},{28,4},{1,9},{5... | collective-permute-start | bytes 1228808 | tf_op jit(solution)/shard_map/ppermute | solution.py:53
  67.8 9.0 %collective-permute-start.11 = (bf16[160,512]{1,0:T(8,128)(2,1)S(1)}, bf16[160,512]{1,0:T(8,128)(2,1)S(1)}, u32[]{:S(2)}, u32[]{:S(2)}) collective-permute-start(bf16[160,512]{1,0:T(8,128)(2,1)S(1)} %get-tuple-element.21.refs_0_.refs_1_), channel_id=1, source_target_pairs={{0,1},{1,2},{2,3},{3,0},{4,5},{5,6},{6,7},{7,4},{8,9},{9,10},{10,1... | collective-permute-start | bytes 491528 | tf_op jit(solution)/shard_map/ppermute | solution.py:53
  70.5 13.3 %collective-permute-start.12 = (bf16[160,512]{1,0:T(8,128)(2,1)S(1)}, bf16[160,512]{1,0:T(8,128)(2,1)S(1)}, u32[]{:S(2)}, u32[]{:S(2)}) collective-permute-start(bf16[160,512]{1,0:T(8,128)(2,1)S(1)} %get-tuple-element.21.refs_0_.refs_1_), channel_id=1, source_target_pairs={{0,2},{1,3},{2,0},{3,1},{4,6},{5,7},{6,4},{7,5},{8,10},{9,11},{10,... | collective-permute-start | bytes 491528 | tf_op jit(solution)/shard_map/ppermute | solution.py:53
  72.0 11.8 %collective-permute-start.13 = (bf16[160,512]{1,0:T(8,128)(2,1)S(1)}, bf16[160,512]{1,0:T(8,128)(2,1)S(1)}, u32[]{:S(2)}, u32[]{:S(2)}) collective-permute-start(bf16[160,512]{1,0:T(8,128)(2,1)S(1)} %get-tuple-element.21.refs_0_.refs_1_), channel_id=1, source_target_pairs={{0,3},{1,0},{2,1},{3,2},{4,7},{5,4},{6,5},{7,6},{8,11},{9,8},{10,9... | collective-permute-start | bytes 491528 | tf_op jit(solution)/shard_map/ppermute | solution.py:53
  73.0 24.3 %collective-permute-start.17 = (bf16[160,640]{1,0:T(8,128)(2,1)S(1)}, bf16[160,640]{1,0:T(8,128)(2,1)S(1)}, u32[]{:S(2)}, u32[]{:S(2)}) collective-permute-start(bf16[160,640]{1,0:T(8,128)(2,1)S(1)} %shard_map.168.refs_5_), channel_id=1, source_target_pairs={{0,1},{1,2},{2,3},{3,0},{4,5},{5,6},{6,7},{7,4},{8,9},{9,10},{10,1... | collective-permute-start | bytes 614408 | tf_op jit(solution)/shard_map/ppermute | solution.py:53
  84.1 24.7 %collective-permute-start.20 = (bf16[640,256]{1,0:T(8,128)(2,1)S(1)}, bf16[640,256]{1,0:T(8,128)(2,1)S(1)}, u32[]{:S(2)}, u32[]{:S(2)}) collective-permute-start(bf16[640,256]{1,0:T(8,128)(2,1)S(1)} %get-tuple-element.25), channel_id=1, source_target_pairs={{0,4},{4,8},{8,12},{12,16},{16,20},{20,24},{24,28},{1,5},{5,9},{9,... | collective-permute-start | bytes 983048 | tf_op jit(solution)/shard_map/ppermute | solution.py:785
  85.8 23.5 %collective-permute-start.21 = (bf16[640,256]{1,0:T(8,128)(2,1)S(1)}, bf16[640,256]{1,0:T(8,128)(2,1)S(1)}, u32[]{:S(2)}, u32[]{:S(2)}) collective-permute-start(bf16[640,256]{1,0:T(8,128)(2,1)S(1)} %get-tuple-element.26), channel_id=1, source_target_pairs={{4,0},{8,4},{12,8},{16,12},{20,16},{24,20},{28,24},{5,1},{9,5},{13... | collective-permute-start | bytes 983048 | tf_op jit(solution)/shard_map/ppermute | solution.py:785
  87.1 26.6 %collective-permute-start.36 = (bf16[4,80,640]{2,1,0:T(8,128)(2,1)S(1)}, bf16[4,80,640]{2,1,0:T(8,128)(2,1)S(1)}, u32[]{:S(2)}, u32[]{:S(2)}) collective-permute-start(bf16[4,80,640]{2,1,0:T(8,128)(2,1)S(1)} %shard_map.173.refs_0_), channel_id=1, source_target_pairs={{0,16},{4,20},{8,24},{12,28},{16,0},{20,4},{24,8},{28,12},{1,17},{... | collective-permute-start | bytes 1228808 | tf_op jit(solution)/shard_map/ppermute | solution.py:53
  91.3 16.3 %collective-permute-start.18 = (bf16[160,640]{1,0:T(8,128)(2,1)S(1)}, bf16[160,640]{1,0:T(8,128)(2,1)S(1)}, u32[]{:S(2)}, u32[]{:S(2)}) collective-permute-start(bf16[160,640]{1,0:T(8,128)(2,1)S(1)} %shard_map.168.refs_5_), channel_id=1, source_target_pairs={{0,2},{1,3},{2,0},{3,1},{4,6},{5,7},{6,4},{7,5},{8,10},{9,11},{10,... | collective-permute-start | bytes 614408 | tf_op jit(solution)/shard_map/ppermute | solution.py:53
  97.3 11.5 %collective-permute-start.19 = (bf16[160,640]{1,0:T(8,128)(2,1)S(1)}, bf16[160,640]{1,0:T(8,128)(2,1)S(1)}, u32[]{:S(2)}, u32[]{:S(2)}) collective-permute-start(bf16[160,640]{1,0:T(8,128)(2,1)S(1)} %shard_map.168.refs_5_), channel_id=1, source_target_pairs={{0,3},{1,0},{2,1},{3,2},{4,7},{5,4},{6,5},{7,6},{8,11},{9,8},{10,9... | collective-permute-start | bytes 614408 | tf_op jit(solution)/shard_map/ppermute | solution.py:53
  107.6 21.4 %collective-permute-start.37 = (bf16[4,80,640]{2,1,0:T(8,128)(2,1)S(1)}, bf16[4,80,640]{2,1,0:T(8,128)(2,1)S(1)}, u32[]{:S(2)}, u32[]{:S(2)}) collective-permute-start(bf16[4,80,640]{2,1,0:T(8,128)(2,1)S(1)} %shard_map.173.refs_0_), channel_id=1, source_target_pairs={{0,24},{4,28},{8,0},{12,4},{16,8},{20,12},{24,16},{28,20},{1,25},{... | collective-permute-start | bytes 1228808 | tf_op jit(solution)/shard_map/ppermute | solution.py:53
  108.8 20.9 %collective-permute-start.38 = (bf16[4,80,640]{2,1,0:T(8,128)(2,1)S(1)}, bf16[4,80,640]{2,1,0:T(8,128)(2,1)S(1)}, u32[]{:S(2)}, u32[]{:S(2)}) collective-permute-start(bf16[4,80,640]{2,1,0:T(8,128)(2,1)S(1)} %shard_map.173.refs_0_), channel_id=1, source_target_pairs={{0,4},{4,0},{8,12},{12,8},{16,20},{20,16},{24,28},{28,24},{1,5},{5... | collective-permute-start | bytes 1228808 | tf_op jit(solution)/shard_map/ppermute | solution.py:680
  108.8 23.0 %collective-permute-start.39 = (bf16[4,80,640]{2,1,0:T(8,128)(2,1)S(1)}, bf16[4,80,640]{2,1,0:T(8,128)(2,1)S(1)}, u32[]{:S(2)}, u32[]{:S(2)}) collective-permute-start(bf16[4,80,640]{2,1,0:T(8,128)(2,1)S(1)} %collective-permute-done.35.refs_1_), channel_id=1, source_target_pairs={{0,4},{4,0},{8,12},{12,8},{16,20},{20,16},{24,28},{28,24},{1,5},{5... | collective-permute-start | bytes 1228808 | tf_op jit(solution)/shard_map/ppermute | solution.py:680
  112.4 9.7 %collective-permute-start.23 = (bf16[1,160,256]{2,1,0:T(8,128)(2,1)S(1)}, bf16[1,160,256]{2,1,0:T(8,128)(2,1)S(1)}, u32[]{:S(2)}, u32[]{:S(2)}) collective-permute-start(bf16[1,160,256]{2,1,0:T(8,128)(2,1)S(1)} %get-tuple-element.31), channel_id=1, source_target_pairs={{0,2},{1,3},{2,0},{3,1},{4,6},{5,7},{6,4},{7,5},{8,10},{9,11},{10,... | collective-permute-start | bytes 245768 | tf_op jit(solution)/shard_map/ppermute | solution.py:53
  113.7 9.2 %collective-permute-start.24 = (bf16[1,160,256]{2,1,0:T(8,128)(2,1)S(1)}, bf16[1,160,256]{2,1,0:T(8,128)(2,1)S(1)}, u32[]{:S(2)}, u32[]{:S(2)}) collective-permute-start(bf16[1,160,256]{2,1,0:T(8,128)(2,1)S(1)} %get-tuple-element.32), channel_id=1, source_target_pairs={{0,1},{1,2},{2,3},{3,0},{4,5},{5,6},{6,7},{7,4},{8,9},{9,10},{10,1... | collective-permute-start | bytes 245768 | tf_op jit(solution)/shard_map/ppermute | solution.py:53
  122.1 9.7 %collective-permute-start.40 = (bf16[4,80,640]{2,1,0:T(8,128)(2,1)S(1)}, bf16[4,80,640]{2,1,0:T(8,128)(2,1)S(1)}, u32[]{:S(2)}, u32[]{:S(2)}) collective-permute-start(bf16[4,80,640]{2,1,0:T(8,128)(2,1)S(1)} %collective-permute-done.36.refs_2_), channel_id=1, source_target_pairs={{0,4},{4,0},{8,12},{12,8},{16,20},{20,16},{24,28},{28,24},{1,5},{5... | collective-permute-start | bytes 1228808 | tf_op jit(solution)/shard_map/ppermute | solution.py:680
  122.9 4.4 %collective-permute-start.22 = (bf16[1,160,256]{2,1,0:T(8,128)(2,1)S(1)}, bf16[1,160,256]{2,1,0:T(8,128)(2,1)S(1)}, u32[]{:S(2)}, u32[]{:S(2)}) collective-permute-start(bf16[1,160,256]{2,1,0:T(8,128)(2,1)S(1)} %get-tuple-element.30), channel_id=1, source_target_pairs={{0,3},{1,0},{2,1},{3,2},{4,7},{5,4},{6,5},{7,6},{8,11},{9,8},{10,9... | collective-permute-start | bytes 245768 | tf_op jit(solution)/shard_map/ppermute | solution.py:53
  127.9 11.5 %collective-permute-start.25 = (bf16[1,640,256]{2,1,0:T(8,128)(2,1)S(1)}, bf16[1,640,256]{2,1,0:T(8,128)(2,1)S(1)}, u32[]{:S(2)}, u32[]{:S(2)}) collective-permute-start(bf16[1,640,256]{2,1,0:T(8,128)(2,1)S(1)} %shard_map.172.refs_0_), channel_id=1, source_target_pairs={{0,8},{4,12},{8,16},{12,20},{16,24},{20,28},{24,0},{28,4},{1,9},{5... | collective-permute-start | bytes 983048 | tf_op jit(solution)/shard_map/ppermute | solution.py:53
  129.0 15.4 %collective-permute-start.26 = (bf16[1,640,256]{2,1,0:T(8,128)(2,1)S(1)}, bf16[1,640,256]{2,1,0:T(8,128)(2,1)S(1)}, u32[]{:S(2)}, u32[]{:S(2)}) collective-permute-start(bf16[1,640,256]{2,1,0:T(8,128)(2,1)S(1)} %shard_map.172.refs_0_), channel_id=1, source_target_pairs={{0,16},{4,20},{8,24},{12,28},{16,0},{20,4},{24,8},{28,12},{1,17},{... | collective-permute-start | bytes 983048 | tf_op jit(solution)/shard_map/ppermute | solution.py:53
  129.7 14.7 %collective-permute-start.27 = (bf16[1,640,256]{2,1,0:T(8,128)(2,1)S(1)}, bf16[1,640,256]{2,1,0:T(8,128)(2,1)S(1)}, u32[]{:S(2)}, u32[]{:S(2)}) collective-permute-start(bf16[1,640,256]{2,1,0:T(8,128)(2,1)S(1)} %shard_map.172.refs_0_), channel_id=1, source_target_pairs={{0,24},{4,28},{8,0},{12,4},{16,8},{20,12},{24,16},{28,20},{1,25},{... | collective-permute-start | bytes 983048 | tf_op jit(solution)/shard_map/ppermute | solution.py:53
  131.8 13.4 %collective-permute-start.41 = (bf16[4,80,640]{2,1,0:T(8,128)(2,1)S(1)}, bf16[4,80,640]{2,1,0:T(8,128)(2,1)S(1)}, u32[]{:S(2)}, u32[]{:S(2)}) collective-permute-start(bf16[4,80,640]{2,1,0:T(8,128)(2,1)S(1)} %collective-permute-done.37.refs_3_), channel_id=1, source_target_pairs={{0,4},{4,0},{8,12},{12,8},{16,20},{20,16},{24,28},{28,24},{1,5},{5... | collective-permute-start | bytes 1228808 | tf_op jit(solution)/shard_map/ppermute | solution.py:680
  131.8 15.9 %collective-permute-start.28 = (bf16[1,640,256]{2,1,0:T(8,128)(2,1)S(1)}, bf16[1,640,256]{2,1,0:T(8,128)(2,1)S(1)}, u32[]{:S(2)}, u32[]{:S(2)}) collective-permute-start(bf16[1,640,256]{2,1,0:T(8,128)(2,1)S(1)} %shard_map.172.refs_0_), channel_id=1, source_target_pairs={{0,4},{4,0},{8,12},{12,8},{16,20},{20,16},{24,28},{28,24},{1,5},{5... | collective-permute-start | bytes 983048 | tf_op jit(solution)/shard_map/ppermute | solution.py:680
  139.4 8.3 %collective-permute-start.29 = (bf16[1,640,256]{2,1,0:T(8,128)(2,1)S(1)}, bf16[1,640,256]{2,1,0:T(8,128)(2,1)S(1)}, u32[]{:S(2)}, u32[]{:S(2)}) collective-permute-start(bf16[1,640,256]{2,1,0:T(8,128)(2,1)S(1)} %collective-permute-done.25.refs_1_), channel_id=1, source_target_pairs={{0,4},{4,0},{8,12},{12,8},{16,20},{20,16},{24,28},{28,24},{1,5},{5... | collective-permute-start | bytes 983048 | tf_op jit(solution)/shard_map/ppermute | solution.py:680
  144.4 3.3 %collective-permute-start.30 = (bf16[1,640,256]{2,1,0:T(8,128)(2,1)S(1)}, bf16[1,640,256]{2,1,0:T(8,128)(2,1)S(1)}, u32[]{:S(2)}, u32[]{:S(2)}) collective-permute-start(bf16[1,640,256]{2,1,0:T(8,128)(2,1)S(1)} %collective-permute-done.26.refs_2_), channel_id=1, source_target_pairs={{0,4},{4,0},{8,12},{12,8},{16,20},{20,16},{24,28},{28,24},{1,5},{5... | collective-permute-start | bytes 983048 | tf_op jit(solution)/shard_map/ppermute | solution.py:680
  144.4 3.3 %collective-permute-start.31 = (bf16[1,640,256]{2,1,0:T(8,128)(2,1)S(1)}, bf16[1,640,256]{2,1,0:T(8,128)(2,1)S(1)}, u32[]{:S(2)}, u32[]{:S(2)}) collective-permute-start(bf16[1,640,256]{2,1,0:T(8,128)(2,1)S(1)} %collective-permute-done.27.refs_3_), channel_id=1, source_target_pairs={{0,4},{4,0},{8,12},{12,8},{16,20},{20,16},{24,28},{28,24},{1,5},{5... | collective-permute-start | bytes 983048 | tf_op jit(solution)/shard_map/ppermute | solution.py:680
  145.2 2.5 %copy-start.4 = (bf16[640,128]{1,0:T(8,128)(2,1)S(1)}, bf16[640,128]{1,0:T(8,128)(2,1)}, u32[]{:S(2)}) copy-start(bf16[640,128]{1,0:T(8,128)(2,1)} %constant.71.clone.g_ref.refs_11_) | copy-start | bytes 491524
  145.2 2.5 %copy-start.5 = (bf16[128,640]{1,0:T(8,128)(2,1)S(1)}, bf16[128,640]{1,0:T(8,128)(2,1)}, u32[]{:S(2)}) copy-start(bf16[128,640]{1,0:T(8,128)(2,1)} %constant.76.refs_10_) | copy-start | bytes 491524
  146.0 1.7 %copy-start = (bf16[2560,640]{1,0:T(8,128)(2,1)}, bf16[2560,640]{1,0:T(8,128)(2,1)S(1)}, u32[]{:S(2)}) copy-start(bf16[2560,640]{1,0:T(8,128)(2,1)S(1)} %shard_map.174.refs_8_) | copy-start | bytes 9830404
